TPU v7x, 256 devices: a 4x2x16 block of a 4x16x16 slice. The times are simulated.
256 devices in a mesh: grp: 2 (over y), gx: 64 (over x, z), gy: 2 (over core).
Axes of the slice: x: 4, y: 2, z: 16, core: 2. Of those that a mesh axis runs over, the one named last changes fastest.
The devices are a block of a 4x16x16 slice.
Arguments:
- residue_feats: bfloat16 [2048, 256], P(('grp', 'gx')), parts along dimension 0, may hold values from -6 to 6
- pair_feats: bfloat16 [64, 2048, 1024], P(None, ('grp', 'gx'), 'gy'), parts along dimension 1, may hold values from -30 to 30
- w_row: bfloat16 [256, 64], replicated, may hold values from -0.375 to 0.375
- w_col: bfloat16 [256, 64], replicated, may hold values from -0.375 to 0.375
- first_taps: bfloat16 [9, 64, 64], replicated, may hold values from -0.25 to 0.25
- second_taps: bfloat16 [9, 64, 64], replicated, may hold values from -0.25 to 0.25
- norm_scale: float32 [2, 64], replicated, may hold values from 0.25 to 1.75
- norm_shift: float32 [2, 64], replicated, may hold values from -2 to 2
Outputs:
- symmetric: bfloat16 [64, 2048, 1024], P(None, ('grp', 'gx'), 'gy'), parts along dimension 1
There are 2 independent parts, one for each index of `grp`. A program takes and returns all parts, laid end to end along the dimension named above; an argument that names none is the same for every part. Nothing has to cross between parts.
All inputs are finite; a program needn't handle non-finite values.
Results may differ from a plain program's by a relative error of at most 0.012.
Values may be sent and summed in bfloat16 or wider, within the bound.
No kernel may reach another device: no remote copies, remote signals or barrier semaphores. Data moves between devices by JAX's collectives and lax.ppermute only.
A program may use at most 64 MiB of HBM per device.

v0:
```python
import functools

import jax
import jax.numpy as jnp
from jax import lax
from jax.experimental import pallas as pl
from jax.experimental.pallas import tpu as pltpu
from jax.sharding import Mesh
from jax.sharding import PartitionSpec as P

STEP = 8
GX = ("gx_0", "gx_1")
GRP_GX = ("grp", "gx_0", "gx_1")
LANES = 128
SWAP = [(0, 1), (1, 0)]
VMEM = pl.BlockSpec(memory_space=pltpu.VMEM)

epsilon = 1e-05


def chain(count, step):
    pairs = [(i, i + 1) for i in range(count - 1)]
    return pairs if step > 0 else [(b, a) for a, b in pairs]


def call(kernel, out_shape, scratch, flops, operands):
    held = [pltpu.with_memory_space_constraint(x, pltpu.VMEM) for x in operands]
    return pl.pallas_call(
        kernel,
        out_shape=jax.tree.map(lambda s: pltpu.VMEM(s.shape, s.dtype), out_shape),
        in_specs=[VMEM] * len(operands),
        out_specs=jax.tree.map(lambda _: VMEM, out_shape),
        scratch_shapes=scratch,
        cost_estimate=pl.CostEstimate(flops=flops, bytes_accessed=1 << 20, transcendentals=0),
        compiler_params=pltpu.CompilerParams(vmem_limit_bytes=16 << 20),
    )(*held)


def elu(v):
    return jnp.where(v > 0, v, jnp.exp(jnp.minimum(v, 0.0)) - 1.0)


def as_float(flag):
    return jnp.asarray(flag, jnp.int32).astype(jnp.float32)


def above_valid(row_at):
    return jnp.minimum(row_at, 1)


def below_valid(row_at, devices):
    return jnp.minimum(devices - 1 - row_at, 1)


def side_mask(core, channels, valid=1):
    lane = lax.broadcasted_iota(jnp.int32, (channels, LANES), 1)
    first = (LANES - STEP) * core
    return (lane >= first) & (lane < first + STEP * valid)


def edge_of(value, core):
    return jnp.where(core == 0, value[..., value.shape[-1] - LANES :], value[..., :LANES])


def term_rows(terms_ref, start, count):
    rows = terms_ref[pl.ds(pl.multiple_of(start, 16), count), :]
    return jnp.transpose(rows.astype(jnp.float32))


def column_of(row):
    return jnp.transpose(jnp.broadcast_to(row, (LANES, LANES)))[:, 0:1]


def arranged(taps_ref):
    return jnp.concatenate(
        [jnp.concatenate([taps_ref[3 * ky + kx] for ky in range(3)], axis=1) for kx in range(3)],
        axis=0,
    )


def flat_of(channels, rows, cols):
    return pltpu.VMEM((cols // LANES, channels * rows, LANES), jnp.float32)


def widen(source_ref, flat_ref):
    channels, rows, cols = source_ref.shape
    some = 64 // rows if channels % (64 // rows) == 0 else 1

    def step(i, _):
        for block in range(cols // LANES):
            value = source_ref[pl.ds(i * some, some), :, block * LANES : (block + 1) * LANES]
            flat_ref[block, pl.ds(pl.multiple_of(i * some * rows, 8), some * rows), :] = (
                value.astype(jnp.float32).reshape(some * rows, LANES)
            )
        return 0

    lax.fori_loop(0, channels // some, step, 0)


def conv_row(x_ref, row, weights):
    stacked = jnp.concatenate([x_ref[row], x_ref[row + STEP], x_ref[row + 2 * STEP]], axis=0)
    taps = jnp.dot(weights, stacked, preferred_element_type=jnp.float32)
    channels, cols = taps.shape[0] // 3, taps.shape[1]
    total = (
        pltpu.roll(taps[:channels], STEP, 1)
        + taps[channels : 2 * channels]
        + pltpu.roll(taps[2 * channels :], cols - STEP, 1)
    )
    return total[:, : cols - LANES]


def folded(value):
    return sum(value[:, i : i + LANES] for i in range(0, value.shape[1], LANES))


def conv_rows(x_ref, weights, rows, store):
    channels = x_ref.shape[1]

    def step(r, carry):
        total, squares = carry
        out = conv_row(x_ref, r, weights)
        store(r, out)
        return total + folded(out), squares + folded(out * out)

    zero = jnp.zeros((channels, LANES), jnp.float32)
    total, squares = lax.fori_loop(0, rows, step, (zero, zero))
    both = jnp.concatenate(
        [jnp.sum(total, axis=1, keepdims=True), jnp.sum(squares, axis=1, keepdims=True)], axis=0
    )
    return jnp.transpose(jnp.broadcast_to(both, (LANES, LANES)))[0:1]


def affine_of(which, stats_refs, gains_ref, cells):
    column = column_of(sum(jnp.sum(ref[...], axis=0, keepdims=True) for ref in stats_refs)) / cells
    gain_shift = column_of(gains_ref[which : which + 1])
    channels = LANES // 2
    average = column[:channels]
    spread = column[channels:] - average * average
    factor = gain_shift[:channels] * lax.rsqrt(spread + epsilon)
    return factor, gain_shift[channels:] - average * factor


def fill_block_in(
    x_ref, to, source, first, count, side_source, side_first, row_terms, skip, col_terms,
    side_terms, valid, core,
):
    cols = col_terms.shape[1]
    channels = col_terms.shape[0]
    mask, inside = side_mask(core, channels, valid), as_float(valid)
    flat, rows = source
    side_flat, side_rows = side_source
    for r in range(count):
        row = jnp.broadcast_to(row_terms[:, skip + r : skip + r + 1], (channels, LANES))
        for block in range(cols // LANES):
            at = slice(block * LANES, (block + 1) * LANES)
            main = flat[block, pl.ds(first + r, channels, stride=rows), :] + row + col_terms[:, at]
            x_ref[to + r, :, at] = (main * inside).astype(jnp.bfloat16)
        beyond = side_flat[0, pl.ds(side_first + r, channels, stride=side_rows), :]
        beyond = beyond + row + side_terms
        x_ref[to + r, :, cols:] = jnp.where(mask, beyond, 0.0).astype(jnp.bfloat16)


def first_kernel(
    devices, own, above, below, side, terms, taps,
    x_ref, conv_ref, edge_ref, give_ref, stats_ref, own_flat, above_flat, below_flat, side_flat,
):
    row_at, core = lax.axis_index(GX), lax.axis_index("gy")
    channels, rows, cols = own.shape
    half = rows // 2
    for ref, flat in ((own, own_flat), (above, above_flat), (below, below_flat), (side, side_flat)):
        widen(ref, flat)
    col_terms = term_rows(terms, core * cols, cols)[channels:]
    side_terms = term_rows(terms, jnp.where(core == 0, cols, cols - LANES), LANES)[channels:]

    def fill(to, flat, flat_rows, count, side_first, at, skip, valid):
        row_terms = term_rows(terms, at * rows, rows)[:channels]
        fill_block_in(
            x_ref, to, (flat, flat_rows), 0, count, (side_flat, rows + 2 * STEP), side_first,
            row_terms, skip, col_terms, side_terms, valid, core,
        )

    up, down = jnp.maximum(row_at - 1, 0), jnp.minimum(row_at + 1, devices - 1)
    fill(0, above_flat, STEP, STEP, 0, up, rows - STEP, above_valid(row_at))
    fill(STEP, own_flat, rows, rows, STEP, row_at, 0, 1)
    fill(STEP + rows, below_flat, STEP, STEP, STEP + rows, down, 0, below_valid(row_at, devices))

    def store(r, out):
        conv_ref[r] = out.astype(jnp.bfloat16)
        edge_ref[r] = edge_of(out, core).astype(jnp.bfloat16)

    stats = conv_rows(x_ref, arranged(taps), rows, store)
    stats_ref[...] = jnp.broadcast_to(stats, stats_ref.shape)
    give_ref[...] = x_ref[pl.ds(STEP + half * (1 - core), half), :, :cols]


def far_kernel(
    devices, near, edge_own, above, below, side, terms, taps,
    conv_ref, edge_ref, x_ref, above_flat, below_flat, side_flat,
):
    row_at, core = lax.axis_index(GX), lax.axis_index("gy")
    channels, _, cols = above.shape
    rows = near.shape[0] - 2 * STEP
    for ref, flat in ((above, above_flat), (below, below_flat), (side, side_flat)):
        widen(ref, flat)
    col_terms = term_rows(terms, core * cols, cols)[channels:]
    side_terms = term_rows(terms, jnp.where(core == 0, cols, cols - LANES), LANES)[channels:]

    def fill(to, flat, side_first, at, skip, valid):
        row_terms = term_rows(terms, at * rows, rows)[:channels]
        fill_block_in(
            x_ref, to, (flat, STEP), 0, STEP, (side_flat, 2 * STEP), side_first,
            row_terms, skip, col_terms, side_terms, valid, core,
        )

    up, down = jnp.maximum(row_at - 1, 0), jnp.minimum(row_at + 1, devices - 1)
    fill(0, above_flat, 0, up, 0, above_valid(row_at))
    fill(5 * STEP, below_flat, STEP, down, rows - STEP, below_valid(row_at, devices))
    x_ref[STEP : 3 * STEP] = near[: 2 * STEP]
    x_ref[3 * STEP : 5 * STEP] = near[rows:]
    w = arranged(taps)

    def step(r, _):
        for half in range(2):
            out = conv_row(x_ref, r + 3 * STEP * half, w)
            conv_ref[r + STEP * half] = out.astype(jnp.bfloat16)
            edge_ref[r + (STEP + rows) * half] = edge_of(out, core).astype(jnp.bfloat16)
        return 0

    lax.fori_loop(0, STEP, step, 0)
    edge_ref[STEP : STEP + rows] = edge_own[...]


def second_kernel(
    devices, cells, own, far, side, stats, stats_other, gains, taps,
    conv_ref, give_ref, stats_ref, a_ref,
):
    row_at, core = lax.axis_index(GX), lax.axis_index("gy")
    rows, channels, cols = own.shape
    half = rows // 2
    factor, offset = affine_of(0, (stats, stats_other), gains, cells)
    factor_side = jnp.broadcast_to(factor, (channels, LANES))
    offset_side = jnp.broadcast_to(offset, (channels, LANES))

    def fill(source, at, to, valid):
        inside = as_float(valid)
        for i in range(0, cols, LANES):
            value = source[at, :, i : i + LANES].astype(jnp.float32)
            value = elu(value * factor_side + offset_side) * inside
            a_ref[to, :, i : i + LANES] = value.astype(jnp.bfloat16)
        beyond = elu(side[to].astype(jnp.float32) * factor_side + offset_side)
        mask = side_mask(core, channels, valid)
        a_ref[to, :, cols:] = jnp.where(mask, beyond, 0.0).astype(jnp.bfloat16)

    def outer(r, _):
        fill(far, r, r, above_valid(row_at))
        fill(far, r + STEP, r + STEP + rows, below_valid(row_at, devices))
        return 0

    def inner(r, _):
        fill(own, r, r + STEP, 1)
        return 0

    lax.fori_loop(0, STEP, outer, 0)
    lax.fori_loop(0, rows, inner, 0)

    def store(r, out):
        conv_ref[r] = out.astype(jnp.bfloat16)

    stats = conv_rows(a_ref, arranged(taps), rows, store)
    stats_ref[...] = jnp.broadcast_to(stats, stats_ref.shape)
    give_ref[...] = conv_ref[pl.ds(half * (1 - core), half)]


def pack_kernel(
    cells, near, near_other, conv, conv_other, stats, stats_other, gains, out_ref, send_ref
):
    core = lax.axis_index("gy")
    rows, channels, cols = conv.shape
    half = rows // 2
    factor, offset = affine_of(1, (stats, stats_other), gains, cells)
    factor = jnp.broadcast_to(factor, (channels, LANES))
    offset = jnp.broadcast_to(offset, (channels, LANES))
    peers = cols // rows

    def block_out(block_in, value):
        value = block_in.astype(jnp.float32) + value.astype(jnp.float32) * factor + offset
        return elu(value).astype(jnp.bfloat16)

    def own(r, _):
        for i in range(0, cols, LANES):
            out_ref[r, :, i : i + LANES] = block_out(
                near[r + STEP, :, i : i + LANES], conv[r, :, i : i + LANES]
            )
        return 0

    lax.fori_loop(0, rows, own, 0)
    some = LANES // rows

    def place_cells(value, r, first):
        value = value.astype(jnp.float32)
        both = jnp.concatenate([value, pltpu.roll(value, LANES - STEP, 1)], axis=0)
        turned = jnp.transpose(both).reshape(some, 2, STEP, 2 * channels)[:, 0]
        send_ref[pl.ds(first, some), r] = turned.astype(jnp.bfloat16)

    def step(r, _):
        for i in range(0, cols, LANES):
            at = i // rows
            place_cells(out_ref[r + half * core, :, i : i + LANES], r, peers * core + at)
            other = block_out(near_other[r, :, i : i + LANES], conv_other[r, :, i : i + LANES])
            place_cells(other, r, peers * (1 - core) + at)
        return 0

    lax.fori_loop(0, half, step, 0)


def merge_kernel(own, received, other, out_ref, cells_ref, flat_ref):
    core = lax.axis_index("gy")
    rows, channels, cols = own.shape
    peers = other.shape[0]

    def gather(s, _):
        cells_ref[s, core] = received[peers * core + s].astype(jnp.float32)
        cells_ref[s, 1 - core] = other[s].astype(jnp.float32)
        return 0

    lax.fori_loop(0, peers, gather, 0)
    flat = cells_ref.reshape(cols * STEP, 2 * channels)
    for low in range(STEP):
        mirrored = jnp.transpose(flat[pl.ds(low, cols, stride=STEP), :])
        for high in range(rows // STEP):
            r = high * STEP + low
            value = own[r].astype(jnp.float32) + mirrored[channels * high : channels * (high + 1)]
            for block in range(cols // LANES):
                flat_ref[block, pl.ds(r, channels, stride=rows), :] = (
                    0.5 * value[:, block * LANES : (block + 1) * LANES]
                )

    def store(c, _):
        for block in range(cols // LANES):
            value = flat_ref[block, pl.ds(pl.multiple_of(c * rows, 8), rows), :]
            out_ref[c, :, block * LANES : (block + 1) * LANES] = value.astype(jnp.bfloat16)
        return 0

    lax.fori_loop(0, channels, store, 0)


def body(residue_feats, pair_feats, w_row, w_col, first_taps, second_taps, norm_scale, norm_shift):
    channels, rows, cols = pair_feats.shape
    cores = lax.axis_size("gy")
    devices = lax.axis_size(GX)
    first_core = lax.axis_index("gy") == 0
    cells = devices * rows * cores * cols
    half = rows // 2
    bf16, f32 = jnp.bfloat16, jnp.float32
    shape = jax.ShapeDtypeStruct
    conv_flops = 2 * 9 * channels * channels * rows * cols

    def edge(x):
        return jnp.where(first_core, x[..., cols - LANES :], x[..., :LANES])

    def swap(x):
        return lax.ppermute(x, "gy", SWAP)

    down = functools.partial(lax.ppermute, axis_name=GX, perm=chain(devices, 1))
    up = functools.partial(lax.ppermute, axis_name=GX, perm=chain(devices, -1))
    top, bottom = pair_feats[:, :STEP], pair_feats[:, STEP:]
    above_near, below_near = down(bottom), up(top)
    above_far, below_far = down(top), up(bottom)
    own_terms = jnp.dot(
        residue_feats, jnp.concatenate([w_row, w_col], axis=1), preferred_element_type=f32
    ).astype(bf16)
    terms = lax.all_to_all(
        jnp.broadcast_to(own_terms[None], (devices, *own_terms.shape)), GX, 0, 0, tiled=True
    )
    terms = terms.reshape(devices * rows, 2 * channels)
    gains = jnp.concatenate([norm_scale, norm_shift], axis=1)

    near_side = swap(
        jnp.concatenate([edge(above_near), edge(pair_feats), edge(below_near)], axis=1)
    )
    far_side = swap(jnp.concatenate([edge(above_far), edge(below_far)], axis=1))

    wide = cols + LANES
    near, conv_own, edge_own, near_give, stats = call(
        functools.partial(first_kernel, devices),
        (
            shape((rows + 2 * STEP, channels, wide), bf16),
            shape((rows, channels, cols), bf16),
            shape((rows, channels, LANES), bf16),
            shape((half, channels, cols), bf16),
            shape((devices, LANES), f32),
        ),
        [
            flat_of(channels, rows, cols),
            flat_of(channels, STEP, cols),
            flat_of(channels, STEP, cols),
            flat_of(channels, rows + 2 * STEP, LANES),
        ],
        conv_flops,
        (pair_feats, above_near, below_near, near_side, terms, first_taps),
    )
    stats = lax.all_to_all(stats, GX, 0, 0, tiled=True)
    stats_other = swap(stats)
    conv_far, edges = call(
        functools.partial(far_kernel, devices),
        (shape((2 * STEP, channels, cols), bf16), shape((rows + 2 * STEP, channels, LANES), bf16)),
        [
            pltpu.VMEM((6 * STEP, channels, wide), bf16),
            flat_of(channels, STEP, cols),
            flat_of(channels, STEP, cols),
            flat_of(channels, 2 * STEP, LANES),
        ],
        conv_flops,
        (near, edge_own, above_far, below_far, far_side, terms, first_taps),
    )
    edges = swap(edges)
    near_other = swap(near_give)
    conv_second, second_give, stats = call(
        functools.partial(second_kernel, devices, cells),
        (
            shape((rows, channels, cols), bf16),
            shape((half, channels, cols), bf16),
            shape((devices, LANES), f32),
        ),
        [pltpu.VMEM((rows + 2 * STEP, channels, wide), bf16)],
        conv_flops,
        (conv_own, conv_far, edges, stats, stats_other, gains, second_taps),
    )
    stats = lax.all_to_all(stats, GX, 0, 0, tiled=True)
    stats_other = swap(stats)
    conv_other = swap(second_give)
    block_out, send = call(
        functools.partial(pack_kernel, cells),
        (
            shape((rows, channels, cols), bf16),
            shape((devices, half, STEP, 2 * channels), bf16),
        ),
        [],
        conv_flops,
        (near, near_other, conv_second, conv_other, stats, stats_other, gains),
    )
    received = lax.all_to_all(send, GX, 0, 0, tiled=True)
    peers = devices // cores
    other = swap(jnp.where(first_core, received[peers:], received[:peers]))
    return call(
        merge_kernel,
        shape((channels, rows, cols), bf16),
        [pltpu.VMEM((peers, cores, half, STEP, 2 * channels), f32), flat_of(channels, rows, cols)],
        conv_flops,
        (block_out, received, other),
    )


def solution(mesh):
    torus = Mesh(
        mesh.devices.reshape(mesh.shape["grp"], 4, 16, mesh.shape["gy"]),
        ("grp", "gx_0", "gx_1", "gy"),
    )
    placed = (P(GRP_GX, None), P(None, GRP_GX, "gy"), P(), P(), P(), P(), P(), P())
    return jax.shard_map(
        body, mesh=torus, in_specs=placed, out_specs=P(None, GRP_GX, "gy"), check_vma=False
    )
```

profile of v0, /device:TPU:33, one launch (start us, length us, event | category | flops | bytes accessed | tf_op | source)
XLA Modules:
  0.0 207.4 jit_solution(16516677045047672355)
XLA Ops:
  0.0 2.3 %fusion.5 = (bf16[64,8,512]{2,1,0:T(8,128)(2,1)}, bf16[64,8,512]{2,1,0:T(8,128)(2,1)}) fusion(bf16[64,16,512]{2,1,0:T(8,128)(2,1)} %own.1), kind=kLoop, calls=%fused_computation.15 | loop fusion | bytes 2097152 | tf_op jit(solution)/shard_map/slice | solution.py:366
  2.3 1.3 collective-permute-start.1
  3.6 5.9 %collective-permute-start = (bf16[64,8,512]{2,1,0:T(8,128)(2,1)}, bf16[64,8,512]{2,1,0:T(8,128)(2,1)S(1)}, u32[]{:S(2)}, u32[]{:S(2)}) collective-permute-start(bf16[64,8,512]{2,1,0:T(8,128)(2,1)} %get-tuple-element.30), channel_id=1, source_target_pairs={{0,2},{2,4},{4,6},{6,8},{8,10},{10,12},{12,14},{14,16},{16,18},{18... | collective-permute-start | bytes 1572872 | tf_op jit(solution)/shard_map/ppermute | solution.py:367
  9.6 1.3 collective-permute-start.5
  10.9 5.1 %collective-permute-start.4 = (bf16[64,8,512]{2,1,0:T(8,128)(2,1)}, bf16[64,8,512]{2,1,0:T(8,128)(2,1)S(1)}, u32[]{:S(2)}, u32[]{:S(2)}) collective-permute-start(bf16[64,8,512]{2,1,0:T(8,128)(2,1)} %get-tuple-element.29), channel_id=1, source_target_pairs={{0,2},{2,4},{4,6},{6,8},{8,10},{10,12},{12,14},{14,16},{16,18},{18... | collective-permute-start | bytes 1572872 | tf_op jit(solution)/shard_map/ppermute | solution.py:368
  16.0 0.9 fusion
  17.6 30.9 %all-to-all-start = ((bf16[64,16,128]{2,1,0:T(8,128)(2,1)}), bf16[64,16,128]{2,1,0:T(8,128)(2,1)S(1)}, u32[]{:S(2)}, u32[]{:S(2)}) async-start(bf16[64,16,128]{2,1,0:T(8,128)(2,1)} %broadcast_in_dim.2), calls=%async_computation | async-start | bytes 524288 | tf_op jit(solution)/shard_map/all_to_all | solution.py:372
  49.5 2.0 collective-permute-start.2
  52.4 16.1 %all-to-all-done = bf16[64,16,128]{2,1,0:T(8,128)(2,1)S(1)} async-done(((bf16[64,16,128]{2,1,0:T(8,128)(2,1)}), bf16[64,16,128]{2,1,0:T(8,128)(2,1)S(1)}, u32[]{:S(2)}, u32[]{:S(2)}) %all-to-all-start) | async-done | bytes 262176 | tf_op jit(solution)/shard_map/all_to_all | solution.py:372
  68.5 0.9 copy-done.2
  69.4 9.2 %shard_map.82 = (bf16[32,64,640]{2,1,0:T(8,128)(2,1)S(1)}, bf16[16,64,512]{2,1,0:T(8,128)(2,1)S(1)}, bf16[16,64,128]{2,1,0:T(8,128)(2,1)S(1)}, bf16[8,64,512]{2,1,0:T(8,128)(2,1)S(1)}, f32[64,128]{1,0:T(8,128)S(1)}) custom-call(bf16[64,16,512]{2,1,0:T(8,128)(2,1)S(1)} %copy-done.1, bf16[64,8,512]{2,1,0:T(8,128)(2,1)S(1)} %collective-permute-done.above, ...), custom_call_target="tpu_custom_call" | custom-call | flops 603979776 | bytes 1048576 | tf_op jit(solution)/shard_map/pallas_call | solution.py:28
  78.6 5.6 %shard_map.83 = (bf16[16,64,512]{2,1,0:T(8,128)(2,1)S(1)}, bf16[32,64,128]{2,1,0:T(8,128)(2,1)S(1)}) custom-call(bf16[32,64,640]{2,1,0:T(8,128)(2,1)S(1)} %get-tuple-element.17.near, bf16[16,64,128]{2,1,0:T(8,128)(2,1)S(1)} %get-tuple-element.20.edge_own, bf16[64,8,512]{2,1,0:T(8,128)(2,1)S(1)} %collective-permute-done.4.above, ...), custom_call_target="tpu_custom_call" | custom-call | flops 603979776 | bytes 1048576 | tf_op jit(solution)/shard_map/pallas_call | solution.py:28
  84.2 2.4 %collective-permute-start.7 = (bf16[32,64,128]{2,1,0:T(8,128)(2,1)S(1)}, bf16[32,64,128]{2,1,0:T(8,128)(2,1)S(1)}, u32[]{:S(2)}, u32[]{:S(2)}) collective-permute-start(bf16[32,64,128]{2,1,0:T(8,128)(2,1)S(1)} %get-tuple-element.22), channel_id=1, source_target_pairs={{0,1},{1,0},{2,3},{3,2},{4,5},{5,4},{6,7},{7,6},{8,9},{9,8},{10,11... | collective-permute-start | bytes 1572872 | tf_op jit(solution)/shard_map/ppermute | solution.py:362
  86.6 22.6 %all_to_all.32 = f32[64,1,128]{2,1,0:T(1,128)S(1)} all-to-all(f32[64,1,128]{2,1,0:T(1,128)S(1)} %bitcast.18), channel_id=1, replica_groups=mesh['grp'=2,'gx_0'=4,'gx_1'=16,'gy'=2] {'gx_0','gx_1'}, dimensions={0} | all-to-all | bytes 65536 | tf_op jit(solution)/shard_map/all_to_all | solution.py:402
  109.2 1.7 collective-permute-start.8
  111.8 7.6 %shard_map.84 = (bf16[16,64,512]{2,1,0:T(8,128)(2,1)S(1)}, bf16[8,64,512]{2,1,0:T(8,128)(2,1)S(1)}, f32[64,128]{1,0:T(8,128)S(1)}) custom-call(bf16[16,64,512]{2,1,0:T(8,128)(2,1)S(1)} %get-tuple-element.19.own, bf16[16,64,512]{2,1,0:T(8,128)(2,1)S(1)} %get-tuple-element.21.far, bf16[32,64,128]{2,1,0:T(8,128)(2,1)S(1)} %collective-permute-done.7.side, ...), custom_call_target="tpu_custom_call" | custom-call | flops 603979776 | bytes 1048576 | tf_op jit(solution)/shard_map/pallas_call | solution.py:28
  119.8 17.6 %all_to_all.33 = f32[64,1,128]{2,1,0:T(1,128)S(1)} all-to-all(f32[64,1,128]{2,1,0:T(1,128)S(1)} %bitcast.19), channel_id=1, replica_groups=mesh['grp'=2,'gx_0'=4,'gx_1'=16,'gy'=2] {'gx_0','gx_1'}, dimensions={0} | all-to-all | bytes 65536 | tf_op jit(solution)/shard_map/all_to_all | solution.py:429
  137.4 1.8 collective-permute-start.10
  140.0 4.0 %shard_map.85 = (bf16[16,64,512]{2,1,0:T(8,128)(2,1)S(1)}, bf16[64,8,8,128]{3,2,1,0:T(8,128)(2,1)S(1)}) custom-call(bf16[32,64,640]{2,1,0:T(8,128)(2,1)S(1)} %get-tuple-element.17.near, bf16[8,64,512]{2,1,0:T(8,128)(2,1)S(1)} %collective-permute-done.3.near_other, bf16[16,64,512]{2,1,0:T(8,128)(2,1)S(1)} %get-tuple-element.24.conv, ...), custom_call_target="tpu_custom_call" | custom-call | flops 603979776 | bytes 1048576 | tf_op jit(solution)/shard_map/pallas_call | solution.py:28
  144.0 55.4 %all_to_all.34.received = bf16[64,8,8,128]{3,2,1,0:T(8,128)(2,1)S(1)} all-to-all(bf16[64,8,8,128]{3,2,1,0:T(8,128)(2,1)S(1)} %get-tuple-element.28), channel_id=1, replica_groups=mesh['grp'=2,'gx_0'=4,'gx_1'=16,'gy'=2] {'gx_0','gx_1'}, dimensions={0} | all-to-all | bytes 2097152 | tf_op jit(solution)/shard_map/all_to_all | solution.py:442
  199.5 3.5 %collective-permute-start.11 = (bf16[32,8,8,128]{3,2,1,0:T(8,128)(2,1)S(1)}, bf16[32,8,8,128]{3,2,1,0:T(8,128)(2,1)S(1)}, u32[]{:S(2)}, u32[]{:S(2)}) collective-permute-start(bf16[32,8,8,128]{3,2,1,0:T(8,128)(2,1)S(1)} %slice_select_fusion), channel_id=1, source_target_pairs={{0,1},{1,0},{2,3},{3,2},{4,5},{5,4},{6,7},{7,6},{8,9},{9,8},{10,11... | collective-permute-start | bytes 1572872 | tf_op jit(solution)/shard_map/ppermute | solution.py:362
  203.0 1.5 collective-permute-done.11.other
  204.5 1.9 shard_map.86
  206.4 1.0 copy.11
  (35 shorter events, 4.8 us)
Async XLA Ops:
  0.0 16.0 %copy-start = (bf16[16,256]{1,0:T(8,128)(2,1)S(1)}, bf16[16,256]{1,0:T(8,128)(2,1)}, u32[]{:S(2)}) copy-start(bf16[16,256]{1,0:T(8,128)(2,1)} %param.8) | copy-start | bytes 24580
  0.0 48.5 %copy-start.1 = (bf16[64,16,512]{2,1,0:T(8,128)(2,1)S(1)}, bf16[64,16,512]{2,1,0:T(8,128)(2,1)}, u32[]{:S(2)}) copy-start(bf16[64,16,512]{2,1,0:T(8,128)(2,1)} %own.1) | copy-start | bytes 3145732
  2.3 46.3 %collective-permute-start.1 = (bf16[64,8,512]{2,1,0:T(8,128)(2,1)}, bf16[64,8,512]{2,1,0:T(8,128)(2,1)S(1)}, u32[]{:S(2)}, u32[]{:S(2)}) collective-permute-start(bf16[64,8,512]{2,1,0:T(8,128)(2,1)} %get-tuple-element.29), channel_id=1, source_target_pairs={{2,0},{4,2},{6,4},{8,6},{10,8},{12,10},{14,12},{16,14},{18,16},{20... | collective-permute-start | bytes 1572872 | tf_op jit(solution)/shard_map/ppermute | solution.py:367
  3.6 45.0 %collective-permute-start = (bf16[64,8,512]{2,1,0:T(8,128)(2,1)}, bf16[64,8,512]{2,1,0:T(8,128)(2,1)S(1)}, u32[]{:S(2)}, u32[]{:S(2)}) collective-permute-start(bf16[64,8,512]{2,1,0:T(8,128)(2,1)} %get-tuple-element.30), channel_id=1, source_target_pairs={{0,2},{2,4},{4,6},{6,8},{8,10},{10,12},{12,14},{14,16},{16,18},{18... | collective-permute-start | bytes 1572872 | tf_op jit(solution)/shard_map/ppermute | solution.py:367
  9.6 42.0 %collective-permute-start.5 = (bf16[64,8,512]{2,1,0:T(8,128)(2,1)}, bf16[64,8,512]{2,1,0:T(8,128)(2,1)S(1)}, u32[]{:S(2)}, u32[]{:S(2)}) collective-permute-start(bf16[64,8,512]{2,1,0:T(8,128)(2,1)} %get-tuple-element.30), channel_id=1, source_target_pairs={{2,0},{4,2},{6,4},{8,6},{10,8},{12,10},{14,12},{16,14},{18,16},{20... | collective-permute-start | bytes 1572872 | tf_op jit(solution)/shard_map/ppermute | solution.py:368
  10.9 40.7 %collective-permute-start.4 = (bf16[64,8,512]{2,1,0:T(8,128)(2,1)}, bf16[64,8,512]{2,1,0:T(8,128)(2,1)S(1)}, u32[]{:S(2)}, u32[]{:S(2)}) collective-permute-start(bf16[64,8,512]{2,1,0:T(8,128)(2,1)} %get-tuple-element.29), channel_id=1, source_target_pairs={{0,2},{2,4},{4,6},{6,8},{8,10},{10,12},{12,14},{14,16},{16,18},{18... | collective-permute-start | bytes 1572872 | tf_op jit(solution)/shard_map/ppermute | solution.py:368
  17.6 50.8 %all-to-all-start = ((bf16[64,16,128]{2,1,0:T(8,128)(2,1)}), bf16[64,16,128]{2,1,0:T(8,128)(2,1)S(1)}, u32[]{:S(2)}, u32[]{:S(2)}) async-start(bf16[64,16,128]{2,1,0:T(8,128)(2,1)} %broadcast_in_dim.2), calls=%async_computation | async-start | bytes 524288 | tf_op jit(solution)/shard_map/all_to_all | solution.py:372
  49.5 18.9 %collective-permute-start.2 = (bf16[64,32,128]{2,1,0:T(8,128)(2,1)}, bf16[64,32,128]{2,1,0:T(8,128)(2,1)}, u32[]{:S(2)}, u32[]{:S(2)}) collective-permute-start(bf16[64,32,128]{2,1,0:T(8,128)(2,1)} %pad_maximum_fusion), channel_id=1, source_target_pairs={{0,1},{1,0},{2,3},{3,2},{4,5},{5,4},{6,7},{7,6},{8,9},{9,8},{10,11... | collective-permute-start | bytes 1572872 | tf_op jit(solution)/shard_map/ppermute | solution.py:362
  52.4 26.2 %collective-permute-start.6 = (bf16[64,16,128]{2,1,0:T(8,128)(2,1)}, bf16[64,16,128]{2,1,0:T(8,128)(2,1)}, u32[]{:S(2)}, u32[]{:S(2)}) collective-permute-start(bf16[64,16,128]{2,1,0:T(8,128)(2,1)} %pad_maximum_fusion.1), channel_id=1, source_target_pairs={{0,1},{1,0},{2,3},{3,2},{4,5},{5,4},{6,7},{7,6},{8,9},{9,8},{10,11... | collective-permute-start | bytes 786440 | tf_op jit(solution)/shard_map/ppermute | solution.py:362
  68.5 0.9 copy-start.2
  78.6 32.3 %copy-start.4 = (f32[2,64]{1,0:T(2,128)S(1)}, f32[2,64]{1,0:T(2,128)}, u32[]{:S(2)}) copy-start(f32[2,64]{1,0:T(2,128)} %param.15) | copy-start | bytes 1540
  78.6 32.3 %copy-start.5 = (f32[2,64]{1,0:T(2,128)S(1)}, f32[2,64]{1,0:T(2,128)}, u32[]{:S(2)}) copy-start(f32[2,64]{1,0:T(2,128)} %param.14) | copy-start | bytes 1540
  78.6 33.2 %copy-start.3 = (bf16[9,64,64]{2,1,0:T(8,128)(2,1)S(1)}, bf16[9,64,64]{2,1,0:T(8,128)(2,1)}, u32[]{:S(2)}) copy-start(bf16[9,64,64]{2,1,0:T(8,128)(2,1)} %taps.5) | copy-start | bytes 221188
  84.2 27.5 %collective-permute-start.7 = (bf16[32,64,128]{2,1,0:T(8,128)(2,1)S(1)}, bf16[32,64,128]{2,1,0:T(8,128)(2,1)S(1)}, u32[]{:S(2)}, u32[]{:S(2)}) collective-permute-start(bf16[32,64,128]{2,1,0:T(8,128)(2,1)S(1)} %get-tuple-element.22), channel_id=1, source_target_pairs={{0,1},{1,0},{2,3},{3,2},{4,5},{5,4},{6,7},{7,6},{8,9},{9,8},{10,11... | collective-permute-start | bytes 1572872 | tf_op jit(solution)/shard_map/ppermute | solution.py:362
  109.2 2.5 %collective-permute-start.8 = (f32[64,128]{1,0:T(8,128)S(1)}, f32[64,128]{1,0:T(8,128)S(1)}, u32[]{:S(2)}, u32[]{:S(2)}) collective-permute-start(f32[64,128]{1,0:T(8,128)S(1)} %bitcast.14), channel_id=1, source_target_pairs={{0,1},{1,0},{2,3},{3,2},{4,5},{5,4},{6,7},{7,6},{8,9},{9,8},{10,11... | collective-permute-start | bytes 98312 | tf_op jit(solution)/shard_map/ppermute | solution.py:362
  111.0 28.2 %collective-permute-start.3 = (bf16[8,64,512]{2,1,0:T(8,128)(2,1)S(1)}, bf16[8,64,512]{2,1,0:T(8,128)(2,1)S(1)}, u32[]{:S(2)}, u32[]{:S(2)}) collective-permute-start(bf16[8,64,512]{2,1,0:T(8,128)(2,1)S(1)} %get-tuple-element.18), channel_id=1, source_target_pairs={{0,1},{1,0},{2,3},{3,2},{4,5},{5,4},{6,7},{7,6},{8,9},{9,8},{10,11... | collective-permute-start | bytes 1572872 | tf_op jit(solution)/shard_map/ppermute | solution.py:362
  119.3 20.7 %collective-permute-start.9 = (bf16[8,64,512]{2,1,0:T(8,128)(2,1)S(1)}, bf16[8,64,512]{2,1,0:T(8,128)(2,1)S(1)}, u32[]{:S(2)}, u32[]{:S(2)}) collective-permute-start(bf16[8,64,512]{2,1,0:T(8,128)(2,1)S(1)} %get-tuple-element.25), channel_id=1, source_target_pairs={{0,1},{1,0},{2,3},{3,2},{4,5},{5,4},{6,7},{7,6},{8,9},{9,8},{10,11... | collective-permute-start | bytes 1572872 | tf_op jit(solution)/shard_map/ppermute | solution.py:362
  137.4 2.6 %collective-permute-start.10 = (f32[64,128]{1,0:T(8,128)S(1)}, f32[64,128]{1,0:T(8,128)S(1)}, u32[]{:S(2)}, u32[]{:S(2)}) collective-permute-start(f32[64,128]{1,0:T(8,128)S(1)} %bitcast.16), channel_id=1, source_target_pairs={{0,1},{1,0},{2,3},{3,2},{4,5},{5,4},{6,7},{7,6},{8,9},{9,8},{10,11... | collective-permute-start | bytes 98312 | tf_op jit(solution)/shard_map/ppermute | solution.py:362
  199.5 5.0 %collective-permute-start.11 = (bf16[32,8,8,128]{3,2,1,0:T(8,128)(2,1)S(1)}, bf16[32,8,8,128]{3,2,1,0:T(8,128)(2,1)S(1)}, u32[]{:S(2)}, u32[]{:S(2)}) collective-permute-start(bf16[32,8,8,128]{3,2,1,0:T(8,128)(2,1)S(1)} %slice_select_fusion), channel_id=1, source_target_pairs={{0,1},{1,0},{2,3},{3,2},{4,5},{5,4},{6,7},{7,6},{8,9},{9,8},{10,11... | collective-permute-start | bytes 1572872 | tf_op jit(solution)/shard_map/ppermute | solution.py:362
where the time goes:
time: 208 us; the launch traced here: 207 us
  blocking collectives  95.6 us (46%)
  starting transfers between devices  56.5 us (27%)
  Pallas kernels  28.2 us (14%)
  waiting for transfers between devices  19 us (9%)
  local copies, waits for them, and re-layouts  5 us (2%)
    all_to_all x1, blocking collectives, body(): received = lax.all_to_all(send, GX, 0, 0, tiled=True)  55.4 us
    all_to_all x2, blocking collectives, body(): stats = lax.all_to_all(stats, GX, 0, 0, tiled=True)  40.2 us
    all_to_all x1, starting transfers between devices, body(): lax.all_to_all(jnp.broadcast_to(own_terms[None], (devices, *own_terms.sha...  30.9 us
    pallas_call x5, Pallas kernels, call(): pl.pallas_call(kernel, out_shape=jax.tree.map(lambda s: pltpu.VMEM(s.shap...  28.2 us
    all_to_all x1, waiting for transfers between devices, body(): lax.all_to_all(jnp.broadcast_to(own_terms[None], (devices, *own_terms.sha...  16.1 us
    ppermute x8, starting transfers between devices, swap(): return lax.ppermute(x, 'gy', SWAP)  12.1 us
    ppermute x2, starting transfers between devices, body(): above_near, below_near = (down(bottom), up(top))  7.22 us
    ppermute x2, starting transfers between devices, body(): above_far, below_far = (down(top), up(bottom))  6.39 us
  transfers between devices with their start and end apart: 13, of which 4 were waited for; matrix products, arithmetic and copies ran while one was open for 2% of the time, Pallas kernels for 8%

commit v1 on v0

--- a/solution.py
+++ b/solution.py
@@ -13,7 +13,7 @@
 GRP_GX = ("grp", "gx_0", "gx_1")
 LANES = 128
 SWAP = [(0, 1), (1, 0)]
-VMEM = pl.BlockSpec(memory_space=pltpu.VMEM)
+HBM, VMEM = pltpu.HBM, pltpu.VMEM
 
 epsilon = 1e-05
 
@@ -23,17 +23,32 @@
     return pairs if step > 0 else [(b, a) for a, b in pairs]
 
 
-def call(kernel, out_shape, scratch, flops, operands):
-    held = [pltpu.with_memory_space_constraint(x, pltpu.VMEM) for x in operands]
+def call(kernel, outs, scratch, n_copies, flops, operands):
+    spaces = [space for space, _ in operands]
+    held = [pltpu.with_memory_space_constraint(x, space) for space, x in operands]
     return pl.pallas_call(
         kernel,
-        out_shape=jax.tree.map(lambda s: pltpu.VMEM(s.shape, s.dtype), out_shape),
-        in_specs=[VMEM] * len(operands),
-        out_specs=jax.tree.map(lambda _: VMEM, out_shape),
-        scratch_shapes=scratch,
+        out_shape=[space(shape, dtype) for space, shape, dtype in outs],
+        in_specs=[pl.BlockSpec(memory_space=space) for space in spaces],
+        out_specs=[pl.BlockSpec(memory_space=space) for space, _, _ in outs],
+        scratch_shapes=[*scratch, pltpu.SemaphoreType.DMA((n_copies,))],
         cost_estimate=pl.CostEstimate(flops=flops, bytes_accessed=1 << 20, transcendentals=0),
-        compiler_params=pltpu.CompilerParams(vmem_limit_bytes=16 << 20),
+        compiler_params=pltpu.CompilerParams(vmem_limit_bytes=24 << 20),
     )(*held)
+
+
+def start_all(sem, first, pairs):
+    copies = [
+        pltpu.make_async_copy(src, dst, sem.at[first + i]) for i, (src, dst) in enumerate(pairs)
+    ]
+    for copy in copies:
+        copy.start()
+    return copies
+
+
+def wait_all(copies):
+    for copy in copies:
+        copy.wait()
 
 
 def elu(v):
@@ -160,63 +175,112 @@
         x_ref[to + r, :, cols:] = jnp.where(mask, beyond, 0.0).astype(jnp.bfloat16)
 
 
+def prepare_kernel(
+    pair, feats, w_row, w_col, top_out, bottom_out, terms_ref, top, bottom, feats_in, row_in,
+    col_in, sem,
+):
+    halves = start_all(sem, 0, ((pair.at[:, :STEP], top), (pair.at[:, STEP:], bottom)))
+    inputs = start_all(sem, 2, ((feats, feats_in), (w_row, row_in), (w_col, col_in)))
+    wait_all(inputs)
+    terms = jnp.concatenate(
+        [
+            lax.dot_general(
+                feats_in[...], w[...], (((1,), (1,)), ((), ())), preferred_element_type=jnp.float32
+            )
+            for w in (row_in, col_in)
+        ],
+        axis=1,
+    ).astype(jnp.bfloat16)
+    terms_ref[...] = jnp.broadcast_to(terms[None], terms_ref.shape)
+    wait_all(halves)
+    wait_all(start_all(sem, 0, ((top, top_out), (bottom, bottom_out))))
+
+
 def first_kernel(
-    devices, own, above, below, side, terms, taps,
-    x_ref, conv_ref, edge_ref, give_ref, stats_ref, own_flat, above_flat, below_flat, side_flat,
+    devices, own_in, above_in, below_in, side_in, terms_in, taps_in,
+    near_out, conv_out, give_out, stats_ref,
+    x_ref, conv_ref, own, above, below, side, terms, taps,
+    own_flat, above_flat, below_flat, side_flat, sem,
 ):
     row_at, core = lax.axis_index(GX), lax.axis_index("gy")
     channels, rows, cols = own.shape
     half = rows // 2
-    for ref, flat in ((own, own_flat), (above, above_flat), (below, below_flat), (side, side_flat)):
-        widen(ref, flat)
+    inputs = start_all(
+        sem, 0,
+        ((terms_in, terms), (side_in, side), (above_in, above), (own_in, own), (below_in, below),
+         (taps_in, taps)),
+    )
+    inputs[0].wait()
     col_terms = term_rows(terms, core * cols, cols)[channels:]
     side_terms = term_rows(terms, jnp.where(core == 0, cols, cols - LANES), LANES)[channels:]
-
-    def fill(to, flat, flat_rows, count, side_first, at, skip, valid):
+    inputs[1].wait()
+    widen(side, side_flat)
+
+    def fill(copy, ref, to, flat, flat_rows, count, side_first, at, skip, valid):
         row_terms = term_rows(terms, at * rows, rows)[:channels]
+        copy.wait()
+        widen(ref, flat)
         fill_block_in(
             x_ref, to, (flat, flat_rows), 0, count, (side_flat, rows + 2 * STEP), side_first,
             row_terms, skip, col_terms, side_terms, valid, core,
         )
 
     up, down = jnp.maximum(row_at - 1, 0), jnp.minimum(row_at + 1, devices - 1)
-    fill(0, above_flat, STEP, STEP, 0, up, rows - STEP, above_valid(row_at))
-    fill(STEP, own_flat, rows, rows, STEP, row_at, 0, 1)
-    fill(STEP + rows, below_flat, STEP, STEP, STEP + rows, down, 0, below_valid(row_at, devices))
+    fill(inputs[2], above, 0, above_flat, STEP, STEP, 0, up, rows - STEP, above_valid(row_at))
+    fill(inputs[3], own, STEP, own_flat, rows, rows, STEP, row_at, 0, 1)
+    fill(inputs[4], below, STEP + rows, below_flat, STEP, STEP, STEP + rows, down, 0,
+         below_valid(row_at, devices))
+    given = x_ref.at[pl.ds(STEP + half * (1 - core), half), :, pl.ds(0, cols)]
+    outputs = start_all(sem, 6, ((x_ref, near_out), (given, give_out)))
+    inputs[5].wait()
 
     def store(r, out):
         conv_ref[r] = out.astype(jnp.bfloat16)
-        edge_ref[r] = edge_of(out, core).astype(jnp.bfloat16)
 
     stats = conv_rows(x_ref, arranged(taps), rows, store)
+    outputs += start_all(sem, 8, ((conv_ref, conv_out),))
     stats_ref[...] = jnp.broadcast_to(stats, stats_ref.shape)
-    give_ref[...] = x_ref[pl.ds(STEP + half * (1 - core), half), :, :cols]
+    wait_all(outputs)
 
 
 def far_kernel(
-    devices, near, edge_own, above, below, side, terms, taps,
-    conv_ref, edge_ref, x_ref, above_flat, below_flat, side_flat,
+    devices, near_in, own_in, above_in, below_in, side_in, terms_in, taps_in,
+    conv_out, edge_out,
+    x_ref, conv_ref, edge_ref, above, below, side, terms, taps,
+    above_flat, below_flat, side_flat, sem,
 ):
     row_at, core = lax.axis_index(GX), lax.axis_index("gy")
     channels, _, cols = above.shape
-    rows = near.shape[0] - 2 * STEP
-    for ref, flat in ((above, above_flat), (below, below_flat), (side, side_flat)):
-        widen(ref, flat)
+    rows = own_in.shape[0]
+    edge_at = pl.multiple_of((cols - LANES) * (1 - core), LANES)
+    inputs = start_all(
+        sem, 0,
+        ((terms_in, terms), (side_in, side), (above_in, above), (below_in, below),
+         (near_in.at[pl.ds(0, 2 * STEP)], x_ref.at[pl.ds(STEP, 2 * STEP)]),
+         (near_in.at[pl.ds(rows, 2 * STEP)], x_ref.at[pl.ds(3 * STEP, 2 * STEP)]),
+         (own_in.at[:, :, pl.ds(edge_at, LANES)], edge_ref.at[pl.ds(STEP, rows)]),
+         (taps_in, taps)),
+    )
+    inputs[0].wait()
     col_terms = term_rows(terms, core * cols, cols)[channels:]
     side_terms = term_rows(terms, jnp.where(core == 0, cols, cols - LANES), LANES)[channels:]
-
-    def fill(to, flat, side_first, at, skip, valid):
+    inputs[1].wait()
+    widen(side, side_flat)
+
+    def fill(copy, ref, to, flat, side_first, at, skip, valid):
         row_terms = term_rows(terms, at * rows, rows)[:channels]
+        copy.wait()
+        widen(ref, flat)
         fill_block_in(
             x_ref, to, (flat, STEP), 0, STEP, (side_flat, 2 * STEP), side_first,
             row_terms, skip, col_terms, side_terms, valid, core,
         )
 
     up, down = jnp.maximum(row_at - 1, 0), jnp.minimum(row_at + 1, devices - 1)
-    fill(0, above_flat, 0, up, 0, above_valid(row_at))
-    fill(5 * STEP, below_flat, STEP, down, rows - STEP, below_valid(row_at, devices))
-    x_ref[STEP : 3 * STEP] = near[: 2 * STEP]
-    x_ref[3 * STEP : 5 * STEP] = near[rows:]
+    fill(inputs[2], above, 0, above_flat, 0, up, 0, above_valid(row_at))
+    fill(inputs[3], below, 5 * STEP, below_flat, STEP, down, rows - STEP,
+         below_valid(row_at, devices))
+    wait_all(inputs[4:])
     w = arranged(taps)
 
     def step(r, _):
@@ -227,16 +291,20 @@
         return 0
 
     lax.fori_loop(0, STEP, step, 0)
-    edge_ref[STEP : STEP + rows] = edge_own[...]
+    wait_all(start_all(sem, 0, ((edge_ref, edge_out), (conv_ref, conv_out))))
 
 
 def second_kernel(
-    devices, cells, own, far, side, stats, stats_other, gains, taps,
-    conv_ref, give_ref, stats_ref, a_ref,
+    devices, cells, own_in, far_in, side_in, stats, stats_other, gains, taps_in,
+    conv_out, give_out, stats_ref,
+    a_ref, conv_ref, own, far, side, taps, sem,
 ):
     row_at, core = lax.axis_index(GX), lax.axis_index("gy")
     rows, channels, cols = own.shape
     half = rows // 2
+    inputs = start_all(
+        sem, 0, ((side_in, side), (far_in, far), (own_in, own), (taps_in, taps))
+    )
     factor, offset = affine_of(0, (stats, stats_other), gains, cells)
     factor_side = jnp.broadcast_to(factor, (channels, LANES))
     offset_side = jnp.broadcast_to(offset, (channels, LANES))
@@ -260,23 +328,34 @@
         fill(own, r, r + STEP, 1)
         return 0
 
+    wait_all(inputs[:2])
     lax.fori_loop(0, STEP, outer, 0)
+    wait_all(inputs[2:])
     lax.fori_loop(0, rows, inner, 0)
 
     def store(r, out):
         conv_ref[r] = out.astype(jnp.bfloat16)
 
     stats = conv_rows(a_ref, arranged(taps), rows, store)
+    given = conv_ref.at[pl.ds(half * (1 - core), half)]
+    outputs = start_all(sem, 0, ((given, give_out), (conv_ref, conv_out)))
     stats_ref[...] = jnp.broadcast_to(stats, stats_ref.shape)
-    give_ref[...] = conv_ref[pl.ds(half * (1 - core), half)]
+    wait_all(outputs)
 
 
 def pack_kernel(
-    cells, near, near_other, conv, conv_other, stats, stats_other, gains, out_ref, send_ref
+    cells, near_in, near_other_in, conv_in, conv_other_in, stats, stats_other, gains,
+    block_out_out, send_ref,
+    out_ref, near, near_other, conv, conv_other, sem,
 ):
     core = lax.axis_index("gy")
     rows, channels, cols = conv.shape
     half = rows // 2
+    inputs = start_all(
+        sem, 0,
+        ((near_in.at[pl.ds(STEP, rows), :, pl.ds(0, cols)], near), (conv_in, conv),
+         (near_other_in, near_other), (conv_other_in, conv_other)),
+    )
     factor, offset = affine_of(1, (stats, stats_other), gains, cells)
     factor = jnp.broadcast_to(factor, (channels, LANES))
     offset = jnp.broadcast_to(offset, (channels, LANES))
@@ -289,11 +368,13 @@
     def own(r, _):
         for i in range(0, cols, LANES):
             out_ref[r, :, i : i + LANES] = block_out(
-                near[r + STEP, :, i : i + LANES], conv[r, :, i : i + LANES]
+                near[r, :, i : i + LANES], conv[r, :, i : i + LANES]
             )
         return 0
 
+    wait_all(inputs[:2])
     lax.fori_loop(0, rows, own, 0)
+    outputs = start_all(sem, 4, ((out_ref, block_out_out),))
     some = LANES // rows
 
     def place_cells(value, r, first):
@@ -310,13 +391,16 @@
             place_cells(other, r, peers * (1 - core) + at)
         return 0
 
+    wait_all(inputs[2:])
     lax.fori_loop(0, half, step, 0)
-
-
-def merge_kernel(own, received, other, out_ref, cells_ref, flat_ref):
+    wait_all(outputs)
+
+
+def merge_kernel(own_in, received, other, result, out_ref, own, cells_ref, flat_ref, sem):
     core = lax.axis_index("gy")
     rows, channels, cols = own.shape
     peers = other.shape[0]
+    inputs = start_all(sem, 0, ((own_in, own),))
 
     def gather(s, _):
         cells_ref[s, core] = received[peers * core + s].astype(jnp.float32)
@@ -324,6 +408,7 @@
         return 0
 
     lax.fori_loop(0, peers, gather, 0)
+    wait_all(inputs)
     flat = cells_ref.reshape(cols * STEP, 2 * channels)
     for low in range(STEP):
         mirrored = jnp.transpose(flat[pl.ds(low, cols, stride=STEP), :])
@@ -341,7 +426,12 @@
             out_ref[c, :, block * LANES : (block + 1) * LANES] = value.astype(jnp.bfloat16)
         return 0
 
-    lax.fori_loop(0, channels, store, 0)
+    part = channels // 2
+    lax.fori_loop(0, part, store, 0)
+    outputs = start_all(sem, 1, ((out_ref.at[pl.ds(0, part)], result.at[pl.ds(0, part)]),))
+    lax.fori_loop(part, channels, store, 0)
+    outputs += start_all(sem, 2, ((out_ref.at[pl.ds(part, part)], result.at[pl.ds(part, part)]),))
+    wait_all(outputs)
 
 
 def body(residue_feats, pair_feats, w_row, w_col, first_taps, second_taps, norm_scale, norm_shift):
@@ -352,8 +442,8 @@
     cells = devices * rows * cores * cols
     half = rows // 2
     bf16, f32 = jnp.bfloat16, jnp.float32
-    shape = jax.ShapeDtypeStruct
     conv_flops = 2 * 9 * channels * channels * rows * cols
+    wide = cols + LANES
 
     def edge(x):
         return jnp.where(first_core, x[..., cols - LANES :], x[..., :LANES])
@@ -363,15 +453,28 @@
 
     down = functools.partial(lax.ppermute, axis_name=GX, perm=chain(devices, 1))
     up = functools.partial(lax.ppermute, axis_name=GX, perm=chain(devices, -1))
-    top, bottom = pair_feats[:, :STEP], pair_feats[:, STEP:]
+    eight = (channels, STEP, cols)
+    top, bottom, terms = call(
+        prepare_kernel,
+        (
+            (HBM, eight, bf16),
+            (HBM, eight, bf16),
+            (VMEM, (devices, rows, 2 * channels), bf16),
+        ),
+        [
+            VMEM(eight, bf16),
+            VMEM(eight, bf16),
+            VMEM(residue_feats.shape, bf16),
+            VMEM(w_row.T.shape, bf16),
+            VMEM(w_col.T.shape, bf16),
+        ],
+        5,
+        conv_flops // 16,
+        ((HBM, pair_feats), (HBM, residue_feats), (HBM, w_row.T), (HBM, w_col.T)),
+    )
     above_near, below_near = down(bottom), up(top)
     above_far, below_far = down(top), up(bottom)
-    own_terms = jnp.dot(
-        residue_feats, jnp.concatenate([w_row, w_col], axis=1), preferred_element_type=f32
-    ).astype(bf16)
-    terms = lax.all_to_all(
-        jnp.broadcast_to(own_terms[None], (devices, *own_terms.shape)), GX, 0, 0, tiled=True
-    )
+    terms = lax.all_to_all(terms, GX, 0, 0, tiled=True)
     terms = terms.reshape(devices * rows, 2 * channels)
     gains = jnp.concatenate([norm_scale, norm_shift], axis=1)
 
@@ -380,75 +483,113 @@
     )
     far_side = swap(jnp.concatenate([edge(above_far), edge(below_far)], axis=1))
 
-    wide = cols + LANES
-    near, conv_own, edge_own, near_give, stats = call(
+    taps_shape = VMEM(first_taps.shape, bf16)
+    terms_shape = VMEM(terms.shape, bf16)
+    whole = (rows, channels, cols)
+    part = (half, channels, cols)
+    sums = (devices, LANES)
+    near, conv_own, near_give, stats = call(
         functools.partial(first_kernel, devices),
         (
-            shape((rows + 2 * STEP, channels, wide), bf16),
-            shape((rows, channels, cols), bf16),
-            shape((rows, channels, LANES), bf16),
-            shape((half, channels, cols), bf16),
-            shape((devices, LANES), f32),
+            (HBM, (rows + 2 * STEP, channels, wide), bf16),
+            (HBM, whole, bf16),
+            (HBM, part, bf16),
+            (VMEM, sums, f32),
         ),
         [
+            VMEM((rows + 2 * STEP, channels, wide), bf16),
+            VMEM(whole, bf16),
+            VMEM(pair_feats.shape, bf16),
+            VMEM(eight, bf16),
+            VMEM(eight, bf16),
+            VMEM(near_side.shape, bf16),
+            terms_shape,
+            taps_shape,
             flat_of(channels, rows, cols),
             flat_of(channels, STEP, cols),
             flat_of(channels, STEP, cols),
             flat_of(channels, rows + 2 * STEP, LANES),
         ],
+        9,
         conv_flops,
-        (pair_feats, above_near, below_near, near_side, terms, first_taps),
+        ((HBM, pair_feats), (HBM, above_near), (HBM, below_near), (HBM, near_side),
+         (HBM, terms), (HBM, first_taps)),
     )
     stats = lax.all_to_all(stats, GX, 0, 0, tiled=True)
     stats_other = swap(stats)
     conv_far, edges = call(
         functools.partial(far_kernel, devices),
-        (shape((2 * STEP, channels, cols), bf16), shape((rows + 2 * STEP, channels, LANES), bf16)),
+        ((HBM, (2 * STEP, channels, cols), bf16), (HBM, (rows + 2 * STEP, channels, LANES), bf16)),
         [
-            pltpu.VMEM((6 * STEP, channels, wide), bf16),
+            VMEM((6 * STEP, channels, wide), bf16),
+            VMEM((2 * STEP, channels, cols), bf16),
+            VMEM((rows + 2 * STEP, channels, LANES), bf16),
+            VMEM(eight, bf16),
+            VMEM(eight, bf16),
+            VMEM(far_side.shape, bf16),
+            terms_shape,
+            taps_shape,
             flat_of(channels, STEP, cols),
             flat_of(channels, STEP, cols),
             flat_of(channels, 2 * STEP, LANES),
         ],
+        8,
         conv_flops,
-        (near, edge_own, above_far, below_far, far_side, terms, first_taps),
+        ((HBM, near), (HBM, conv_own), (HBM, above_far), (HBM, below_far), (HBM, far_side),
+         (HBM, terms), (HBM, first_taps)),
     )
     edges = swap(edges)
     near_other = swap(near_give)
     conv_second, second_give, stats = call(
         functools.partial(second_kernel, devices, cells),
-        (
-            shape((rows, channels, cols), bf16),
-            shape((half, channels, cols), bf16),
-            shape((devices, LANES), f32),
-        ),
-        [pltpu.VMEM((rows + 2 * STEP, channels, wide), bf16)],
+        ((HBM, whole, bf16), (HBM, part, bf16), (VMEM, sums, f32)),
+        [
+            VMEM((rows + 2 * STEP, channels, wide), bf16),
+            VMEM(whole, bf16),
+            VMEM(whole, bf16),
+            VMEM((2 * STEP, channels, cols), bf16),
+            VMEM(edges.shape, bf16),
+            taps_shape,
+        ],
+        4,
         conv_flops,
-        (conv_own, conv_far, edges, stats, stats_other, gains, second_taps),
+        ((HBM, conv_own), (HBM, conv_far), (HBM, edges), (VMEM, stats), (VMEM, stats_other),
+         (VMEM, gains), (HBM, second_taps)),
     )
     stats = lax.all_to_all(stats, GX, 0, 0, tiled=True)
     stats_other = swap(stats)
     conv_other = swap(second_give)
     block_out, send = call(
         functools.partial(pack_kernel, cells),
-        (
-            shape((rows, channels, cols), bf16),
-            shape((devices, half, STEP, 2 * channels), bf16),
-        ),
-        [],
+        ((HBM, whole, bf16), (VMEM, (devices, half, STEP, 2 * channels), bf16)),
+        [
+            VMEM(whole, bf16),
+            VMEM(whole, bf16),
+            VMEM(part, bf16),
+            VMEM(whole, bf16),
+            VMEM(part, bf16),
+        ],
+        5,
         conv_flops,
-        (near, near_other, conv_second, conv_other, stats, stats_other, gains),
+        ((HBM, near), (HBM, near_other), (HBM, conv_second), (HBM, conv_other),
+         (VMEM, stats), (VMEM, stats_other), (VMEM, gains)),
     )
     received = lax.all_to_all(send, GX, 0, 0, tiled=True)
     peers = devices // cores
     other = swap(jnp.where(first_core, received[peers:], received[:peers]))
     return call(
         merge_kernel,
-        shape((channels, rows, cols), bf16),
-        [pltpu.VMEM((peers, cores, half, STEP, 2 * channels), f32), flat_of(channels, rows, cols)],
+        ((HBM, pair_feats.shape, bf16),),
+        [
+            VMEM(pair_feats.shape, bf16),
+            VMEM(whole, bf16),
+            VMEM((peers, cores, half, STEP, 2 * channels), f32),
+            flat_of(channels, rows, cols),
+        ],
+        3,
         conv_flops,
-        (block_out, received, other),
-    )
+        ((HBM, block_out), (VMEM, received), (VMEM, other)),
+    )[0]
 
 
 def solution(mesh):

time: 208 us -> 217 us (1.043)
  Pallas kernels: 28.2 us -> 38.7 us
  blocking collectives: 95.6 us -> 99.8 us
  local copies, waits for them, and re-layouts: 5 us -> 2.54 us
  waiting for transfers between devices: 19 us -> 16.7 us
    pallas_call x5 -> x6, Pallas kernels: 28.2 us -> 38.7 us  [call(): pl.pallas_call(kernel, out_shape=[space(shape, dtype) for space, shape, d...]
    all_to_all x2, blocking collectives: 40.2 us -> 44.4 us  [body(): stats = lax.all_to_all(stats, GX, 0, 0, tiled=True)]
    all_to_all x1, waiting for transfers between devices: 16.1 us -> 13.6 us  [body(): terms = lax.all_to_all(terms, GX, 0, 0, tiled=True)]
    slice x1 -> x0, local copies, waits for them, and re-layouts: 2.32 us -> none  [body(): top, bottom = (pair_feats[:, :STEP], pair_feats[:, STEP:])]
  transfers between devices with their start and end apart: 13 -> 13, of which waited for: 4 -> 4; matrix products, arithmetic and copies ran while one was open for 2% -> 1% of each run, Pallas kernels for 8% -> 9%
where the time goes in v1:
time: 217 us; the launch traced here: 216 us
  blocking collectives  99.8 us (46%)
  starting transfers between devices  56 us (26%)
  Pallas kernels  38.7 us (18%)
  waiting for transfers between devices  16.7 us (8%)
  local copies, waits for them, and re-layouts  2.54 us (1%)
  other arithmetic  2.26 us (1%)
    all_to_all x1, blocking collectives, body(): received = lax.all_to_all(send, GX, 0, 0, tiled=True)  55.4 us
    all_to_all x2, blocking collectives, body(): stats = lax.all_to_all(stats, GX, 0, 0, tiled=True)  44.4 us
    pallas_call x6, Pallas kernels, call(): pl.pallas_call(kernel, out_shape=[space(shape, dtype) for space, shape, d...  38.7 us
    all_to_all x1, starting transfers between devices, body(): terms = lax.all_to_all(terms, GX, 0, 0, tiled=True)  28.8 us
    all_to_all x1, waiting for transfers between devices, body(): terms = lax.all_to_all(terms, GX, 0, 0, tiled=True)  13.6 us
    ppermute x8, starting transfers between devices, swap(): return lax.ppermute(x, 'gy', SWAP)  13.6 us
    ppermute x2, starting transfers between devices, body(): above_far, below_far = (down(top), up(bottom))  7.03 us
    ppermute x2, starting transfers between devices, body(): above_near, below_near = (down(bottom), up(top))  6.59 us
  transfers between devices with their start and end apart: 13, of which 4 were waited for; matrix products, arithmetic and copies ran while one was open for 1% of the time, Pallas kernels for 9%

profile of v1, /device:TPU:33, one launch (start us, length us, event | category | flops | bytes accessed | tf_op | source)
XLA Modules:
  0.0 216.4 jit_solution(16140078211672844401)
XLA Ops:
  0.0 3.1 %shard_map.82 = (bf16[64,8,512]{2,1,0:T(8,128)(2,1)}, bf16[64,8,512]{2,1,0:T(8,128)(2,1)}, bf16[64,16,128]{2,1,0:T(8,128)(2,1)}) custom-call(bf16[64,16,512]{2,1,0:T(8,128)(2,1)} %own_in.1, bf16[16,256]{1,0:T(8,128)(2,1)} %feats.1, bf16[64,256]{1,0:T(8,128)(2,1)} %bitcast.19, bf16[64,256]{1,0:T(8,128)(2,1)} %bitcast.20), custom_call_target="tpu_custom_call" | custom-call | flops 37748736 | bytes 1048576 | tf_op jit(solution)/shard_map/pallas_call | solution.py:29
  3.1 5.3 %collective-permute-start = (bf16[64,8,512]{2,1,0:T(8,128)(2,1)}, bf16[64,8,512]{2,1,0:T(8,128)(2,1)S(1)}, u32[]{:S(2)}, u32[]{:S(2)}) collective-permute-start(bf16[64,8,512]{2,1,0:T(8,128)(2,1)} %get-tuple-element.19), channel_id=1, source_target_pairs={{0,2},{2,4},{4,6},{6,8},{8,10},{10,12},{12,14},{14,16},{16,18},{18... | collective-permute-start | bytes 1572872 | tf_op jit(solution)/shard_map/ppermute | solution.py:475
  8.4 1.3 collective-permute-start.1
  9.7 1.3 collective-permute-start.5
  11.0 5.7 %collective-permute-start.4 = (bf16[64,8,512]{2,1,0:T(8,128)(2,1)}, bf16[64,8,512]{2,1,0:T(8,128)(2,1)S(1)}, u32[]{:S(2)}, u32[]{:S(2)}) collective-permute-start(bf16[64,8,512]{2,1,0:T(8,128)(2,1)} %get-tuple-element.20), channel_id=1, source_target_pairs={{0,2},{2,4},{4,6},{6,8},{8,10},{10,12},{12,14},{14,16},{16,18},{18... | collective-permute-start | bytes 1572872 | tf_op jit(solution)/shard_map/ppermute | solution.py:476
  16.7 28.8 %all-to-all-start = ((bf16[64,16,128]{2,1,0:T(8,128)(2,1)}), bf16[64,16,128]{2,1,0:T(8,128)(2,1)S(1)}, u32[]{:S(2)}, u32[]{:S(2)}) async-start(bf16[64,16,128]{2,1,0:T(8,128)(2,1)} %get-tuple-element.21), calls=%async_computation | async-start | bytes 524288 | tf_op jit(solution)/shard_map/all_to_all | solution.py:477
  45.5 1.1 slice_select_fusion.1
  46.7 2.1 collective-permute-start.2
  49.0 0.9 pad_maximum_fusion.1
  50.0 13.6 %all-to-all-done = bf16[64,16,128]{2,1,0:T(8,128)(2,1)S(1)} async-done(((bf16[64,16,128]{2,1,0:T(8,128)(2,1)}), bf16[64,16,128]{2,1,0:T(8,128)(2,1)S(1)}, u32[]{:S(2)}, u32[]{:S(2)}) %all-to-all-start) | async-done | bytes 262176 | tf_op jit(solution)/shard_map/all_to_all | solution.py:477
  64.5 10.0 %shard_map.83 = (bf16[32,64,640]{2,1,0:T(8,128)(2,1)}, bf16[16,64,512]{2,1,0:T(8,128)(2,1)}, bf16[8,64,512]{2,1,0:T(8,128)(2,1)}, f32[64,128]{1,0:T(8,128)S(1)}) custom-call(bf16[64,16,512]{2,1,0:T(8,128)(2,1)} %own_in.1, bf16[64,8,512]{2,1,0:T(8,128)(2,1)} %copy-done.1, bf16[64,8,512]{2,1,0:T(8,128)(2,1)} %copy-done.2, bf16[64,32,128]{2,1,0:T(8,128)(2,1)} %copy-done.6, ...), custom_call_target="tpu_custom_call" | custom-call | flops 603979776 | bytes 1048576 | tf_op jit(solution)/shard_map/pallas_call | solution.py:29
  74.5 6.8 %shard_map.84 = (bf16[16,64,512]{2,1,0:T(8,128)(2,1)}, bf16[32,64,128]{2,1,0:T(8,128)(2,1)}) custom-call(bf16[32,64,640]{2,1,0:T(8,128)(2,1)} %get-tuple-element.22.near_in, bf16[16,64,512]{2,1,0:T(8,128)(2,1)} %get-tuple-element.24.own_in, bf16[64,8,512]{2,1,0:T(8,128)(2,1)} %copy-done.4, bf16[64,8,512]{2,1,0:T(8,128)(2,1)} %copy-done.3, ...), custom_call_target="tpu_custom_call" | custom-call | flops 603979776 | bytes 1048576 | tf_op jit(solution)/shard_map/pallas_call | solution.py:29
  81.4 3.7 %collective-permute-start.7 = (bf16[32,64,128]{2,1,0:T(8,128)(2,1)}, bf16[32,64,128]{2,1,0:T(8,128)(2,1)S(1)}, u32[]{:S(2)}, u32[]{:S(2)}) collective-permute-start(bf16[32,64,128]{2,1,0:T(8,128)(2,1)} %get-tuple-element.26), channel_id=1, source_target_pairs={{0,1},{1,0},{2,3},{3,2},{4,5},{5,4},{6,7},{7,6},{8,9},{9,8},{10,11... | collective-permute-start | bytes 1572872 | tf_op jit(solution)/shard_map/ppermute | solution.py:452
  85.0 26.8 %all_to_all.32 = f32[64,1,128]{2,1,0:T(1,128)S(1)} all-to-all(f32[64,1,128]{2,1,0:T(1,128)S(1)} %bitcast.15), channel_id=1, replica_groups=mesh['grp'=2,'gx_0'=4,'gx_1'=16,'gy'=2] {'gx_0','gx_1'}, dimensions={0} | all-to-all | bytes 65536 | tf_op jit(solution)/shard_map/all_to_all | solution.py:518
  111.9 1.7 collective-permute-start.8
  115.2 9.7 %shard_map.85 = (bf16[16,64,512]{2,1,0:T(8,128)(2,1)}, bf16[8,64,512]{2,1,0:T(8,128)(2,1)}, f32[64,128]{1,0:T(8,128)S(1)}) custom-call(bf16[16,64,512]{2,1,0:T(8,128)(2,1)} %get-tuple-element.24.own_in, bf16[16,64,512]{2,1,0:T(8,128)(2,1)} %get-tuple-element.25.far_in, bf16[32,64,128]{2,1,0:T(8,128)(2,1)} %copy-done.5, f32[64,128]{1,0:T(8,128)S(1)} %bitcast.12, ...), custom_call_target="tpu_custom_call" | custom-call | flops 603979776 | bytes 1048576 | tf_op jit(solution)/shard_map/pallas_call | solution.py:29
  125.6 17.6 %all_to_all.33 = f32[64,1,128]{2,1,0:T(1,128)S(1)} all-to-all(f32[64,1,128]{2,1,0:T(1,128)S(1)} %bitcast.16), channel_id=1, replica_groups=mesh['grp'=2,'gx_0'=4,'gx_1'=16,'gy'=2] {'gx_0','gx_1'}, dimensions={0} | all-to-all | bytes 65536 | tf_op jit(solution)/shard_map/all_to_all | solution.py:559
  143.2 1.8 collective-permute-start.10
  145.0 0.9 collective-permute-done.10.stats_other
  146.7 5.4 %shard_map.86 = (bf16[16,64,512]{2,1,0:T(8,128)(2,1)}, bf16[64,8,8,128]{3,2,1,0:T(8,128)(2,1)S(1)}) custom-call(bf16[32,64,640]{2,1,0:T(8,128)(2,1)} %get-tuple-element.22.near_in, bf16[8,64,512]{2,1,0:T(8,128)(2,1)} %copy-done.7, bf16[16,64,512]{2,1,0:T(8,128)(2,1)} %get-tuple-element.28.conv_in, bf16[8,64,512]{2,1,0:T(8,128)(2,1)} %copy-done.8, ...), custom_call_target="tpu_custom_call" | custom-call | flops 603979776 | bytes 1048576 | tf_op jit(solution)/shard_map/pallas_call | solution.py:29
  152.1 55.4 %all_to_all.34.received = bf16[64,8,8,128]{3,2,1,0:T(8,128)(2,1)S(1)} all-to-all(bf16[64,8,8,128]{3,2,1,0:T(8,128)(2,1)S(1)} %get-tuple-element.32), channel_id=1, replica_groups=mesh['grp'=2,'gx_0'=4,'gx_1'=16,'gy'=2] {'gx_0','gx_1'}, dimensions={0} | all-to-all | bytes 2097152 | tf_op jit(solution)/shard_map/all_to_all | solution.py:577
  207.6 3.4 %collective-permute-start.11 = (bf16[32,8,8,128]{3,2,1,0:T(8,128)(2,1)S(1)}, bf16[32,8,8,128]{3,2,1,0:T(8,128)(2,1)S(1)}, u32[]{:S(2)}, u32[]{:S(2)}) collective-permute-start(bf16[32,8,8,128]{3,2,1,0:T(8,128)(2,1)S(1)} %slice_select_fusion), channel_id=1, source_target_pairs={{0,1},{1,0},{2,3},{3,2},{4,5},{5,4},{6,7},{7,6},{8,9},{9,8},{10,11... | collective-permute-start | bytes 1572872 | tf_op jit(solution)/shard_map/ppermute | solution.py:452
  211.0 1.5 collective-permute-done.11.other
  212.5 3.7 %shard_map.87 = bf16[64,16,512]{2,1,0:T(8,128)(2,1)} custom-call(bf16[16,64,512]{2,1,0:T(8,128)(2,1)} %get-tuple-element.31.own_in, bf16[64,8,8,128]{3,2,1,0:T(8,128)(2,1)S(1)} %all_to_all.34.received, bf16[32,8,8,128]{3,2,1,0:T(8,128)(2,1)S(1)} %collective-permute-done.11.other), custom_call_target="tpu_custom_call" | custom-call | flops 603979776 | bytes 1048576 | tf_op jit(solution)/shard_map/pallas_call | solution.py:29
  (44 shorter events, 4.4 us)
Async XLA Ops:
  3.1 43.5 %collective-permute-start = (bf16[64,8,512]{2,1,0:T(8,128)(2,1)}, bf16[64,8,512]{2,1,0:T(8,128)(2,1)S(1)}, u32[]{:S(2)}, u32[]{:S(2)}) collective-permute-start(bf16[64,8,512]{2,1,0:T(8,128)(2,1)} %get-tuple-element.19), channel_id=1, source_target_pairs={{0,2},{2,4},{4,6},{6,8},{8,10},{10,12},{12,14},{14,16},{16,18},{18... | collective-permute-start | bytes 1572872 | tf_op jit(solution)/shard_map/ppermute | solution.py:475
  8.4 38.3 %collective-permute-start.1 = (bf16[64,8,512]{2,1,0:T(8,128)(2,1)}, bf16[64,8,512]{2,1,0:T(8,128)(2,1)S(1)}, u32[]{:S(2)}, u32[]{:S(2)}) collective-permute-start(bf16[64,8,512]{2,1,0:T(8,128)(2,1)} %get-tuple-element.20), channel_id=1, source_target_pairs={{2,0},{4,2},{6,4},{8,6},{10,8},{12,10},{14,12},{16,14},{18,16},{20... | collective-permute-start | bytes 1572872 | tf_op jit(solution)/shard_map/ppermute | solution.py:475
  9.7 39.2 %collective-permute-start.5 = (bf16[64,8,512]{2,1,0:T(8,128)(2,1)}, bf16[64,8,512]{2,1,0:T(8,128)(2,1)S(1)}, u32[]{:S(2)}, u32[]{:S(2)}) collective-permute-start(bf16[64,8,512]{2,1,0:T(8,128)(2,1)} %get-tuple-element.19), channel_id=1, source_target_pairs={{2,0},{4,2},{6,4},{8,6},{10,8},{12,10},{14,12},{16,14},{18,16},{20... | collective-permute-start | bytes 1572872 | tf_op jit(solution)/shard_map/ppermute | solution.py:476
  11.0 37.9 %collective-permute-start.4 = (bf16[64,8,512]{2,1,0:T(8,128)(2,1)}, bf16[64,8,512]{2,1,0:T(8,128)(2,1)S(1)}, u32[]{:S(2)}, u32[]{:S(2)}) collective-permute-start(bf16[64,8,512]{2,1,0:T(8,128)(2,1)} %get-tuple-element.20), channel_id=1, source_target_pairs={{0,2},{2,4},{4,6},{6,8},{8,10},{10,12},{12,14},{14,16},{16,18},{18... | collective-permute-start | bytes 1572872 | tf_op jit(solution)/shard_map/ppermute | solution.py:476
  16.7 46.9 %all-to-all-start = ((bf16[64,16,128]{2,1,0:T(8,128)(2,1)}), bf16[64,16,128]{2,1,0:T(8,128)(2,1)S(1)}, u32[]{:S(2)}, u32[]{:S(2)}) async-start(bf16[64,16,128]{2,1,0:T(8,128)(2,1)} %get-tuple-element.21), calls=%async_computation | async-start | bytes 524288 | tf_op jit(solution)/shard_map/all_to_all | solution.py:477
  46.6 17.0 %copy-start.1 = (bf16[64,8,512]{2,1,0:T(8,128)(2,1)}, bf16[64,8,512]{2,1,0:T(8,128)(2,1)S(1)}, u32[]{:S(2)}) copy-start(bf16[64,8,512]{2,1,0:T(8,128)(2,1)S(1)} %collective-permute-done.above_in) | copy-start | bytes 1572868
  46.6 17.0 %copy-start.2 = (bf16[64,8,512]{2,1,0:T(8,128)(2,1)}, bf16[64,8,512]{2,1,0:T(8,128)(2,1)S(1)}, u32[]{:S(2)}) copy-start(bf16[64,8,512]{2,1,0:T(8,128)(2,1)S(1)} %collective-permute-done.1.below_in) | copy-start | bytes 1572868
  46.7 16.9 %collective-permute-start.2 = (bf16[64,32,128]{2,1,0:T(8,128)(2,1)S(1)}, bf16[64,32,128]{2,1,0:T(8,128)(2,1)S(1)}, u32[]{:S(2)}, u32[]{:S(2)}) collective-permute-start(bf16[64,32,128]{2,1,0:T(8,128)(2,1)S(1)} %pad_maximum_fusion), channel_id=1, source_target_pairs={{0,1},{1,0},{2,3},{3,2},{4,5},{5,4},{6,7},{7,6},{8,9},{9,8},{10,11... | collective-permute-start | bytes 1572872 | tf_op jit(solution)/shard_map/ppermute | solution.py:452
  48.9 25.6 %copy-start.3 = (bf16[64,8,512]{2,1,0:T(8,128)(2,1)}, bf16[64,8,512]{2,1,0:T(8,128)(2,1)S(1)}, u32[]{:S(2)}) copy-start(bf16[64,8,512]{2,1,0:T(8,128)(2,1)S(1)} %collective-permute-done.5.below_in) | copy-start | bytes 1572868
  48.9 25.6 %copy-start.4 = (bf16[64,8,512]{2,1,0:T(8,128)(2,1)}, bf16[64,8,512]{2,1,0:T(8,128)(2,1)S(1)}, u32[]{:S(2)}) copy-start(bf16[64,8,512]{2,1,0:T(8,128)(2,1)S(1)} %collective-permute-done.4.above_in) | copy-start | bytes 1572868
  49.9 24.6 %collective-permute-start.6 = (bf16[64,16,128]{2,1,0:T(8,128)(2,1)}, bf16[64,16,128]{2,1,0:T(8,128)(2,1)}, u32[]{:S(2)}, u32[]{:S(2)}) collective-permute-start(bf16[64,16,128]{2,1,0:T(8,128)(2,1)} %pad_maximum_fusion.1), channel_id=1, source_target_pairs={{0,1},{1,0},{2,3},{3,2},{4,5},{5,4},{6,7},{7,6},{8,9},{9,8},{10,11... | collective-permute-start | bytes 786440 | tf_op jit(solution)/shard_map/ppermute | solution.py:452
  63.6 0.9 copy-start.6
  74.5 39.0 %copy-start.9 = (f32[2,64]{1,0:T(2,128)S(1)}, f32[2,64]{1,0:T(2,128)}, u32[]{:S(2)}) copy-start(f32[2,64]{1,0:T(2,128)} %param.15) | copy-start | bytes 1540
  74.5 39.0 %copy-start.10 = (f32[2,64]{1,0:T(2,128)S(1)}, f32[2,64]{1,0:T(2,128)}, u32[]{:S(2)}) copy-start(f32[2,64]{1,0:T(2,128)} %param.14) | copy-start | bytes 1540
  74.5 39.1 %copy-start.11 = (bf16[8,64,512]{2,1,0:T(8,128)(2,1)S(1)}, bf16[8,64,512]{2,1,0:T(8,128)(2,1)}, u32[]{:S(2)}) copy-start(bf16[8,64,512]{2,1,0:T(8,128)(2,1)} %get-tuple-element.23) | copy-start | bytes 1572868
  81.4 33.0 %collective-permute-start.7 = (bf16[32,64,128]{2,1,0:T(8,128)(2,1)}, bf16[32,64,128]{2,1,0:T(8,128)(2,1)S(1)}, u32[]{:S(2)}, u32[]{:S(2)}) collective-permute-start(bf16[32,64,128]{2,1,0:T(8,128)(2,1)} %get-tuple-element.26), channel_id=1, source_target_pairs={{0,1},{1,0},{2,3},{3,2},{4,5},{5,4},{6,7},{7,6},{8,9},{9,8},{10,11... | collective-permute-start | bytes 1572872 | tf_op jit(solution)/shard_map/ppermute | solution.py:452
  111.9 2.5 %collective-permute-start.8 = (f32[64,128]{1,0:T(8,128)S(1)}, f32[64,128]{1,0:T(8,128)S(1)}, u32[]{:S(2)}, u32[]{:S(2)}) collective-permute-start(f32[64,128]{1,0:T(8,128)S(1)} %bitcast.11), channel_id=1, source_target_pairs={{0,1},{1,0},{2,3},{3,2},{4,5},{5,4},{6,7},{7,6},{8,9},{9,8},{10,11... | collective-permute-start | bytes 98312 | tf_op jit(solution)/shard_map/ppermute | solution.py:452
  113.6 31.4 %collective-permute-start.3 = (bf16[8,64,512]{2,1,0:T(8,128)(2,1)S(1)}, bf16[8,64,512]{2,1,0:T(8,128)(2,1)S(1)}, u32[]{:S(2)}, u32[]{:S(2)}) collective-permute-start(bf16[8,64,512]{2,1,0:T(8,128)(2,1)S(1)} %copy-done.11), channel_id=1, source_target_pairs={{0,1},{1,0},{2,3},{3,2},{4,5},{5,4},{6,7},{7,6},{8,9},{9,8},{10,11... | collective-permute-start | bytes 1572872 | tf_op jit(solution)/shard_map/ppermute | solution.py:452
  114.4 0.8 copy-start.5
  125.0 20.9 %collective-permute-start.9 = (bf16[8,64,512]{2,1,0:T(8,128)(2,1)}, bf16[8,64,512]{2,1,0:T(8,128)(2,1)S(1)}, u32[]{:S(2)}, u32[]{:S(2)}) collective-permute-start(bf16[8,64,512]{2,1,0:T(8,128)(2,1)} %get-tuple-element.29), channel_id=1, source_target_pairs={{0,1},{1,0},{2,3},{3,2},{4,5},{5,4},{6,7},{7,6},{8,9},{9,8},{10,11... | collective-permute-start | bytes 1572872 | tf_op jit(solution)/shard_map/ppermute | solution.py:452
  143.2 2.6 %collective-permute-start.10 = (f32[64,128]{1,0:T(8,128)S(1)}, f32[64,128]{1,0:T(8,128)S(1)}, u32[]{:S(2)}, u32[]{:S(2)}) collective-permute-start(f32[64,128]{1,0:T(8,128)S(1)} %bitcast.13), channel_id=1, source_target_pairs={{0,1},{1,0},{2,3},{3,2},{4,5},{5,4},{6,7},{7,6},{8,9},{9,8},{10,11... | collective-permute-start | bytes 98312 | tf_op jit(solution)/shard_map/ppermute | solution.py:452
  145.0 0.9 copy-start.7
  145.9 0.8 copy-start.8
  207.6 5.0 %collective-permute-start.11 = (bf16[32,8,8,128]{3,2,1,0:T(8,128)(2,1)S(1)}, bf16[32,8,8,128]{3,2,1,0:T(8,128)(2,1)S(1)}, u32[]{:S(2)}, u32[]{:S(2)}) collective-permute-start(bf16[32,8,8,128]{3,2,1,0:T(8,128)(2,1)S(1)} %slice_select_fusion), channel_id=1, source_target_pairs={{0,1},{1,0},{2,3},{3,2},{4,5},{5,4},{6,7},{7,6},{8,9},{9,8},{10,11... | collective-permute-start | bytes 1572872 | tf_op jit(solution)/shard_map/ppermute | solution.py:452
  (1 other events, 0.7 us)

commit v2 on v1

v2 whole, which is shorter than its diff:
```python
import functools

import jax
import jax.numpy as jnp
from jax import lax
from jax.experimental import pallas as pl
from jax.experimental.pallas import tpu as pltpu
from jax.sharding import Mesh
from jax.sharding import PartitionSpec as P

STEP = 8
GX = ("gx_0", "gx_1")
GRP_GX = ("grp", "gx_0", "gx_1")
LANES = 128
SWAP = [(0, 1), (1, 0)]
HBM, VMEM = pltpu.HBM, pltpu.VMEM

epsilon = 1e-05


def chain(count, step):
    pairs = [(i, i + 1) for i in range(count - 1)]
    return pairs if step > 0 else [(b, a) for a, b in pairs]


def call(kernel, outs, scratch, n_copies, flops, operands):
    spaces = [space for space, _ in operands]
    held = [pltpu.with_memory_space_constraint(x, space) for space, x in operands]
    return pl.pallas_call(
        kernel,
        out_shape=[space(shape, dtype) for space, shape, dtype in outs],
        in_specs=[pl.BlockSpec(memory_space=space) for space in spaces],
        out_specs=[pl.BlockSpec(memory_space=space) for space, _, _ in outs],
        scratch_shapes=[*scratch, pltpu.SemaphoreType.DMA((n_copies,))],
        cost_estimate=pl.CostEstimate(flops=flops, bytes_accessed=1 << 20, transcendentals=0),
        compiler_params=pltpu.CompilerParams(vmem_limit_bytes=24 << 20),
    )(*held)


def start_all(sem, first, pairs):
    copies = [
        pltpu.make_async_copy(src, dst, sem.at[first + i]) for i, (src, dst) in enumerate(pairs)
    ]
    for copy in copies:
        copy.start()
    return copies


def wait_all(copies):
    for copy in copies:
        copy.wait()


def elu(v):
    return jnp.where(v > 0, v, jnp.exp(jnp.minimum(v, 0.0)) - 1.0)


def as_float(flag):
    return jnp.asarray(flag, jnp.int32).astype(jnp.float32)


def lane_half(rows):
    return lax.broadcasted_iota(jnp.int32, (rows, LANES), 1) < LANES // 2


def halves(first, second):
    return jnp.where(lane_half(first.shape[0]), first, pltpu.roll(second, LANES // 2, 1))


def reach_mask(core):
    row = lax.broadcasted_iota(jnp.int32, (2 * STEP, LANES), 0)
    first = STEP * core
    return (row >= first) & (row < first + STEP)


def inside_of(row_at, devices):
    above = as_float(jnp.minimum(row_at, 1))
    below = as_float(jnp.minimum(devices - 1 - row_at, 1))
    return jnp.where(lane_half(1), above, below)


def flat_of(channels, rows, cols):
    return pltpu.VMEM((cols // LANES, channels * rows, LANES), jnp.float32)


def widen(source_ref, flat_ref):
    channels, rows, cols = source_ref.shape
    some = 64 // rows

    def step(i, _):
        for block in range(cols // LANES):
            value = source_ref[pl.ds(i * some, some), :, block * LANES : (block + 1) * LANES]
            flat_ref[block, pl.ds(pl.multiple_of(i * some * rows, 8), some * rows), :] = (
                value.astype(jnp.float32).reshape(some * rows, LANES)
            )
        return 0

    lax.fori_loop(0, channels // some, step, 0)


def term_group(terms_ref, start):
    return terms_ref[pl.ds(pl.multiple_of(start, 2 * STEP), 2 * STEP), :].astype(jnp.float32)


def column_terms(terms_ref, core, cols, out_ref):
    def twice(rows):
        return jnp.where(lane_half(rows.shape[0]), pltpu.roll(rows, LANES // 2, 1), rows)

    for first in range(0, cols, LANES):
        at = pl.multiple_of(core * cols + first, LANES)
        out_ref[first : first + LANES] = twice(terms_ref[pl.ds(at, LANES), :].astype(jnp.float32))
    out_ref[cols:] = twice(term_group(terms_ref, cols - 2 * STEP * core))


def fill_rows(x_ref, sources, side_sources, row_terms, col_terms, scale, core, mask):
    cols = col_terms.shape[0] - 2 * STEP
    channels = LANES // 2

    def pair(sources, block, i):
        return jnp.transpose(
            jnp.concatenate(
                [
                    flat[block, pl.ds(first + i, channels, stride=rows), :]
                    for flat, first, rows in sources
                ],
                axis=0,
            )
        )

    def step(i, _):
        row = row_terms[pl.ds(i, 1), :]
        for block in range(cols // LANES):
            at = slice(block * LANES, (block + 1) * LANES)
            value = pair(sources, block, i) + (row + col_terms[at, :])
            if scale is not None:
                value = value * scale
            x_ref[i, at, :] = value.astype(jnp.bfloat16)
        side = pair(side_sources, 0, i)
        value = jnp.where(core == 0, side[: 2 * STEP], side[LANES - 2 * STEP :])
        value = value + (row + col_terms[cols:, :])
        if scale is not None:
            value = value * scale
        x_ref[i, cols:, :] = jnp.where(mask, value, 0.0).astype(jnp.bfloat16)
        return 0

    lax.fori_loop(0, STEP, step, 0)


def weights_of(taps_ref, wanted):
    channels = taps_ref.shape[1]
    zero = jnp.zeros((channels, channels), jnp.bfloat16)
    return jnp.concatenate(
        [
            jnp.concatenate(
                [zero if ky is None else taps_ref[3 * ky + kx] for ky in inputs], axis=1
            )
            for kx in range(3)
            for inputs in wanted
        ],
        axis=0,
    )


OWN_TAPS = ((1, 2, 0, None), (0, 1, None, 2))
NEAR_TAPS = ((2, None, 1, None), (None, 0, None, 1))
FAR_TAPS = ((0, None), (None, 2))


def product(values, weights):
    return lax.dot_general(
        values, weights, (((1,), (1,)), ((), ())), preferred_element_type=jnp.float32
    )


def shifted_sum(p_ref, first):
    last = p_ref.shape[0]
    if first == 0:
        left = jnp.concatenate([p_ref[last - STEP :, :LANES], p_ref[: LANES - STEP, :LANES]], axis=0)
    else:
        left = p_ref[first - STEP : first - STEP + LANES, :LANES]
    centre = p_ref[first : first + LANES, LANES : 2 * LANES]
    right = p_ref[first + STEP : first + STEP + LANES, 2 * LANES :]
    return left + centre + right


def conv_own_rows(own_ref, near_ref, weights, p_ref, out_ref):
    cols = out_ref.shape[1]
    total = jnp.zeros((STEP, LANES), jnp.float32)
    squares = total
    for i in range(STEP):
        p = p_ref.at[i % 2]
        p[...] = product(jnp.concatenate([own_ref[i], near_ref[i]], axis=1), weights)
        for first in range(0, cols, LANES):
            value = shifted_sum(p, first)
            out_ref[i, first : first + LANES, :] = value.astype(jnp.bfloat16)
            value = value.reshape(LANES // STEP, STEP, LANES)
            total = total + jnp.sum(value, axis=0)
            squares = squares + jnp.sum(value * value, axis=0)
    total = total + pltpu.roll(total, LANES // 2, 1)
    squares = squares + pltpu.roll(squares, LANES // 2, 1)
    return jnp.sum(jnp.where(lane_half(STEP), total, squares), axis=0, keepdims=True)


def affine_of(which, stats_refs, gains_ref, cells):
    row = sum(jnp.sum(ref[...], axis=0, keepdims=True) for ref in stats_refs) / cells
    row = jnp.broadcast_to(row, (STEP, LANES))
    other = pltpu.roll(row, LANES // 2, 1)
    average = jnp.where(lane_half(STEP), row, other)
    spread = jnp.where(lane_half(STEP), other, row) - average * average
    factor = gains_ref[which : which + 1] * lax.rsqrt(spread + epsilon)
    offset = gains_ref[2 + which : 3 + which] - average * factor
    return factor[0:1], offset[0:1]


def prepare_kernel(
    pair, feats, w_row, w_col, top_out, bottom_out, terms_ref, top, bottom, feats_in, row_in,
    col_in, sem,
):
    parts = start_all(sem, 0, ((pair.at[:, :STEP], top), (pair.at[:, STEP:], bottom)))
    inputs = start_all(sem, 2, ((feats, feats_in), (w_row, row_in), (w_col, col_in)))
    wait_all(inputs)
    terms = jnp.concatenate(
        [product(feats_in[...], w[...]) for w in (row_in, col_in)], axis=1
    ).astype(jnp.bfloat16)
    terms_ref[...] = jnp.broadcast_to(terms[None], terms_ref.shape)
    wait_all(parts)
    wait_all(start_all(sem, 0, ((top, top_out), (bottom, bottom_out))))


def first_kernel(
    devices, own_in, above_in, below_in, side_in, terms_in, taps_in,
    own_out, near_out, conv_out, give_out, stats_ref,
    x_own, x_near, conv_ref, p_ref, own, above, below, side, terms, taps,
    own_flat, above_flat, below_flat, side_flat, col_terms, row_terms, sem,
):
    row_at, core = lax.axis_index(GX), lax.axis_index("gy")
    _, rows, cols = own.shape
    half = STEP // 2
    inputs = start_all(
        sem, 0,
        ((terms_in, terms), (side_in, side), (own_in, own), (above_in, above), (below_in, below),
         (taps_in, taps)),
    )
    inputs[0].wait()
    column_terms(terms, core, cols, col_terms)
    mine = term_group(terms, row_at * rows)
    up = term_group(terms, jnp.maximum(row_at - 1, 0) * rows)
    down = term_group(terms, jnp.minimum(row_at + 1, devices - 1) * rows)
    row_terms[0] = halves(mine[:STEP], mine[STEP:])
    row_terms[1] = halves(up[STEP:], down[:STEP])
    mask = reach_mask(core)
    tall = rows + 2 * STEP
    inputs[1].wait()
    widen(side, side_flat)
    inputs[2].wait()
    widen(own, own_flat)
    fill_rows(
        x_own, ((own_flat, 0, rows), (own_flat, STEP, rows)),
        ((side_flat, STEP, tall), (side_flat, 2 * STEP, tall)),
        row_terms.at[0], col_terms, None, core, mask,
    )
    given = x_own.at[pl.ds(half * (1 - core), half), pl.ds(0, cols)]
    outputs = start_all(sem, 6, ((x_own, own_out), (given, give_out)))
    wait_all(inputs[3:5])
    widen(above, above_flat)
    widen(below, below_flat)
    fill_rows(
        x_near, ((above_flat, 0, STEP), (below_flat, 0, STEP)),
        ((side_flat, 0, tall), (side_flat, STEP + rows, tall)),
        row_terms.at[1], col_terms, inside_of(row_at, devices), core, mask,
    )
    outputs += start_all(sem, 8, ((x_near, near_out),))
    inputs[5].wait()
    stats = conv_own_rows(x_own, x_near, weights_of(taps, OWN_TAPS), p_ref, conv_ref)
    outputs += start_all(sem, 9, ((conv_ref, conv_out),))
    stats_ref[...] = jnp.broadcast_to(stats, stats_ref.shape)
    wait_all(outputs)


def far_kernel(
    devices, own_in, near_in, conv_in, above_in, below_in, side_in, terms_in, taps_in,
    conv_out, edge_out,
    x_own, x_near, x_far, conv_ref, edge_ref, p_ref, above, below, side, terms, taps,
    above_flat, below_flat, side_flat, col_terms, row_terms, sem,
):
    row_at, core = lax.axis_index(GX), lax.axis_index("gy")
    _, _, cols = above.shape
    rows = 2 * STEP
    edge_at = pl.multiple_of((cols - 2 * STEP) * (1 - core), 2 * STEP)
    inputs = start_all(
        sem, 0,
        ((terms_in, terms), (side_in, side), (above_in, above), (below_in, below),
         (own_in, x_own), (near_in, x_near),
         (conv_in.at[:, pl.ds(edge_at, 2 * STEP)], edge_ref.at[0]), (taps_in, taps)),
    )
    inputs[0].wait()
    column_terms(terms, core, cols, col_terms)
    up = term_group(terms, jnp.maximum(row_at - 1, 0) * rows)
    down = term_group(terms, jnp.minimum(row_at + 1, devices - 1) * rows)
    row_terms[...] = halves(up[:STEP], down[STEP:])
    wait_all(inputs[1:4])
    widen(side, side_flat)
    widen(above, above_flat)
    widen(below, below_flat)
    fill_rows(
        x_far, ((above_flat, 0, STEP), (below_flat, 0, STEP)),
        ((side_flat, 0, 2 * STEP), (side_flat, STEP, 2 * STEP)),
        row_terms, col_terms, inside_of(row_at, devices), core, reach_mask(core),
    )
    wait_all(inputs[4:])
    near_weights, far_weights = weights_of(taps, NEAR_TAPS), weights_of(taps, FAR_TAPS)
    for i in range(STEP):
        p = p_ref.at[i % 2]
        near = jnp.concatenate([x_own[i], x_near[i]], axis=1)
        p[...] = product(near, near_weights) + product(x_far[i], far_weights)
        for first in range(0, cols, LANES):
            conv_ref[i, first : first + LANES, :] = shifted_sum(p, first).astype(jnp.bfloat16)
    edge_ref[1] = conv_ref[:, pl.ds(edge_at, 2 * STEP), :]
    wait_all(start_all(sem, 0, ((edge_ref, edge_out), (conv_ref, conv_out))))


def second_kernel(
    devices, cells, own_in, far_in, side, stats, stats_other, gains, taps_in,
    conv_out, give_out, stats_ref,
    a_own, a_near, conv_ref, p_ref, own, far, taps, sem,
):
    row_at, core = lax.axis_index(GX), lax.axis_index("gy")
    cols = own.shape[1]
    half = STEP // 2
    inputs = start_all(sem, 0, ((far_in, far), (own_in, own), (taps_in, taps)))
    factor, offset = affine_of(0, (stats, stats_other), gains, cells)
    inside = inside_of(row_at, devices)
    mask = reach_mask(core)

    def activated(value, scale):
        value = elu(value.astype(jnp.float32) * factor + offset)
        return value if scale is None else value * scale

    def fill(to_ref, source, which, scale):
        def step(i, _):
            for first in range(0, cols, LANES):
                at = slice(first, first + LANES)
                to_ref[i, at, :] = activated(source[i, at, :], scale).astype(jnp.bfloat16)
            beyond = jnp.where(mask, activated(side[which, i], scale), 0.0)
            to_ref[i, cols:, :] = beyond.astype(jnp.bfloat16)
            return 0

        lax.fori_loop(0, STEP, step, 0)

    inputs[0].wait()
    fill(a_near, far, 1, inside)
    wait_all(inputs[1:])
    fill(a_own, own, 0, None)
    stats = conv_own_rows(a_own, a_near, weights_of(taps, OWN_TAPS), p_ref, conv_ref)
    given = conv_ref.at[pl.ds(half * (1 - core), half)]
    outputs = start_all(sem, 0, ((given, give_out), (conv_ref, conv_out)))
    stats_ref[...] = jnp.broadcast_to(stats, stats_ref.shape)
    wait_all(outputs)


def pack_kernel(
    cells, block_in, block_in_other, conv_in, conv_other_in, stats, stats_other, gains,
    block_out_out, send_ref,
    out_ref, own, other, conv, conv_other, sem,
):
    core = lax.axis_index("gy")
    cols = conv.shape[1]
    half = STEP // 2
    inputs = start_all(
        sem, 0,
        ((block_in.at[:, pl.ds(0, cols)], own), (conv_in, conv), (block_in_other, other),
         (conv_other_in, conv_other)),
    )
    factor, offset = affine_of(1, (stats, stats_other), gains, cells)
    wide = 2 * STEP
    peers, some = cols // wide, LANES // wide

    def block_out(x, value):
        value = x.astype(jnp.float32) + value.astype(jnp.float32) * factor + offset
        return elu(value).astype(jnp.bfloat16)

    def mine(i, _):
        for first in range(0, cols, LANES):
            at = slice(first, first + LANES)
            out_ref[i, at, :] = block_out(own[i, at, :], conv[i, at, :])
        return 0

    wait_all(inputs[:2])
    lax.fori_loop(0, STEP, mine, 0)
    outputs = start_all(sem, 4, ((out_ref, block_out_out),))

    def step(i, _):
        for first in range(0, cols, LANES):
            at = slice(first, first + LANES)
            value = out_ref[half * core + i, at, :].reshape(some, wide, LANES)
            send_ref[pl.ds(peers * core + first // wide, some), i] = value
            value = block_out(other[i, at, :], conv_other[i, at, :]).reshape(some, wide, LANES)
            send_ref[pl.ds(peers * (1 - core) + first // wide, some), i] = value
        return 0

    wait_all(inputs[2:])
    lax.fori_loop(0, half, step, 0)
    wait_all(outputs)


def merge_kernel(own_in, received, other, result, out_ref, own, cells_ref, flat_ref, sem):
    core = lax.axis_index("gy")
    channels, rows, cols = out_ref.shape
    peers = other.shape[0]
    inputs = start_all(sem, 0, ((own_in, own),))

    def gather(s, _):
        cells_ref[s, core] = received[peers * core + s].astype(jnp.float32)
        cells_ref[s, 1 - core] = other[s].astype(jnp.float32)
        return 0

    lax.fori_loop(0, peers, gather, 0)
    wait_all(inputs)
    flat = cells_ref.reshape(peers * STEP * rows, LANES)
    some = LANES // rows
    lower = lane_half(some * STEP)

    def step(i, _):
        for block in range(cols // LANES):
            first = block * some * STEP * rows
            upper_row = flat[pl.ds(first + i, some * STEP, stride=rows), :]
            lower_row = flat[pl.ds(first + STEP + i, some * STEP, stride=rows), :]
            even = jnp.where(lower, upper_row, pltpu.roll(lower_row, channels, 1))
            odd = jnp.where(lower, pltpu.roll(upper_row, channels, 1), lower_row)
            mirrored = jnp.concatenate(
                [
                    part[s * STEP : (s + 1) * STEP]
                    for s in range(some)
                    for part in (even, odd)
                ],
                axis=0,
            )
            value = own[i, block * LANES : (block + 1) * LANES, :].astype(jnp.float32) + mirrored
            value = jnp.transpose(0.5 * value)
            for high in range(rows // STEP):
                flat_ref[block, pl.ds(high * STEP + i, channels, stride=rows), :] = value[
                    channels * high : channels * (high + 1)
                ]
        return 0

    lax.fori_loop(0, STEP, step, 0)

    def store(c, _):
        for block in range(cols // LANES):
            value = flat_ref[block, pl.ds(pl.multiple_of(c * rows, 8), rows), :]
            out_ref[c, :, block * LANES : (block + 1) * LANES] = value.astype(jnp.bfloat16)
        return 0

    part = channels // 2
    lax.fori_loop(0, part, store, 0)
    outputs = start_all(sem, 1, ((out_ref.at[pl.ds(0, part)], result.at[pl.ds(0, part)]),))
    lax.fori_loop(part, channels, store, 0)
    outputs += start_all(sem, 2, ((out_ref.at[pl.ds(part, part)], result.at[pl.ds(part, part)]),))
    wait_all(outputs)


def body(residue_feats, pair_feats, w_row, w_col, first_taps, second_taps, norm_scale, norm_shift):
    channels, rows, cols = pair_feats.shape
    cores = lax.axis_size("gy")
    devices = lax.axis_size(GX)
    first_core = lax.axis_index("gy") == 0
    cells = devices * rows * cores * cols
    bf16, f32 = jnp.bfloat16, jnp.float32
    conv_flops = 2 * 9 * channels * channels * rows * cols

    def edge(x):
        return jnp.where(first_core, x[..., cols - LANES :], x[..., :LANES])

    def swap(x):
        return lax.ppermute(x, "gy", SWAP)

    down = functools.partial(lax.ppermute, axis_name=GX, perm=chain(devices, 1))
    up = functools.partial(lax.ppermute, axis_name=GX, perm=chain(devices, -1))
    eight = (channels, STEP, cols)
    top, bottom, terms = call(
        prepare_kernel,
        (
            (HBM, eight, bf16),
            (HBM, eight, bf16),
            (VMEM, (devices, rows, 2 * channels), bf16),
        ),
        [
            VMEM(eight, bf16),
            VMEM(eight, bf16),
            VMEM(residue_feats.shape, bf16),
            VMEM(w_row.T.shape, bf16),
            VMEM(w_col.T.shape, bf16),
        ],
        5,
        conv_flops // 16,
        ((HBM, pair_feats), (HBM, residue_feats), (HBM, w_row.T), (HBM, w_col.T)),
    )
    above_near, below_near = down(bottom), up(top)
    above_far, below_far = down(top), up(bottom)
    terms = lax.all_to_all(terms, GX, 0, 0, tiled=True)
    terms = terms.reshape(devices * rows, 2 * channels)
    gains = jnp.tile(jnp.concatenate([norm_scale, norm_shift], axis=0), (1, 2))

    near_side = swap(
        jnp.concatenate([edge(above_near), edge(pair_feats), edge(below_near)], axis=1)
    )
    far_side = swap(jnp.concatenate([edge(above_far), edge(below_far)], axis=1))

    taps_shape = VMEM(first_taps.shape, bf16)
    terms_shape = VMEM(terms.shape, bf16)
    whole = (STEP, cols, LANES)
    part = (STEP // 2, cols, LANES)
    wide = (STEP, cols + 2 * STEP, LANES)
    products = VMEM((2, cols + 2 * STEP, 3 * LANES), f32)
    sums = (devices, LANES)
    own_rows, near_rows, conv_own, own_give, stats = call(
        functools.partial(first_kernel, devices),
        (
            (HBM, wide, bf16),
            (HBM, wide, bf16),
            (HBM, whole, bf16),
            (HBM, part, bf16),
            (VMEM, sums, f32),
        ),
        [
            VMEM(wide, bf16),
            VMEM(wide, bf16),
            VMEM(whole, bf16),
            products,
            VMEM(pair_feats.shape, bf16),
            VMEM(eight, bf16),
            VMEM(eight, bf16),
            VMEM(near_side.shape, bf16),
            terms_shape,
            taps_shape,
            flat_of(channels, rows, cols),
            flat_of(channels, STEP, cols),
            flat_of(channels, STEP, cols),
            flat_of(channels, rows + 2 * STEP, LANES),
            VMEM(wide[1:], f32),
            VMEM((2, STEP, LANES), f32),
        ],
        10,
        conv_flops,
        ((HBM, pair_feats), (HBM, above_near), (HBM, below_near), (HBM, near_side),
         (HBM, terms), (HBM, first_taps)),
    )
    stats = lax.all_to_all(stats, GX, 0, 0, tiled=True)
    stats_other = swap(stats)
    conv_far, edges = call(
        functools.partial(far_kernel, devices),
        ((HBM, whole, bf16), (HBM, (2, STEP, 2 * STEP, LANES), bf16)),
        [
            VMEM(wide, bf16),
            VMEM(wide, bf16),
            VMEM(wide, bf16),
            VMEM(whole, bf16),
            VMEM((2, STEP, 2 * STEP, LANES), bf16),
            products,
            VMEM(eight, bf16),
            VMEM(eight, bf16),
            VMEM(far_side.shape, bf16),
            terms_shape,
            taps_shape,
            flat_of(channels, STEP, cols),
            flat_of(channels, STEP, cols),
            flat_of(channels, 2 * STEP, LANES),
            VMEM(wide[1:], f32),
            VMEM((STEP, LANES), f32),
        ],
        8,
        conv_flops,
        ((HBM, own_rows), (HBM, near_rows), (HBM, conv_own), (HBM, above_far),
         (HBM, below_far), (HBM, far_side), (HBM, terms), (HBM, first_taps)),
    )
    edges = swap(edges)
    own_other = swap(own_give)
    conv_second, second_give, stats = call(
        functools.partial(second_kernel, devices, cells),
        ((HBM, whole, bf16), (HBM, part, bf16), (VMEM, sums, f32)),
        [
            VMEM(wide, bf16),
            VMEM(wide, bf16),
            VMEM(whole, bf16),
            products,
            VMEM(whole, bf16),
            VMEM(whole, bf16),
            taps_shape,
        ],
        3,
        conv_flops,
        ((HBM, conv_own), (HBM, conv_far), (VMEM, edges), (VMEM, stats), (VMEM, stats_other),
         (VMEM, gains), (HBM, second_taps)),
    )
    stats = lax.all_to_all(stats, GX, 0, 0, tiled=True)
    stats_other = swap(stats)
    conv_other = swap(second_give)
    block_out, send = call(
        functools.partial(pack_kernel, cells),
        ((HBM, whole, bf16), (VMEM, (devices, STEP // 2, rows, LANES), bf16)),
        [
            VMEM(whole, bf16),
            VMEM(whole, bf16),
            VMEM(part, bf16),
            VMEM(whole, bf16),
            VMEM(part, bf16),
        ],
        5,
        conv_flops,
        ((HBM, own_rows), (HBM, own_other), (HBM, conv_second), (HBM, conv_other),
         (VMEM, stats), (VMEM, stats_other), (VMEM, gains)),
    )
    received = lax.all_to_all(send, GX, 0, 0, tiled=True)
    peers = devices // cores
    other = swap(jnp.where(first_core, received[peers:], received[:peers]))
    return call(
        merge_kernel,
        ((HBM, pair_feats.shape, bf16),),
        [
            VMEM(pair_feats.shape, bf16),
            VMEM(whole, bf16),
            VMEM((peers, cores, STEP // 2, rows, LANES), f32),
            flat_of(channels, rows, cols),
        ],
        3,
        conv_flops,
        ((HBM, block_out), (VMEM, received), (VMEM, other)),
    )[0]


def solution(mesh):
    torus = Mesh(
        mesh.devices.reshape(mesh.shape["grp"], 4, 16, mesh.shape["gy"]),
        ("grp", "gx_0", "gx_1", "gy"),
    )
    placed = (P(GRP_GX, None), P(None, GRP_GX, "gy"), P(), P(), P(), P(), P(), P())
    return jax.shard_map(
        body, mesh=torus, in_specs=placed, out_specs=P(None, GRP_GX, "gy"), check_vma=False
    )
```

time: 217 us -> 207 us (0.954)
  blocking collectives: 99.8 us -> 77.8 us
  starting transfers between devices: 56 us -> 70.4 us
  Pallas kernels: 38.7 us -> 31.5 us
  waiting for transfers between devices: 16.7 us -> 23.5 us
    all_to_all x2 -> x1, blocking collectives: 44.4 us -> 22.4 us  [body(): stats = lax.all_to_all(stats, GX, 0, 0, tiled=True)]
    all_to_all x0 -> x1, starting transfers between devices: none -> 11.2 us  [body(): stats = lax.all_to_all(stats, GX, 0, 0, tiled=True)]
    pallas_call x6, Pallas kernels: 38.7 us -> 31.5 us  [call(): pl.pallas_call(kernel, out_shape=[space(shape, dtype) for space, shape, d...]
    all_to_all x1, waiting for transfers between devices: 13.6 us -> 18.5 us  [body(): terms = lax.all_to_all(terms, GX, 0, 0, tiled=True)]
  transfers between devices with their start and end apart: 13 -> 14, of which waited for: 4 -> 5; matrix products, arithmetic and copies ran while one was open for 1% -> 0% of each run, Pallas kernels for 9% -> 10%
where the time goes in v2:
time: 207 us; the launch traced here: 206 us
  blocking collectives  77.8 us (38%)
  starting transfers between devices  70.4 us (34%)
  Pallas kernels  31.5 us (15%)
  waiting for transfers between devices  23.5 us (11%)
  local copies, waits for them, and re-layouts  2.46 us (1%)
    all_to_all x1, blocking collectives, body(): received = lax.all_to_all(send, GX, 0, 0, tiled=True)  55.4 us
    pallas_call x6, Pallas kernels, call(): pl.pallas_call(kernel, out_shape=[space(shape, dtype) for space, shape, d...  31.5 us
    all_to_all x1, starting transfers between devices, body(): terms = lax.all_to_all(terms, GX, 0, 0, tiled=True)  30.9 us
    all_to_all x1, blocking collectives, body(): stats = lax.all_to_all(stats, GX, 0, 0, tiled=True)  22.4 us
    all_to_all x1, waiting for transfers between devices, body(): terms = lax.all_to_all(terms, GX, 0, 0, tiled=True)  18.5 us
    ppermute x8, starting transfers between devices, swap(): return lax.ppermute(x, 'gy', SWAP)  14.6 us
    all_to_all x1, starting transfers between devices, body(): stats = lax.all_to_all(stats, GX, 0, 0, tiled=True)  11.2 us
    ppermute x2, starting transfers between devices, body(): above_near, below_near = (down(bottom), up(top))  7.23 us
  transfers between devices with their start and end apart: 14, of which 5 were waited for; matrix products, arithmetic and copies ran while one was open for 0% of the time, Pallas kernels for 10%

profile of v2, /device:TPU:33, one launch (start us, length us, event | category | flops | bytes accessed | tf_op | source)
XLA Modules:
  0.0 206.4 jit_solution(9919604219314103212)
XLA Ops:
  0.0 3.1 %shard_map.82 = (bf16[64,8,512]{2,1,0:T(8,128)(2,1)}, bf16[64,8,512]{2,1,0:T(8,128)(2,1)}, bf16[64,16,128]{2,1,0:T(8,128)(2,1)}) custom-call(bf16[64,16,512]{2,1,0:T(8,128)(2,1)} %own_in.1, bf16[16,256]{1,0:T(8,128)(2,1)} %feats.1, bf16[64,256]{1,0:T(8,128)(2,1)} %bitcast.18, bf16[64,256]{1,0:T(8,128)(2,1)} %bitcast.19), custom_call_target="tpu_custom_call" | custom-call | flops 37748736 | bytes 1048576 | tf_op jit(solution)/shard_map/pallas_call | solution.py:29
  3.1 1.3 collective-permute-start.1
  4.4 5.9 %collective-permute-start = (bf16[64,8,512]{2,1,0:T(8,128)(2,1)}, bf16[64,8,512]{2,1,0:T(8,128)(2,1)S(1)}, u32[]{:S(2)}, u32[]{:S(2)}) collective-permute-start(bf16[64,8,512]{2,1,0:T(8,128)(2,1)} %get-tuple-element.20), channel_id=1, source_target_pairs={{0,2},{2,4},{4,6},{6,8},{8,10},{10,12},{12,14},{14,16},{16,18},{18... | collective-permute-start | bytes 1572872 | tf_op jit(solution)/shard_map/ppermute | solution.py:498
  10.4 1.3 collective-permute-start.5
  11.7 5.1 %collective-permute-start.4 = (bf16[64,8,512]{2,1,0:T(8,128)(2,1)}, bf16[64,8,512]{2,1,0:T(8,128)(2,1)S(1)}, u32[]{:S(2)}, u32[]{:S(2)}) collective-permute-start(bf16[64,8,512]{2,1,0:T(8,128)(2,1)} %get-tuple-element.21), channel_id=1, source_target_pairs={{0,2},{2,4},{4,6},{6,8},{8,10},{10,12},{12,14},{14,16},{16,18},{18... | collective-permute-start | bytes 1572872 | tf_op jit(solution)/shard_map/ppermute | solution.py:499
  16.8 30.9 %all-to-all-start = ((bf16[64,16,128]{2,1,0:T(8,128)(2,1)}), bf16[64,16,128]{2,1,0:T(8,128)(2,1)S(1)}, u32[]{:S(2)}, u32[]{:S(2)}) async-start(bf16[64,16,128]{2,1,0:T(8,128)(2,1)} %get-tuple-element.22), calls=%async_computation | async-start | bytes 524288 | tf_op jit(solution)/shard_map/all_to_all | solution.py:500
  47.9 2.1 %collective-permute-start.2 = (bf16[64,32,128]{2,1,0:T(8,128)(2,1)S(1)}, bf16[64,32,128]{2,1,0:T(8,128)(2,1)}, u32[]{:S(2)}, u32[]{:S(2)}) collective-permute-start(bf16[64,32,128]{2,1,0:T(8,128)(2,1)S(1)} %pad_maximum_fusion), channel_id=1, source_target_pairs={{0,1},{1,0},{2,3},{3,2},{4,5},{5,4},{6,7},{7,6},{8,9},{9,8},{10,11... | collective-permute-start | bytes 1572872 | tf_op jit(solution)/shard_map/ppermute | solution.py:475
  50.9 18.5 %all-to-all-done = bf16[64,16,128]{2,1,0:T(8,128)(2,1)S(1)} async-done(((bf16[64,16,128]{2,1,0:T(8,128)(2,1)}), bf16[64,16,128]{2,1,0:T(8,128)(2,1)S(1)}, u32[]{:S(2)}, u32[]{:S(2)}) %all-to-all-start) | async-done | bytes 262176 | tf_op jit(solution)/shard_map/all_to_all | solution.py:500
  70.1 8.3 %shard_map.83 = (bf16[8,528,128]{2,1,0:T(8,128)(2,1)}, bf16[8,528,128]{2,1,0:T(8,128)(2,1)}, bf16[8,512,128]{2,1,0:T(8,128)(2,1)}, bf16[4,512,128]{2,1,0:T(8,128)(2,1)}, f32[64,128]{1,0:T(8,128)}) custom-call(bf16[64,16,512]{2,1,0:T(8,128)(2,1)} %own_in.1, bf16[64,8,512]{2,1,0:T(8,128)(2,1)} %copy-done.5, bf16[64,8,512]{2,1,0:T(8,128)(2,1)} %copy-done.4, ...), custom_call_target="tpu_custom_call" | custom-call | flops 603979776 | bytes 1048576 | tf_op jit(solution)/shard_map/pallas_call | solution.py:29
  78.4 11.2 %all-to-all-start.1 = ((f32[64,1,128]{2,1,0:T(1,128)}), f32[64,1,128]{2,1,0:T(1,128)S(1)}, u32[]{:S(2)}, u32[]{:S(2)}) async-start(f32[64,1,128]{2,1,0:T(1,128)} %bitcast.4), calls=%async_computation.1 | async-start | bytes 65536 | tf_op jit(solution)/shard_map/all_to_all | solution.py:548
  90.3 6.7 %shard_map.84 = (bf16[8,512,128]{2,1,0:T(8,128)(2,1)}, bf16[2,8,16,128]{3,2,1,0:T(8,128)(2,1)}) custom-call(bf16[8,528,128]{2,1,0:T(8,128)(2,1)} %get-tuple-element.23.own_in.block_in, bf16[8,528,128]{2,1,0:T(8,128)(2,1)} %get-tuple-element.26.near_in, bf16[8,512,128]{2,1,0:T(8,128)(2,1)} %get-tuple-element.25.conv_in.own_in, bf16[64,8,512]{2,1,0:T(8,128)(2,1)} %copy-done.3, ...), custom_call_target="tpu_custom_call" | custom-call | flops 603979776 | bytes 1048576 | tf_op jit(solution)/shard_map/pallas_call | solution.py:29
  97.1 2.4 %collective-permute-start.7 = (bf16[2,8,16,128]{3,2,1,0:T(8,128)(2,1)}, bf16[2,8,16,128]{3,2,1,0:T(8,128)(2,1)S(1)}, u32[]{:S(2)}, u32[]{:S(2)}) collective-permute-start(bf16[2,8,16,128]{3,2,1,0:T(8,128)(2,1)} %get-tuple-element.28), channel_id=1, source_target_pairs={{0,1},{1,0},{2,3},{3,2},{4,5},{5,4},{6,7},{7,6},{8,9},{9,8},{10,11... | collective-permute-start | bytes 196616 | tf_op jit(solution)/shard_map/ppermute | solution.py:475
  99.4 2.1 %all-to-all-done.1 = f32[64,1,128]{2,1,0:T(1,128)S(1)} async-done(((f32[64,1,128]{2,1,0:T(1,128)}), f32[64,1,128]{2,1,0:T(1,128)S(1)}, u32[]{:S(2)}, u32[]{:S(2)}) %all-to-all-start.1) | async-done | bytes 32800 | tf_op jit(solution)/shard_map/all_to_all | solution.py:548
  101.5 3.4 %collective-permute-start.8 = (f32[64,128]{1,0:T(8,128)S(1)}, f32[64,128]{1,0:T(8,128)S(1)}, u32[]{:S(2)}, u32[]{:S(2)}) collective-permute-start(f32[64,128]{1,0:T(8,128)S(1)} %bitcast.11), channel_id=1, source_target_pairs={{0,1},{1,0},{2,3},{3,2},{4,5},{5,4},{6,7},{7,6},{8,9},{9,8},{10,11... | collective-permute-start | bytes 98312 | tf_op jit(solution)/shard_map/ppermute | solution.py:475
  105.8 5.3 %shard_map.85 = (bf16[8,512,128]{2,1,0:T(8,128)(2,1)}, bf16[4,512,128]{2,1,0:T(8,128)(2,1)}, f32[64,128]{1,0:T(8,128)S(1)}) custom-call(bf16[8,512,128]{2,1,0:T(8,128)(2,1)} %get-tuple-element.25.conv_in.own_in, bf16[8,512,128]{2,1,0:T(8,128)(2,1)} %get-tuple-element.27.far_in, bf16[2,8,16,128]{3,2,1,0:T(8,128)(2,1)S(1)} %collective-permute-done.7.side, ...), custom_call_target="tpu_custom_call" | custom-call | flops 603979776 | bytes 1048576 | tf_op jit(solution)/shard_map/pallas_call | solution.py:29
  111.6 22.4 %all_to_all.32 = f32[64,1,128]{2,1,0:T(1,128)S(1)} all-to-all(f32[64,1,128]{2,1,0:T(1,128)S(1)} %bitcast.15), channel_id=1, replica_groups=mesh['grp'=2,'gx_0'=4,'gx_1'=16,'gy'=2] {'gx_0','gx_1'}, dimensions={0} | all-to-all | bytes 65536 | tf_op jit(solution)/shard_map/all_to_all | solution.py:595
  134.0 1.8 collective-permute-start.10
  135.9 0.9 collective-permute-done.10.stats_other
  136.7 0.8 copy-done.6
  137.7 3.4 %shard_map.86 = (bf16[8,512,128]{2,1,0:T(8,128)(2,1)}, bf16[64,4,16,128]{3,2,1,0:T(8,128)(2,1)S(1)}) custom-call(bf16[8,528,128]{2,1,0:T(8,128)(2,1)} %get-tuple-element.23.own_in.block_in, bf16[4,512,128]{2,1,0:T(8,128)(2,1)} %copy-done.6, bf16[8,512,128]{2,1,0:T(8,128)(2,1)} %get-tuple-element.30.conv_in, bf16[4,512,128]{2,1,0:T(8,128)(2,1)} %copy-done.7, ...), custom_call_target="tpu_custom_call" | custom-call | flops 603979776 | bytes 1048576 | tf_op jit(solution)/shard_map/pallas_call | solution.py:29
  141.1 55.4 %all_to_all.33.received = bf16[64,4,16,128]{3,2,1,0:T(8,128)(2,1)S(1)} all-to-all(bf16[64,4,16,128]{3,2,1,0:T(8,128)(2,1)S(1)} %get-tuple-element.34), channel_id=1, replica_groups=mesh['grp'=2,'gx_0'=4,'gx_1'=16,'gy'=2] {'gx_0','gx_1'}, dimensions={0} | all-to-all | bytes 2097152 | tf_op jit(solution)/shard_map/all_to_all | solution.py:613
  196.6 3.4 %collective-permute-start.11 = (bf16[32,4,16,128]{3,2,1,0:T(8,128)(2,1)S(1)}, bf16[32,4,16,128]{3,2,1,0:T(8,128)(2,1)S(1)}, u32[]{:S(2)}, u32[]{:S(2)}) collective-permute-start(bf16[32,4,16,128]{3,2,1,0:T(8,128)(2,1)S(1)} %slice_select_fusion), channel_id=1, source_target_pairs={{0,1},{1,0},{2,3},{3,2},{4,5},{5,4},{6,7},{7,6},{8,9},{9,8},{10,11... | collective-permute-start | bytes 1572872 | tf_op jit(solution)/shard_map/ppermute | solution.py:475
  200.0 1.5 collective-permute-done.11.other
  201.6 4.6 %shard_map.87 = bf16[64,16,512]{2,1,0:T(8,128)(2,1)} custom-call(bf16[8,512,128]{2,1,0:T(8,128)(2,1)} %get-tuple-element.33.own_in, bf16[64,4,16,128]{3,2,1,0:T(8,128)(2,1)S(1)} %all_to_all.33.received, bf16[32,4,16,128]{3,2,1,0:T(8,128)(2,1)S(1)} %collective-permute-done.11.other), custom_call_target="tpu_custom_call" | custom-call | flops 603979776 | bytes 1048576 | tf_op jit(solution)/shard_map/pallas_call | solution.py:29
  (47 shorter events, 3.9 us)
Async XLA Ops:
  0.0 47.7 %copy-start = (bf16[64,16,512]{2,1,0:T(8,128)(2,1)S(1)}, bf16[64,16,512]{2,1,0:T(8,128)(2,1)}, u32[]{:S(2)}) copy-start(bf16[64,16,512]{2,1,0:T(8,128)(2,1)} %own_in.1) | copy-start | bytes 3145732
  3.1 44.6 %collective-permute-start.1 = (bf16[64,8,512]{2,1,0:T(8,128)(2,1)}, bf16[64,8,512]{2,1,0:T(8,128)(2,1)S(1)}, u32[]{:S(2)}, u32[]{:S(2)}) collective-permute-start(bf16[64,8,512]{2,1,0:T(8,128)(2,1)} %get-tuple-element.21), channel_id=1, source_target_pairs={{2,0},{4,2},{6,4},{8,6},{10,8},{12,10},{14,12},{16,14},{18,16},{20... | collective-permute-start | bytes 1572872 | tf_op jit(solution)/shard_map/ppermute | solution.py:498
  4.4 43.3 %collective-permute-start = (bf16[64,8,512]{2,1,0:T(8,128)(2,1)}, bf16[64,8,512]{2,1,0:T(8,128)(2,1)S(1)}, u32[]{:S(2)}, u32[]{:S(2)}) collective-permute-start(bf16[64,8,512]{2,1,0:T(8,128)(2,1)} %get-tuple-element.20), channel_id=1, source_target_pairs={{0,2},{2,4},{4,6},{6,8},{8,10},{10,12},{12,14},{14,16},{16,18},{18... | collective-permute-start | bytes 1572872 | tf_op jit(solution)/shard_map/ppermute | solution.py:498
  10.4 39.6 %collective-permute-start.5 = (bf16[64,8,512]{2,1,0:T(8,128)(2,1)}, bf16[64,8,512]{2,1,0:T(8,128)(2,1)S(1)}, u32[]{:S(2)}, u32[]{:S(2)}) collective-permute-start(bf16[64,8,512]{2,1,0:T(8,128)(2,1)} %get-tuple-element.20), channel_id=1, source_target_pairs={{2,0},{4,2},{6,4},{8,6},{10,8},{12,10},{14,12},{16,14},{18,16},{20... | collective-permute-start | bytes 1572872 | tf_op jit(solution)/shard_map/ppermute | solution.py:499
  11.7 38.4 %collective-permute-start.4 = (bf16[64,8,512]{2,1,0:T(8,128)(2,1)}, bf16[64,8,512]{2,1,0:T(8,128)(2,1)S(1)}, u32[]{:S(2)}, u32[]{:S(2)}) collective-permute-start(bf16[64,8,512]{2,1,0:T(8,128)(2,1)} %get-tuple-element.21), channel_id=1, source_target_pairs={{0,2},{2,4},{4,6},{6,8},{8,10},{10,12},{12,14},{14,16},{16,18},{18... | collective-permute-start | bytes 1572872 | tf_op jit(solution)/shard_map/ppermute | solution.py:499
  16.8 52.6 %all-to-all-start = ((bf16[64,16,128]{2,1,0:T(8,128)(2,1)}), bf16[64,16,128]{2,1,0:T(8,128)(2,1)S(1)}, u32[]{:S(2)}, u32[]{:S(2)}) async-start(bf16[64,16,128]{2,1,0:T(8,128)(2,1)} %get-tuple-element.22), calls=%async_computation | async-start | bytes 524288 | tf_op jit(solution)/shard_map/all_to_all | solution.py:500
  47.7 2.3 %copy-start.4 = (bf16[64,8,512]{2,1,0:T(8,128)(2,1)}, bf16[64,8,512]{2,1,0:T(8,128)(2,1)S(1)}, u32[]{:S(2)}) copy-start(bf16[64,8,512]{2,1,0:T(8,128)(2,1)S(1)} %collective-permute-done.1.below_in) | copy-start | bytes 1572868
  47.8 2.3 %copy-start.5 = (bf16[64,8,512]{2,1,0:T(8,128)(2,1)}, bf16[64,8,512]{2,1,0:T(8,128)(2,1)S(1)}, u32[]{:S(2)}) copy-start(bf16[64,8,512]{2,1,0:T(8,128)(2,1)S(1)} %collective-permute-done.above_in) | copy-start | bytes 1572868
  47.9 21.5 %collective-permute-start.2 = (bf16[64,32,128]{2,1,0:T(8,128)(2,1)S(1)}, bf16[64,32,128]{2,1,0:T(8,128)(2,1)}, u32[]{:S(2)}, u32[]{:S(2)}) collective-permute-start(bf16[64,32,128]{2,1,0:T(8,128)(2,1)S(1)} %pad_maximum_fusion), channel_id=1, source_target_pairs={{0,1},{1,0},{2,3},{3,2},{4,5},{5,4},{6,7},{7,6},{8,9},{9,8},{10,11... | collective-permute-start | bytes 1572872 | tf_op jit(solution)/shard_map/ppermute | solution.py:475
  50.0 28.4 %copy-start.2 = (bf16[64,8,512]{2,1,0:T(8,128)(2,1)}, bf16[64,8,512]{2,1,0:T(8,128)(2,1)S(1)}, u32[]{:S(2)}) copy-start(bf16[64,8,512]{2,1,0:T(8,128)(2,1)S(1)} %collective-permute-done.5.below_in) | copy-start | bytes 1572868
  50.1 28.3 %copy-start.3 = (bf16[64,8,512]{2,1,0:T(8,128)(2,1)}, bf16[64,8,512]{2,1,0:T(8,128)(2,1)S(1)}, u32[]{:S(2)}) copy-start(bf16[64,8,512]{2,1,0:T(8,128)(2,1)S(1)} %collective-permute-done.4.above_in) | copy-start | bytes 1572868
  50.2 39.5 %collective-permute-start.6 = (bf16[64,16,128]{2,1,0:T(8,128)(2,1)S(1)}, bf16[64,16,128]{2,1,0:T(8,128)(2,1)S(1)}, u32[]{:S(2)}, u32[]{:S(2)}) collective-permute-start(bf16[64,16,128]{2,1,0:T(8,128)(2,1)S(1)} %pad_maximum_fusion.1), channel_id=1, source_target_pairs={{0,1},{1,0},{2,3},{3,2},{4,5},{5,4},{6,7},{7,6},{8,9},{9,8},{10,11... | collective-permute-start | bytes 786440 | tf_op jit(solution)/shard_map/ppermute | solution.py:475
  78.4 23.1 %all-to-all-start.1 = ((f32[64,1,128]{2,1,0:T(1,128)}), f32[64,1,128]{2,1,0:T(1,128)S(1)}, u32[]{:S(2)}, u32[]{:S(2)}) async-start(f32[64,1,128]{2,1,0:T(1,128)} %bitcast.4), calls=%async_computation.1 | async-start | bytes 65536 | tf_op jit(solution)/shard_map/all_to_all | solution.py:548
  90.3 14.6 %copy-start.9 = (f32[2,64]{1,0:T(2,128)S(1)}, f32[2,64]{1,0:T(2,128)}, u32[]{:S(2)}) copy-start(f32[2,64]{1,0:T(2,128)} %param.15) | copy-start | bytes 1540
  90.3 14.6 %copy-start.10 = (f32[2,64]{1,0:T(2,128)S(1)}, f32[2,64]{1,0:T(2,128)}, u32[]{:S(2)}) copy-start(f32[2,64]{1,0:T(2,128)} %param.14) | copy-start | bytes 1540
  90.3 14.7 %copy-start.11 = (bf16[4,512,128]{2,1,0:T(8,128)(2,1)S(1)}, bf16[4,512,128]{2,1,0:T(8,128)(2,1)}, u32[]{:S(2)}) copy-start(bf16[4,512,128]{2,1,0:T(8,128)(2,1)} %get-tuple-element.24) | copy-start | bytes 1572868
  97.1 8.3 %collective-permute-start.7 = (bf16[2,8,16,128]{3,2,1,0:T(8,128)(2,1)}, bf16[2,8,16,128]{3,2,1,0:T(8,128)(2,1)S(1)}, u32[]{:S(2)}, u32[]{:S(2)}) collective-permute-start(bf16[2,8,16,128]{3,2,1,0:T(8,128)(2,1)} %get-tuple-element.28), channel_id=1, source_target_pairs={{0,1},{1,0},{2,3},{3,2},{4,5},{5,4},{6,7},{7,6},{8,9},{9,8},{10,11... | collective-permute-start | bytes 196616 | tf_op jit(solution)/shard_map/ppermute | solution.py:475
  101.5 4.3 %collective-permute-start.8 = (f32[64,128]{1,0:T(8,128)S(1)}, f32[64,128]{1,0:T(8,128)S(1)}, u32[]{:S(2)}, u32[]{:S(2)}) collective-permute-start(f32[64,128]{1,0:T(8,128)S(1)} %bitcast.11), channel_id=1, source_target_pairs={{0,1},{1,0},{2,3},{3,2},{4,5},{5,4},{6,7},{7,6},{8,9},{9,8},{10,11... | collective-permute-start | bytes 98312 | tf_op jit(solution)/shard_map/ppermute | solution.py:475
  105.1 31.7 %collective-permute-start.3 = (bf16[4,512,128]{2,1,0:T(8,128)(2,1)S(1)}, bf16[4,512,128]{2,1,0:T(8,128)(2,1)S(1)}, u32[]{:S(2)}, u32[]{:S(2)}) collective-permute-start(bf16[4,512,128]{2,1,0:T(8,128)(2,1)S(1)} %copy-done.11), channel_id=1, source_target_pairs={{0,1},{1,0},{2,3},{3,2},{4,5},{5,4},{6,7},{7,6},{8,9},{9,8},{10,11... | collective-permute-start | bytes 1572872 | tf_op jit(solution)/shard_map/ppermute | solution.py:475
  111.1 25.6 %collective-permute-start.9 = (bf16[4,512,128]{2,1,0:T(8,128)(2,1)}, bf16[4,512,128]{2,1,0:T(8,128)(2,1)S(1)}, u32[]{:S(2)}, u32[]{:S(2)}) collective-permute-start(bf16[4,512,128]{2,1,0:T(8,128)(2,1)} %get-tuple-element.31), channel_id=1, source_target_pairs={{0,1},{1,0},{2,3},{3,2},{4,5},{5,4},{6,7},{7,6},{8,9},{9,8},{10,11... | collective-permute-start | bytes 1572872 | tf_op jit(solution)/shard_map/ppermute | solution.py:475
  134.0 2.7 %collective-permute-start.10 = (f32[64,128]{1,0:T(8,128)S(1)}, f32[64,128]{1,0:T(8,128)S(1)}, u32[]{:S(2)}, u32[]{:S(2)}) collective-permute-start(f32[64,128]{1,0:T(8,128)S(1)} %bitcast.13), channel_id=1, source_target_pairs={{0,1},{1,0},{2,3},{3,2},{4,5},{5,4},{6,7},{7,6},{8,9},{9,8},{10,11... | collective-permute-start | bytes 98312 | tf_op jit(solution)/shard_map/ppermute | solution.py:475
  136.7 0.8 copy-start.6
  136.7 1.0 copy-start.7
  196.6 5.0 %collective-permute-start.11 = (bf16[32,4,16,128]{3,2,1,0:T(8,128)(2,1)S(1)}, bf16[32,4,16,128]{3,2,1,0:T(8,128)(2,1)S(1)}, u32[]{:S(2)}, u32[]{:S(2)}) collective-permute-start(bf16[32,4,16,128]{3,2,1,0:T(8,128)(2,1)S(1)} %slice_select_fusion), channel_id=1, source_target_pairs={{0,1},{1,0},{2,3},{3,2},{4,5},{5,4},{6,7},{7,6},{8,9},{9,8},{10,11... | collective-permute-start | bytes 1572872 | tf_op jit(solution)/shard_map/ppermute | solution.py:475
  (2 other events, 1.4 us)

commit v3 on v2

--- a/solution.py
+++ b/solution.py
@@ -96,20 +96,6 @@
         return 0
 
     lax.fori_loop(0, channels // some, step, 0)
-
-
-def term_group(terms_ref, start):
-    return terms_ref[pl.ds(pl.multiple_of(start, 2 * STEP), 2 * STEP), :].astype(jnp.float32)
-
-
-def column_terms(terms_ref, core, cols, out_ref):
-    def twice(rows):
-        return jnp.where(lane_half(rows.shape[0]), pltpu.roll(rows, LANES // 2, 1), rows)
-
-    for first in range(0, cols, LANES):
-        at = pl.multiple_of(core * cols + first, LANES)
-        out_ref[first : first + LANES] = twice(terms_ref[pl.ds(at, LANES), :].astype(jnp.float32))
-    out_ref[cols:] = twice(term_group(terms_ref, cols - 2 * STEP * core))
 
 
 def fill_rows(x_ref, sources, side_sources, row_terms, col_terms, scale, core, mask):
@@ -162,8 +148,6 @@
 
 
 OWN_TAPS = ((1, 2, 0, None), (0, 1, None, 2))
-NEAR_TAPS = ((2, None, 1, None), (None, 0, None, 1))
-FAR_TAPS = ((0, None), (None, 2))
 
 
 def product(values, weights):
@@ -213,46 +197,60 @@
 
 
 def prepare_kernel(
-    pair, feats, w_row, w_col, top_out, bottom_out, terms_ref, top, bottom, feats_in, row_in,
-    col_in, sem,
+    pair, feats, w_row, w_col, top, bottom, col_terms, row_terms, feats_in, row_in, col_in, sem
 ):
-    parts = start_all(sem, 0, ((pair.at[:, :STEP], top), (pair.at[:, STEP:], bottom)))
+    channels = pair.shape[0]
+    parts = start_all(
+        sem, 0,
+        ((pair.at[:, :STEP], top.at[pl.ds(0, channels)]),
+         (pair.at[:, STEP:], bottom.at[pl.ds(0, channels)])),
+    )
     inputs = start_all(sem, 2, ((feats, feats_in), (w_row, row_in), (w_col, col_in)))
     wait_all(inputs)
-    terms = jnp.concatenate(
-        [product(feats_in[...], w[...]) for w in (row_in, col_in)], axis=1
-    ).astype(jnp.bfloat16)
-    terms_ref[...] = jnp.broadcast_to(terms[None], terms_ref.shape)
+    zero = jnp.zeros((2 * STEP, LANES - channels), jnp.float32)
+    row = jnp.concatenate([product(feats_in[...], row_in[...]), zero], axis=1)
+    col = jnp.concatenate([product(feats_in[...], col_in[...]), zero], axis=1)
+    packed = halves(col[:STEP], col[STEP:]).astype(jnp.bfloat16)
+    col_terms[...] = jnp.broadcast_to(packed[None], col_terms.shape)
+    row_terms[...] = halves(row[:STEP], row[STEP:])
+    empty = jnp.zeros((STEP, top.shape[2] - LANES), jnp.float32)
+    for ref, rows in ((top, row[:STEP]), (bottom, row[STEP:])):
+        ref[channels] = jnp.concatenate([rows, empty], axis=1).astype(jnp.bfloat16)
     wait_all(parts)
-    wait_all(start_all(sem, 0, ((top, top_out), (bottom, bottom_out))))
 
 
 def first_kernel(
-    devices, own_in, above_in, below_in, side_in, terms_in, taps_in,
-    own_out, near_out, conv_out, give_out, stats_ref,
-    x_own, x_near, conv_ref, p_ref, own, above, below, side, terms, taps,
+    devices, own_in, above_in, below_in, side, terms, mine, taps_in,
+    own_out, conv_out, give_out, down_out, up_out, edge_ref, stats_ref,
+    x_own, x_near, conv_ref, p_ref, down_ref, up_ref, own, above, below, taps,
     own_flat, above_flat, below_flat, side_flat, col_terms, row_terms, sem,
 ):
     row_at, core = lax.axis_index(GX), lax.axis_index("gy")
-    _, rows, cols = own.shape
+    channels, rows, cols = own.shape
     half = STEP // 2
     inputs = start_all(
-        sem, 0,
-        ((terms_in, terms), (side_in, side), (own_in, own), (above_in, above), (below_in, below),
-         (taps_in, taps)),
-    )
-    inputs[0].wait()
-    column_terms(terms, core, cols, col_terms)
-    mine = term_group(terms, row_at * rows)
-    up = term_group(terms, jnp.maximum(row_at - 1, 0) * rows)
-    down = term_group(terms, jnp.minimum(row_at + 1, devices - 1) * rows)
-    row_terms[0] = halves(mine[:STEP], mine[STEP:])
-    row_terms[1] = halves(up[STEP:], down[:STEP])
+        sem, 0, ((own_in, own), (above_in, above), (below_in, below), (taps_in, taps))
+    )
+
+    def put_terms(source, at):
+        value = terms[source].astype(jnp.float32)
+        other = pltpu.roll(value, LANES // 2, 1)
+        col_terms[pl.ds(at, STEP), :] = jnp.where(lane_half(STEP), value, other)
+        col_terms[pl.ds(at + STEP, STEP), :] = jnp.where(lane_half(STEP), other, value)
+
+    peers = cols // rows
+
+    def put_own(i, _):
+        put_terms(peers * core + i, pl.multiple_of(i * rows, 2 * STEP))
+        return 0
+
+    lax.fori_loop(0, peers, put_own, 0)
+    put_terms(peers - core, cols)
+    row_terms[0] = mine[...].astype(jnp.bfloat16).astype(jnp.float32)
     mask = reach_mask(core)
     tall = rows + 2 * STEP
-    inputs[1].wait()
     widen(side, side_flat)
-    inputs[2].wait()
+    inputs[0].wait()
     widen(own, own_flat)
     fill_rows(
         x_own, ((own_flat, 0, rows), (own_flat, STEP, rows)),
@@ -260,97 +258,89 @@
         row_terms.at[0], col_terms, None, core, mask,
     )
     given = x_own.at[pl.ds(half * (1 - core), half), pl.ds(0, cols)]
-    outputs = start_all(sem, 6, ((x_own, own_out), (given, give_out)))
-    wait_all(inputs[3:5])
-    widen(above, above_flat)
-    widen(below, below_flat)
+    outputs = start_all(sem, 4, ((x_own.at[:, pl.ds(0, cols)], own_out), (given, give_out)))
+    wait_all(inputs[1:3])
+    widen(above.at[pl.ds(0, channels)], above_flat)
+    widen(below.at[pl.ds(0, channels)], below_flat)
+    row_terms[1] = halves(
+        above[channels, :, :LANES].astype(jnp.float32),
+        below[channels, :, :LANES].astype(jnp.float32),
+    )
     fill_rows(
         x_near, ((above_flat, 0, STEP), (below_flat, 0, STEP)),
         ((side_flat, 0, tall), (side_flat, STEP + rows, tall)),
         row_terms.at[1], col_terms, inside_of(row_at, devices), core, mask,
     )
-    outputs += start_all(sem, 8, ((x_near, near_out),))
-    inputs[5].wait()
+    inputs[3].wait()
     stats = conv_own_rows(x_own, x_near, weights_of(taps, OWN_TAPS), p_ref, conv_ref)
-    outputs += start_all(sem, 9, ((conv_ref, conv_out),))
+    outputs += start_all(sem, 6, ((conv_ref, conv_out),))
+    lower = lane_half(LANES)
+    for i in range(half):
+        for first in range(0, cols, LANES):
+            at = slice(first, first + LANES)
+            one = conv_ref[i, at, :].astype(jnp.float32)
+            two = conv_ref[i + half, at, :].astype(jnp.float32)
+            up_ref[i, at, :] = jnp.where(lower, one, pltpu.roll(two, LANES // 2, 1)).astype(
+                jnp.bfloat16
+            )
+            down_ref[i, at, :] = jnp.where(lower, pltpu.roll(one, LANES // 2, 1), two).astype(
+                jnp.bfloat16
+            )
+    outputs += start_all(sem, 7, ((down_ref, down_out), (up_ref, up_out)))
+    edge_at = pl.multiple_of((cols - 2 * STEP) * (1 - core), 2 * STEP)
+    edge_ref[...] = conv_ref[:, pl.ds(edge_at, 2 * STEP), :]
     stats_ref[...] = jnp.broadcast_to(stats, stats_ref.shape)
     wait_all(outputs)
 
 
-def far_kernel(
-    devices, own_in, near_in, conv_in, above_in, below_in, side_in, terms_in, taps_in,
-    conv_out, edge_out,
-    x_own, x_near, x_far, conv_ref, edge_ref, p_ref, above, below, side, terms, taps,
-    above_flat, below_flat, side_flat, col_terms, row_terms, sem,
-):
-    row_at, core = lax.axis_index(GX), lax.axis_index("gy")
-    _, _, cols = above.shape
-    rows = 2 * STEP
-    edge_at = pl.multiple_of((cols - 2 * STEP) * (1 - core), 2 * STEP)
-    inputs = start_all(
-        sem, 0,
-        ((terms_in, terms), (side_in, side), (above_in, above), (below_in, below),
-         (own_in, x_own), (near_in, x_near),
-         (conv_in.at[:, pl.ds(edge_at, 2 * STEP)], edge_ref.at[0]), (taps_in, taps)),
-    )
-    inputs[0].wait()
-    column_terms(terms, core, cols, col_terms)
-    up = term_group(terms, jnp.maximum(row_at - 1, 0) * rows)
-    down = term_group(terms, jnp.minimum(row_at + 1, devices - 1) * rows)
-    row_terms[...] = halves(up[:STEP], down[STEP:])
-    wait_all(inputs[1:4])
-    widen(side, side_flat)
-    widen(above, above_flat)
-    widen(below, below_flat)
-    fill_rows(
-        x_far, ((above_flat, 0, STEP), (below_flat, 0, STEP)),
-        ((side_flat, 0, 2 * STEP), (side_flat, STEP, 2 * STEP)),
-        row_terms, col_terms, inside_of(row_at, devices), core, reach_mask(core),
-    )
-    wait_all(inputs[4:])
-    near_weights, far_weights = weights_of(taps, NEAR_TAPS), weights_of(taps, FAR_TAPS)
-    for i in range(STEP):
-        p = p_ref.at[i % 2]
-        near = jnp.concatenate([x_own[i], x_near[i]], axis=1)
-        p[...] = product(near, near_weights) + product(x_far[i], far_weights)
-        for first in range(0, cols, LANES):
-            conv_ref[i, first : first + LANES, :] = shifted_sum(p, first).astype(jnp.bfloat16)
-    edge_ref[1] = conv_ref[:, pl.ds(edge_at, 2 * STEP), :]
-    wait_all(start_all(sem, 0, ((edge_ref, edge_out), (conv_ref, conv_out))))
-
-
 def second_kernel(
-    devices, cells, own_in, far_in, side, stats, stats_other, gains, taps_in,
+    devices, cells, own_in, above_in, below_in, edge, corner, stats, stats_other, gains, taps_in,
     conv_out, give_out, stats_ref,
-    a_own, a_near, conv_ref, p_ref, own, far, taps, sem,
+    a_own, a_near, conv_ref, p_ref, own, above, below, taps, sem,
 ):
     row_at, core = lax.axis_index(GX), lax.axis_index("gy")
     cols = own.shape[1]
     half = STEP // 2
-    inputs = start_all(sem, 0, ((far_in, far), (own_in, own), (taps_in, taps)))
+    inputs = start_all(
+        sem, 0, ((own_in, own), (above_in, above), (below_in, below), (taps_in, taps))
+    )
     factor, offset = affine_of(0, (stats, stats_other), gains, cells)
     inside = inside_of(row_at, devices)
     mask = reach_mask(core)
 
-    def activated(value, scale):
-        value = elu(value.astype(jnp.float32) * factor + offset)
-        return value if scale is None else value * scale
-
-    def fill(to_ref, source, which, scale):
-        def step(i, _):
-            for first in range(0, cols, LANES):
-                at = slice(first, first + LANES)
-                to_ref[i, at, :] = activated(source[i, at, :], scale).astype(jnp.bfloat16)
-            beyond = jnp.where(mask, activated(side[which, i], scale), 0.0)
-            to_ref[i, cols:, :] = beyond.astype(jnp.bfloat16)
-            return 0
-
-        lax.fori_loop(0, STEP, step, 0)
+    def activated(value):
+        return elu(value.astype(jnp.float32) * factor + offset)
+
+    def fill_own(i, _):
+        for first in range(0, cols, LANES):
+            at = slice(first, first + LANES)
+            a_own[i, at, :] = activated(own[i, at, :]).astype(jnp.bfloat16)
+        beyond = jnp.where(mask, activated(edge[i]), 0.0)
+        a_own[i, cols:, :] = beyond.astype(jnp.bfloat16)
+        return 0
+
+    def two_rows(up, down):
+        up, down = up.astype(jnp.float32), down.astype(jnp.float32)
+        lower = lane_half(up.shape[0])
+        return (
+            jnp.where(lower, up, pltpu.roll(down, LANES // 2, 1)),
+            jnp.where(lower, pltpu.roll(up, LANES // 2, 1), down),
+        )
+
+    def fill_near(i, _):
+        for first in range(0, cols, LANES):
+            at = slice(first, first + LANES)
+            for k, value in enumerate(two_rows(above[i, at, :], below[i, at, :])):
+                a_near[i + half * k, at, :] = (activated(value) * inside).astype(jnp.bfloat16)
+        for k, value in enumerate(two_rows(corner[0, i], corner[1, i])):
+            beyond = jnp.where(mask, activated(value) * inside, 0.0)
+            a_near[i + half * k, cols:, :] = beyond.astype(jnp.bfloat16)
+        return 0
 
     inputs[0].wait()
-    fill(a_near, far, 1, inside)
+    lax.fori_loop(0, STEP, fill_own, 0)
     wait_all(inputs[1:])
-    fill(a_own, own, 0, None)
+    lax.fori_loop(0, half, fill_near, 0)
     stats = conv_own_rows(a_own, a_near, weights_of(taps, OWN_TAPS), p_ref, conv_ref)
     given = conv_ref.at[pl.ds(half * (1 - core), half)]
     outputs = start_all(sem, 0, ((given, give_out), (conv_ref, conv_out)))
@@ -359,18 +349,14 @@
 
 
 def pack_kernel(
-    cells, block_in, block_in_other, conv_in, conv_other_in, stats, stats_other, gains,
+    cells, block_in, other, conv_in, conv_other, stats, stats_other, gains,
     block_out_out, send_ref,
-    out_ref, own, other, conv, conv_other, sem,
+    out_ref, own, conv, sem,
 ):
     core = lax.axis_index("gy")
     cols = conv.shape[1]
     half = STEP // 2
-    inputs = start_all(
-        sem, 0,
-        ((block_in.at[:, pl.ds(0, cols)], own), (conv_in, conv), (block_in_other, other),
-         (conv_other_in, conv_other)),
-    )
+    inputs = start_all(sem, 0, ((block_in, own), (conv_in, conv)))
     factor, offset = affine_of(1, (stats, stats_other), gains, cells)
     wide = 2 * STEP
     peers, some = cols // wide, LANES // wide
@@ -387,7 +373,7 @@
 
     wait_all(inputs[:2])
     lax.fori_loop(0, STEP, mine, 0)
-    outputs = start_all(sem, 4, ((out_ref, block_out_out),))
+    outputs = start_all(sem, 2, ((out_ref, block_out_out),))
 
     def step(i, _):
         for first in range(0, cols, LANES):
@@ -398,7 +384,6 @@
             send_ref[pl.ds(peers * (1 - core) + first // wide, some), i] = value
         return 0
 
-    wait_all(inputs[2:])
     lax.fori_loop(0, half, step, 0)
     wait_all(outputs)
 
@@ -476,17 +461,16 @@
 
     down = functools.partial(lax.ppermute, axis_name=GX, perm=chain(devices, 1))
     up = functools.partial(lax.ppermute, axis_name=GX, perm=chain(devices, -1))
-    eight = (channels, STEP, cols)
-    top, bottom, terms = call(
+    eight = (channels + 1, STEP, cols)
+    top, bottom, terms, mine = call(
         prepare_kernel,
         (
-            (HBM, eight, bf16),
-            (HBM, eight, bf16),
-            (VMEM, (devices, rows, 2 * channels), bf16),
+            (VMEM, eight, bf16),
+            (VMEM, eight, bf16),
+            (VMEM, (devices, STEP, LANES), bf16),
+            (VMEM, (STEP, LANES), f32),
         ),
         [
-            VMEM(eight, bf16),
-            VMEM(eight, bf16),
             VMEM(residue_feats.shape, bf16),
             VMEM(w_row.T.shape, bf16),
             VMEM(w_col.T.shape, bf16),
@@ -495,31 +479,28 @@
         conv_flops // 16,
         ((HBM, pair_feats), (HBM, residue_feats), (HBM, w_row.T), (HBM, w_col.T)),
     )
-    above_near, below_near = down(bottom), up(top)
-    above_far, below_far = down(top), up(bottom)
+    above, below = down(bottom), up(top)
     terms = lax.all_to_all(terms, GX, 0, 0, tiled=True)
-    terms = terms.reshape(devices * rows, 2 * channels)
     gains = jnp.tile(jnp.concatenate([norm_scale, norm_shift], axis=0), (1, 2))
-
     near_side = swap(
-        jnp.concatenate([edge(above_near), edge(pair_feats), edge(below_near)], axis=1)
-    )
-    far_side = swap(jnp.concatenate([edge(above_far), edge(below_far)], axis=1))
+        jnp.concatenate([edge(above[:channels]), edge(pair_feats), edge(below[:channels])], axis=1)
+    )
 
     taps_shape = VMEM(first_taps.shape, bf16)
-    terms_shape = VMEM(terms.shape, bf16)
     whole = (STEP, cols, LANES)
     part = (STEP // 2, cols, LANES)
     wide = (STEP, cols + 2 * STEP, LANES)
     products = VMEM((2, cols + 2 * STEP, 3 * LANES), f32)
     sums = (devices, LANES)
-    own_rows, near_rows, conv_own, own_give, stats = call(
+    own_rows, conv_own, own_give, conv_down, conv_up, edges, stats = call(
         functools.partial(first_kernel, devices),
         (
-            (HBM, wide, bf16),
-            (HBM, wide, bf16),
+            (HBM, whole, bf16),
             (HBM, whole, bf16),
             (HBM, part, bf16),
+            (HBM, part, bf16),
+            (HBM, part, bf16),
+            (VMEM, (STEP, 2 * STEP, LANES), bf16),
             (VMEM, sums, f32),
         ),
         [
@@ -527,11 +508,11 @@
             VMEM(wide, bf16),
             VMEM(whole, bf16),
             products,
+            VMEM(part, bf16),
+            VMEM(part, bf16),
             VMEM(pair_feats.shape, bf16),
             VMEM(eight, bf16),
             VMEM(eight, bf16),
-            VMEM(near_side.shape, bf16),
-            terms_shape,
             taps_shape,
             flat_of(channels, rows, cols),
             flat_of(channels, STEP, cols),
@@ -540,40 +521,21 @@
             VMEM(wide[1:], f32),
             VMEM((2, STEP, LANES), f32),
         ],
-        10,
+        9,
         conv_flops,
-        ((HBM, pair_feats), (HBM, above_near), (HBM, below_near), (HBM, near_side),
-         (HBM, terms), (HBM, first_taps)),
-    )
+        ((HBM, pair_feats), (HBM, above), (HBM, below), (VMEM, near_side), (VMEM, terms),
+         (VMEM, mine), (HBM, first_taps)),
+    )
+    conv_above, conv_below = down(conv_down), up(conv_up)
     stats = lax.all_to_all(stats, GX, 0, 0, tiled=True)
     stats_other = swap(stats)
-    conv_far, edges = call(
-        functools.partial(far_kernel, devices),
-        ((HBM, whole, bf16), (HBM, (2, STEP, 2 * STEP, LANES), bf16)),
-        [
-            VMEM(wide, bf16),
-            VMEM(wide, bf16),
-            VMEM(wide, bf16),
-            VMEM(whole, bf16),
-            VMEM((2, STEP, 2 * STEP, LANES), bf16),
-            products,
-            VMEM(eight, bf16),
-            VMEM(eight, bf16),
-            VMEM(far_side.shape, bf16),
-            terms_shape,
-            taps_shape,
-            flat_of(channels, STEP, cols),
-            flat_of(channels, STEP, cols),
-            flat_of(channels, 2 * STEP, LANES),
-            VMEM(wide[1:], f32),
-            VMEM((STEP, LANES), f32),
-        ],
-        8,
-        conv_flops,
-        ((HBM, own_rows), (HBM, near_rows), (HBM, conv_own), (HBM, above_far),
-         (HBM, below_far), (HBM, far_side), (HBM, terms), (HBM, first_taps)),
-    )
     edges = swap(edges)
+    last = cols - 2 * STEP
+    corners = swap(
+        jnp.stack(
+            [jnp.where(first_core, x[:, last:], x[:, : 2 * STEP]) for x in (conv_above, conv_below)]
+        )
+    )
     own_other = swap(own_give)
     conv_second, second_give, stats = call(
         functools.partial(second_kernel, devices, cells),
@@ -584,13 +546,15 @@
             VMEM(whole, bf16),
             products,
             VMEM(whole, bf16),
-            VMEM(whole, bf16),
+            VMEM(part, bf16),
+            VMEM(part, bf16),
             taps_shape,
         ],
-        3,
+        4,
         conv_flops,
-        ((HBM, conv_own), (HBM, conv_far), (VMEM, edges), (VMEM, stats), (VMEM, stats_other),
-         (VMEM, gains), (HBM, second_taps)),
+        ((HBM, conv_own), (HBM, conv_above), (HBM, conv_below), (VMEM, edges),
+         (VMEM, corners), (VMEM, stats), (VMEM, stats_other), (VMEM, gains),
+         (HBM, second_taps)),
     )
     stats = lax.all_to_all(stats, GX, 0, 0, tiled=True)
     stats_other = swap(stats)
@@ -601,13 +565,11 @@
         [
             VMEM(whole, bf16),
             VMEM(whole, bf16),
-            VMEM(part, bf16),
             VMEM(whole, bf16),
-            VMEM(part, bf16),
         ],
-        5,
+        3,
         conv_flops,
-        ((HBM, own_rows), (HBM, own_other), (HBM, conv_second), (HBM, conv_other),
+        ((HBM, own_rows), (VMEM, own_other), (HBM, conv_second), (VMEM, conv_other),
          (VMEM, stats), (VMEM, stats_other), (VMEM, gains)),
     )
     received = lax.all_to_all(send, GX, 0, 0, tiled=True)

time: 207 us -> 203 us (0.981)
  blocking collectives: 77.8 us -> 104 us
  starting transfers between devices: 70.4 us -> 53.3 us
  Pallas kernels: 31.5 us -> 24.8 us
  waiting for transfers between devices: 23.5 us -> 18.6 us
    all_to_all x1 -> x0, starting transfers between devices: 30.9 us -> none  [body(): terms = lax.all_to_all(terms, GX, 0, 0, tiled=True)]
    all_to_all x0 -> x1, blocking collectives: none -> 30.6 us  [body(): terms = lax.all_to_all(terms, GX, 0, 0, tiled=True)]
    all_to_all x1 -> x0, waiting for transfers between devices: 18.5 us -> none  [body(): terms = lax.all_to_all(terms, GX, 0, 0, tiled=True)]
    ppermute x8, starting transfers between devices: 14.6 us -> 30.9 us  [swap(): return lax.ppermute(x, 'gy', SWAP)]
    all_to_all x1, waiting for transfers between devices: 2.11 us -> 9.71 us  [body(): stats = lax.all_to_all(stats, GX, 0, 0, tiled=True)]
    pallas_call x6 -> x5, Pallas kernels: 31.5 us -> 24.8 us  [call(): pl.pallas_call(kernel, out_shape=[space(shape, dtype) for space, shape, d...]
    ppermute x4, waiting for transfers between devices: 0.01 us -> 6.13 us  [the longest x2 6.12 us: body(): above, below = (down(bottom), up(top))]
    all_to_all x1, blocking collectives: 22.4 us -> 18 us  [body(): stats = lax.all_to_all(stats, GX, 0, 0, tiled=True)]
  transfers between devices with their start and end apart: 14 -> 13, of which waited for: 5 -> 6; matrix products, arithmetic and copies ran while one was open for 0% -> 0% of each run, Pallas kernels for 10% -> 3%
where the time goes in v3:
time: 203 us
  blocking collectives  104 us (51%)
  starting transfers between devices  53.3 us (26%)
  Pallas kernels  24.8 us (12%)
  waiting for transfers between devices  18.6 us (9%)
    all_to_all x1, blocking collectives, body(): received = lax.all_to_all(send, GX, 0, 0, tiled=True)  55.5 us
    ppermute x8, starting transfers between devices, swap(): return lax.ppermute(x, 'gy', SWAP)  30.9 us
    all_to_all x1, blocking collectives, body(): terms = lax.all_to_all(terms, GX, 0, 0, tiled=True)  30.6 us
    pallas_call x5, Pallas kernels, call(): pl.pallas_call(kernel, out_shape=[space(shape, dtype) for space, shape, d...  24.8 us
    all_to_all x1, blocking collectives, body(): stats = lax.all_to_all(stats, GX, 0, 0, tiled=True)  18 us
    all_to_all x1, starting transfers between devices, body(): stats = lax.all_to_all(stats, GX, 0, 0, tiled=True)  9.8 us
    all_to_all x1, waiting for transfers between devices, body(): stats = lax.all_to_all(stats, GX, 0, 0, tiled=True)  9.71 us
    ppermute x2, starting transfers between devices, body(): above, below = (down(bottom), up(top))  7.23 us
  transfers between devices with their start and end apart: 13, of which 6 were waited for; matrix products, arithmetic and copies ran while one was open for 0% of the time, Pallas kernels for 3%

profile of v3, /device:TPU:33, one launch (start us, length us, event | category | flops | bytes accessed | tf_op | source)
XLA Modules:
  0.0 202.9 jit_solution(15200973392571753677)
XLA Ops:
  0.0 1.4 shard_map.82
  1.5 1.3 collective-permute-start.1
  2.8 5.9 %collective-permute-start = (bf16[65,8,512]{2,1,0:T(8,128)(2,1)S(1)}, bf16[65,8,512]{2,1,0:T(8,128)(2,1)S(1)}, u32[]{:S(2)}, u32[]{:S(2)}) collective-permute-start(bf16[65,8,512]{2,1,0:T(8,128)(2,1)S(1)} %get-tuple-element.21), channel_id=1, source_target_pairs={{0,2},{2,4},{4,6},{6,8},{8,10},{10,12},{12,14},{14,16},{16,18},{18... | collective-permute-start | bytes 1597448 | tf_op jit(solution)/shard_map/ppermute | solution.py:482
  8.8 4.6 %collective-permute-done.1.below_in = bf16[65,8,512]{2,1,0:T(8,128)(2,1)S(1)} collective-permute-done((bf16[65,8,512]{2,1,0:T(8,128)(2,1)S(1)}, bf16[65,8,512]{2,1,0:T(8,128)(2,1)S(1)}, u32[]{:S(2)}, u32[]{:S(2)}) %collective-permute-start.1) | collective-permute-done | bytes 532512 | tf_op jit(solution)/shard_map/ppermute | solution.py:482
  13.4 1.5 collective-permute-done.above_in
  15.0 0.7 copy-done.2
  15.7 19.6 %collective-permute-start.2 = (bf16[64,32,128]{2,1,0:T(8,128)(2,1)S(1)}, bf16[64,32,128]{2,1,0:T(8,128)(2,1)S(1)}, u32[]{:S(2)}, u32[]{:S(2)}) collective-permute-start(bf16[64,32,128]{2,1,0:T(8,128)(2,1)S(1)} %pad_maximum_fusion), channel_id=1, source_target_pairs={{0,1},{1,0},{2,3},{3,2},{4,5},{5,4},{6,7},{7,6},{8,9},{9,8},{10,11... | collective-permute-start | bytes 1572872 | tf_op jit(solution)/shard_map/ppermute | solution.py:460
  35.4 30.6 %all_to_all.32.terms = bf16[64,8,128]{2,1,0:T(8,128)(2,1)S(1)} all-to-all(bf16[64,8,128]{2,1,0:T(8,128)(2,1)S(1)} %get-tuple-element.23), channel_id=1, replica_groups=mesh['grp'=2,'gx_0'=4,'gx_1'=16,'gy'=2] {'gx_0','gx_1'}, dimensions={0} | all-to-all | bytes 262144 | tf_op jit(solution)/shard_map/all_to_all | solution.py:483
  66.0 9.7 %shard_map.83 = (bf16[8,512,128]{2,1,0:T(8,128)(2,1)}, bf16[8,512,128]{2,1,0:T(8,128)(2,1)}, bf16[4,512,128]{2,1,0:T(8,128)(2,1)}, bf16[4,512,128]{2,1,0:T(8,128...) custom-call(bf16[64,16,512]{2,1,0:T(8,128)(2,1)} %own_in.1, ...), custom_call_target="tpu_custom_call" | custom-call | flops 603979776 | bytes 1048576 | tf_op jit(solution)/shard_map/pallas_call | solution.py:29
  75.7 1.3 collective-permute-start.5
  77.0 4.1 %collective-permute-start.4 = (bf16[4,512,128]{2,1,0:T(8,128)(2,1)}, bf16[4,512,128]{2,1,0:T(8,128)(2,1)S(1)}, u32[]{:S(2)}, u32[]{:S(2)}) collective-permute-start(bf16[4,512,128]{2,1,0:T(8,128)(2,1)} %get-tuple-element.28), channel_id=1, source_target_pairs={{0,2},{2,4},{4,6},{6,8},{8,10},{10,12},{12,14},{14,16},{16,18},{18... | collective-permute-start | bytes 1572872 | tf_op jit(solution)/shard_map/ppermute | solution.py:529
  81.1 9.8 %all-to-all-start.1 = ((f32[64,1,128]{2,1,0:T(1,128)}), f32[64,1,128]{2,1,0:T(1,128)S(1)}, u32[]{:S(2)}, u32[]{:S(2)}) async-start(f32[64,1,128]{2,1,0:T(1,128)} %bitcast.5), calls=%async_computation.1 | async-start | bytes 65536 | tf_op jit(solution)/shard_map/all_to_all | solution.py:530
  90.9 2.2 %collective-permute-start.6 = (bf16[8,16,128]{2,1,0:T(8,128)(2,1)S(1)}, bf16[8,16,128]{2,1,0:T(8,128)(2,1)S(1)}, u32[]{:S(2)}, u32[]{:S(2)}) collective-permute-start(bf16[8,16,128]{2,1,0:T(8,128)(2,1)S(1)} %get-tuple-element.30), channel_id=1, source_target_pairs={{0,1},{1,0},{2,3},{3,2},{4,5},{5,4},{6,7},{7,6},{8,9},{9,8},{10,11... | collective-permute-start | bytes 98312 | tf_op jit(solution)/shard_map/ppermute | solution.py:460
  93.1 9.7 %all-to-all-done.1 = f32[64,1,128]{2,1,0:T(1,128)S(1)} async-done(((f32[64,1,128]{2,1,0:T(1,128)}), f32[64,1,128]{2,1,0:T(1,128)S(1)}, u32[]{:S(2)}, u32[]{:S(2)}) %all-to-all-start.1) | async-done | bytes 32800 | tf_op jit(solution)/shard_map/all_to_all | solution.py:530
  102.8 3.3 %collective-permute-start.8 = (f32[64,128]{1,0:T(8,128)S(1)}, f32[64,128]{1,0:T(8,128)S(1)}, u32[]{:S(2)}, u32[]{:S(2)}) collective-permute-start(f32[64,128]{1,0:T(8,128)S(1)} %bitcast.14), channel_id=1, source_target_pairs={{0,1},{1,0},{2,3},{3,2},{4,5},{5,4},{6,7},{7,6},{8,9},{9,8},{10,11... | collective-permute-start | bytes 98312 | tf_op jit(solution)/shard_map/ppermute | solution.py:460
  107.5 5.6 %shard_map.84 = (bf16[8,512,128]{2,1,0:T(8,128)(2,1)}, bf16[4,512,128]{2,1,0:T(8,128)(2,1)}, f32[64,128]{1,0:T(8,128)S(1)}) custom-call(bf16[8,512,128]{2,1,0:T(8,128)(2,1)} %get-tuple-element.27.own_in, bf16[4,512,128]{2,1,0:T(8,128)(2,1)} %copy-done.4, bf16[4,512,128]{2,1,0:T(8,128)(2,1)} %copy-done.3, ...), custom_call_target="tpu_custom_call" | custom-call | flops 603979776 | bytes 1048576 | tf_op jit(solution)/shard_map/pallas_call | solution.py:29
  113.4 18.0 %all_to_all.33 = f32[64,1,128]{2,1,0:T(1,128)S(1)} all-to-all(f32[64,1,128]{2,1,0:T(1,128)S(1)} %bitcast.18), channel_id=1, replica_groups=mesh['grp'=2,'gx_0'=4,'gx_1'=16,'gy'=2] {'gx_0','gx_1'}, dimensions={0} | all-to-all | bytes 65536 | tf_op jit(solution)/shard_map/all_to_all | solution.py:559
  131.4 1.8 collective-permute-start.10
  133.3 0.9 collective-permute-done.10.stats_other
  134.1 3.4 %shard_map.85 = (bf16[8,512,128]{2,1,0:T(8,128)(2,1)}, bf16[64,4,16,128]{3,2,1,0:T(8,128)(2,1)S(1)}) custom-call(bf16[8,512,128]{2,1,0:T(8,128)(2,1)} %get-tuple-element.25.block_in, bf16[4,512,128]{2,1,0:T(8,128)(2,1)S(1)} %collective-permute-done.3.other, bf16[8,512,128]{2,1,0:T(8,128)(2,1)} %get-tuple-element.32.conv_in, ...), custom_call_target="tpu_custom_call" | custom-call | flops 603979776 | bytes 1048576 | tf_op jit(solution)/shard_map/pallas_call | solution.py:29
  137.5 55.5 %all_to_all.34.received = bf16[64,4,16,128]{3,2,1,0:T(8,128)(2,1)S(1)} all-to-all(bf16[64,4,16,128]{3,2,1,0:T(8,128)(2,1)S(1)} %get-tuple-element.36), channel_id=1, replica_groups=mesh['grp'=2,'gx_0'=4,'gx_1'=16,'gy'=2] {'gx_0','gx_1'}, dimensions={0} | all-to-all | bytes 2097152 | tf_op jit(solution)/shard_map/all_to_all | solution.py:575
  193.1 3.5 %collective-permute-start.11 = (bf16[32,4,16,128]{3,2,1,0:T(8,128)(2,1)S(1)}, bf16[32,4,16,128]{3,2,1,0:T(8,128)(2,1)S(1)}, u32[]{:S(2)}, u32[]{:S(2)}) collective-permute-start(bf16[32,4,16,128]{3,2,1,0:T(8,128)(2,1)S(1)} %slice_select_fusion), channel_id=1, source_target_pairs={{0,1},{1,0},{2,3},{3,2},{4,5},{5,4},{6,7},{7,6},{8,9},{9,8},{10,11... | collective-permute-start | bytes 1572872 | tf_op jit(solution)/shard_map/ppermute | solution.py:460
  196.6 1.5 collective-permute-done.11.other
  198.1 4.6 %shard_map.86 = bf16[64,16,512]{2,1,0:T(8,128)(2,1)} custom-call(bf16[8,512,128]{2,1,0:T(8,128)(2,1)} %get-tuple-element.35.own_in, bf16[64,4,16,128]{3,2,1,0:T(8,128)(2,1)S(1)} %all_to_all.34.received, bf16[32,4,16,128]{3,2,1,0:T(8,128)(2,1)S(1)} %collective-permute-done.11.other), custom_call_target="tpu_custom_call" | custom-call | flops 603979776 | bytes 1048576 | tf_op jit(solution)/shard_map/pallas_call | solution.py:29
  (35 shorter events, 1.8 us)
Async XLA Ops:
  0.0 8.7 %copy-start = (bf16[64,16,512]{2,1,0:T(8,128)(2,1)S(1)}, bf16[64,16,512]{2,1,0:T(8,128)(2,1)}, u32[]{:S(2)}) copy-start(bf16[64,16,512]{2,1,0:T(8,128)(2,1)} %own_in.1) | copy-start | bytes 3145732
  1.5 11.9 %collective-permute-start.1 = (bf16[65,8,512]{2,1,0:T(8,128)(2,1)S(1)}, bf16[65,8,512]{2,1,0:T(8,128)(2,1)S(1)}, u32[]{:S(2)}, u32[]{:S(2)}) collective-permute-start(bf16[65,8,512]{2,1,0:T(8,128)(2,1)S(1)} %get-tuple-element.22), channel_id=1, source_target_pairs={{2,0},{4,2},{6,4},{8,6},{10,8},{12,10},{14,12},{16,14},{18,16},{20... | collective-permute-start | bytes 1597448 | tf_op jit(solution)/shard_map/ppermute | solution.py:482
  2.8 12.1 %collective-permute-start = (bf16[65,8,512]{2,1,0:T(8,128)(2,1)S(1)}, bf16[65,8,512]{2,1,0:T(8,128)(2,1)S(1)}, u32[]{:S(2)}, u32[]{:S(2)}) collective-permute-start(bf16[65,8,512]{2,1,0:T(8,128)(2,1)S(1)} %get-tuple-element.21), channel_id=1, source_target_pairs={{0,2},{2,4},{4,6},{6,8},{8,10},{10,12},{12,14},{14,16},{16,18},{18... | collective-permute-start | bytes 1597448 | tf_op jit(solution)/shard_map/ppermute | solution.py:482
  13.4 1.6 copy-start.1
  14.9 0.8 copy-start.2
  15.7 50.2 %collective-permute-start.2 = (bf16[64,32,128]{2,1,0:T(8,128)(2,1)S(1)}, bf16[64,32,128]{2,1,0:T(8,128)(2,1)S(1)}, u32[]{:S(2)}, u32[]{:S(2)}) collective-permute-start(bf16[64,32,128]{2,1,0:T(8,128)(2,1)S(1)} %pad_maximum_fusion), channel_id=1, source_target_pairs={{0,1},{1,0},{2,3},{3,2},{4,5},{5,4},{6,7},{7,6},{8,9},{9,8},{10,11... | collective-permute-start | bytes 1572872 | tf_op jit(solution)/shard_map/ppermute | solution.py:460
  75.7 30.4 %collective-permute-start.5 = (bf16[4,512,128]{2,1,0:T(8,128)(2,1)}, bf16[4,512,128]{2,1,0:T(8,128)(2,1)S(1)}, u32[]{:S(2)}, u32[]{:S(2)}) collective-permute-start(bf16[4,512,128]{2,1,0:T(8,128)(2,1)} %get-tuple-element.29), channel_id=1, source_target_pairs={{2,0},{4,2},{6,4},{8,6},{10,8},{12,10},{14,12},{16,14},{18,16},{20... | collective-permute-start | bytes 1572872 | tf_op jit(solution)/shard_map/ppermute | solution.py:529
  77.0 29.1 %collective-permute-start.4 = (bf16[4,512,128]{2,1,0:T(8,128)(2,1)}, bf16[4,512,128]{2,1,0:T(8,128)(2,1)S(1)}, u32[]{:S(2)}, u32[]{:S(2)}) collective-permute-start(bf16[4,512,128]{2,1,0:T(8,128)(2,1)} %get-tuple-element.28), channel_id=1, source_target_pairs={{0,2},{2,4},{4,6},{6,8},{8,10},{10,12},{12,14},{14,16},{16,18},{18... | collective-permute-start | bytes 1572872 | tf_op jit(solution)/shard_map/ppermute | solution.py:529
  81.1 21.8 %all-to-all-start.1 = ((f32[64,1,128]{2,1,0:T(1,128)}), f32[64,1,128]{2,1,0:T(1,128)S(1)}, u32[]{:S(2)}, u32[]{:S(2)}) async-start(f32[64,1,128]{2,1,0:T(1,128)} %bitcast.5), calls=%async_computation.1 | async-start | bytes 65536 | tf_op jit(solution)/shard_map/all_to_all | solution.py:530
  90.9 16.2 %collective-permute-start.6 = (bf16[8,16,128]{2,1,0:T(8,128)(2,1)S(1)}, bf16[8,16,128]{2,1,0:T(8,128)(2,1)S(1)}, u32[]{:S(2)}, u32[]{:S(2)}) collective-permute-start(bf16[8,16,128]{2,1,0:T(8,128)(2,1)S(1)} %get-tuple-element.30), channel_id=1, source_target_pairs={{0,1},{1,0},{2,3},{3,2},{4,5},{5,4},{6,7},{7,6},{8,9},{9,8},{10,11... | collective-permute-start | bytes 98312 | tf_op jit(solution)/shard_map/ppermute | solution.py:460
  102.8 4.3 %collective-permute-start.8 = (f32[64,128]{1,0:T(8,128)S(1)}, f32[64,128]{1,0:T(8,128)S(1)}, u32[]{:S(2)}, u32[]{:S(2)}) collective-permute-start(f32[64,128]{1,0:T(8,128)S(1)} %bitcast.14), channel_id=1, source_target_pairs={{0,1},{1,0},{2,3},{3,2},{4,5},{5,4},{6,7},{7,6},{8,9},{9,8},{10,11... | collective-permute-start | bytes 98312 | tf_op jit(solution)/shard_map/ppermute | solution.py:460
  106.1 1.4 copy-start.3
  106.1 1.4 copy-start.4
  106.1 0.7 copy-start.5
  106.1 0.8 copy-start.6
  106.2 1.3 collective-permute-start.7
  107.0 26.2 %collective-permute-start.3 = (bf16[4,512,128]{2,1,0:T(8,128)(2,1)}, bf16[4,512,128]{2,1,0:T(8,128)(2,1)S(1)}, u32[]{:S(2)}, u32[]{:S(2)}) collective-permute-start(bf16[4,512,128]{2,1,0:T(8,128)(2,1)} %get-tuple-element.26), channel_id=1, source_target_pairs={{0,1},{1,0},{2,3},{3,2},{4,5},{5,4},{6,7},{7,6},{8,9},{9,8},{10,11... | collective-permute-start | bytes 1572872 | tf_op jit(solution)/shard_map/ppermute | solution.py:460
  113.1 21.0 %collective-permute-start.9 = (bf16[4,512,128]{2,1,0:T(8,128)(2,1)}, bf16[4,512,128]{2,1,0:T(8,128)(2,1)S(1)}, u32[]{:S(2)}, u32[]{:S(2)}) collective-permute-start(bf16[4,512,128]{2,1,0:T(8,128)(2,1)} %get-tuple-element.33), channel_id=1, source_target_pairs={{0,1},{1,0},{2,3},{3,2},{4,5},{5,4},{6,7},{7,6},{8,9},{9,8},{10,11... | collective-permute-start | bytes 1572872 | tf_op jit(solution)/shard_map/ppermute | solution.py:460
  131.4 2.7 %collective-permute-start.10 = (f32[64,128]{1,0:T(8,128)S(1)}, f32[64,128]{1,0:T(8,128)S(1)}, u32[]{:S(2)}, u32[]{:S(2)}) collective-permute-start(f32[64,128]{1,0:T(8,128)S(1)} %bitcast.16), channel_id=1, source_target_pairs={{0,1},{1,0},{2,3},{3,2},{4,5},{5,4},{6,7},{7,6},{8,9},{9,8},{10,11... | collective-permute-start | bytes 98312 | tf_op jit(solution)/shard_map/ppermute | solution.py:460
  193.1 5.0 %collective-permute-start.11 = (bf16[32,4,16,128]{3,2,1,0:T(8,128)(2,1)S(1)}, bf16[32,4,16,128]{3,2,1,0:T(8,128)(2,1)S(1)}, u32[]{:S(2)}, u32[]{:S(2)}) collective-permute-start(bf16[32,4,16,128]{3,2,1,0:T(8,128)(2,1)S(1)} %slice_select_fusion), channel_id=1, source_target_pairs={{0,1},{1,0},{2,3},{3,2},{4,5},{5,4},{6,7},{7,6},{8,9},{9,8},{10,11... | collective-permute-start | bytes 1572872 | tf_op jit(solution)/shard_map/ppermute | solution.py:460

commit v4 on v3

--- a/solution.py
+++ b/solution.py
@@ -18,9 +18,8 @@
 epsilon = 1e-05
 
 
-def chain(count, step):
-    pairs = [(i, i + 1) for i in range(count - 1)]
-    return pairs if step > 0 else [(b, a) for a, b in pairs]
+def pairs_of(count, first):
+    return [p for i in range(first, count - 1, 2) for p in ((i, i + 1), (i + 1, i))]
 
 
 def call(kernel, outs, scratch, n_copies, flops, operands):
@@ -197,13 +196,15 @@
 
 
 def prepare_kernel(
-    pair, feats, w_row, w_col, top, bottom, col_terms, row_terms, feats_in, row_in, col_in, sem
+    pair, feats, w_row, w_col, one, two, col_terms, row_terms, feats_in, row_in, col_in, sem
 ):
+    odd = lax.rem(lax.axis_index(GX), 2)
     channels = pair.shape[0]
+    lower, upper = pl.multiple_of(STEP * (1 - odd), STEP), pl.multiple_of(STEP * odd, STEP)
     parts = start_all(
         sem, 0,
-        ((pair.at[:, :STEP], top.at[pl.ds(0, channels)]),
-         (pair.at[:, STEP:], bottom.at[pl.ds(0, channels)])),
+        ((pair.at[:, pl.ds(lower, STEP)], one.at[pl.ds(0, channels)]),
+         (pair.at[:, pl.ds(upper, STEP)], two.at[pl.ds(0, channels)])),
     )
     inputs = start_all(sem, 2, ((feats, feats_in), (w_row, row_in), (w_col, col_in)))
     wait_all(inputs)
@@ -213,24 +214,28 @@
     packed = halves(col[:STEP], col[STEP:]).astype(jnp.bfloat16)
     col_terms[...] = jnp.broadcast_to(packed[None], col_terms.shape)
     row_terms[...] = halves(row[:STEP], row[STEP:])
-    empty = jnp.zeros((STEP, top.shape[2] - LANES), jnp.float32)
-    for ref, rows in ((top, row[:STEP]), (bottom, row[STEP:])):
+    empty = jnp.zeros((STEP, one.shape[2] - LANES), jnp.float32)
+    for ref, which in ((one, odd), (two, 1 - odd)):
+        rows = jnp.where(which == 0, row[STEP:], row[:STEP])
         ref[channels] = jnp.concatenate([rows, empty], axis=1).astype(jnp.bfloat16)
     wait_all(parts)
 
 
 def first_kernel(
-    devices, own_in, above_in, below_in, side, terms, mine, taps_in,
-    own_out, conv_out, give_out, down_out, up_out, edge_ref, stats_ref,
-    x_own, x_near, conv_ref, p_ref, down_ref, up_ref, own, above, below, taps,
+    devices, own_in, one_in, two_in, side, terms, mine, taps_in,
+    own_out, conv_out, give_out, one_out, two_out, edge_ref, stats_ref,
+    x_own, x_near, conv_ref, p_ref, border_ref, own, halo, taps,
     own_flat, above_flat, below_flat, side_flat, col_terms, row_terms, sem,
 ):
     row_at, core = lax.axis_index(GX), lax.axis_index("gy")
     channels, rows, cols = own.shape
     half = STEP // 2
+    odd = lax.rem(row_at, 2)
     inputs = start_all(
-        sem, 0, ((own_in, own), (above_in, above), (below_in, below), (taps_in, taps))
-    )
+        sem, 0,
+        ((own_in, own), (one_in, halo.at[1 - odd]), (two_in, halo.at[odd]), (taps_in, taps)),
+    )
+    above, below = halo.at[0], halo.at[1]
 
     def put_terms(source, at):
         value = terms[source].astype(jnp.float32)
@@ -249,6 +254,7 @@
     row_terms[0] = mine[...].astype(jnp.bfloat16).astype(jnp.float32)
     mask = reach_mask(core)
     tall = rows + 2 * STEP
+    above_at, below_at = (STEP + rows) * (1 - odd), (STEP + rows) * odd
     widen(side, side_flat)
     inputs[0].wait()
     widen(own, own_flat)
@@ -268,7 +274,7 @@
     )
     fill_rows(
         x_near, ((above_flat, 0, STEP), (below_flat, 0, STEP)),
-        ((side_flat, 0, tall), (side_flat, STEP + rows, tall)),
+        ((side_flat, above_at, tall), (side_flat, below_at, tall)),
         row_terms.at[1], col_terms, inside_of(row_at, devices), core, mask,
     )
     inputs[3].wait()
@@ -280,13 +286,13 @@
             at = slice(first, first + LANES)
             one = conv_ref[i, at, :].astype(jnp.float32)
             two = conv_ref[i + half, at, :].astype(jnp.float32)
-            up_ref[i, at, :] = jnp.where(lower, one, pltpu.roll(two, LANES // 2, 1)).astype(
-                jnp.bfloat16
-            )
-            down_ref[i, at, :] = jnp.where(lower, pltpu.roll(one, LANES // 2, 1), two).astype(
-                jnp.bfloat16
-            )
-    outputs += start_all(sem, 7, ((down_ref, down_out), (up_ref, up_out)))
+            up = jnp.where(lower, one, pltpu.roll(two, LANES // 2, 1))
+            down = jnp.where(lower, pltpu.roll(one, LANES // 2, 1), two)
+            border_ref[0, i, at, :] = up.astype(jnp.bfloat16)
+            border_ref[1, i, at, :] = down.astype(jnp.bfloat16)
+    outputs += start_all(
+        sem, 7, ((border_ref.at[1 - odd], one_out), (border_ref.at[odd], two_out))
+    )
     edge_at = pl.multiple_of((cols - 2 * STEP) * (1 - core), 2 * STEP)
     edge_ref[...] = conv_ref[:, pl.ds(edge_at, 2 * STEP), :]
     stats_ref[...] = jnp.broadcast_to(stats, stats_ref.shape)
@@ -294,15 +300,17 @@
 
 
 def second_kernel(
-    devices, cells, own_in, above_in, below_in, edge, corner, stats, stats_other, gains, taps_in,
+    devices, cells, own_in, one_in, two_in, edge, corner, stats, stats_other, gains, taps_in,
     conv_out, give_out, stats_ref,
-    a_own, a_near, conv_ref, p_ref, own, above, below, taps, sem,
+    a_own, a_near, conv_ref, p_ref, own, halo, taps, sem,
 ):
     row_at, core = lax.axis_index(GX), lax.axis_index("gy")
     cols = own.shape[1]
     half = STEP // 2
+    odd = lax.rem(row_at, 2)
     inputs = start_all(
-        sem, 0, ((own_in, own), (above_in, above), (below_in, below), (taps_in, taps))
+        sem, 0,
+        ((own_in, own), (one_in, halo.at[1 - odd]), (two_in, halo.at[odd]), (taps_in, taps)),
     )
     factor, offset = affine_of(0, (stats, stats_other), gains, cells)
     inside = inside_of(row_at, devices)
@@ -330,9 +338,9 @@
     def fill_near(i, _):
         for first in range(0, cols, LANES):
             at = slice(first, first + LANES)
-            for k, value in enumerate(two_rows(above[i, at, :], below[i, at, :])):
+            for k, value in enumerate(two_rows(halo[0, i, at, :], halo[1, i, at, :])):
                 a_near[i + half * k, at, :] = (activated(value) * inside).astype(jnp.bfloat16)
-        for k, value in enumerate(two_rows(corner[0, i], corner[1, i])):
+        for k, value in enumerate(two_rows(corner[1 - odd, i], corner[odd, i])):
             beyond = jnp.where(mask, activated(value) * inside, 0.0)
             a_near[i + half * k, cols:, :] = beyond.astype(jnp.bfloat16)
         return 0
@@ -459,10 +467,10 @@
     def swap(x):
         return lax.ppermute(x, "gy", SWAP)
 
-    down = functools.partial(lax.ppermute, axis_name=GX, perm=chain(devices, 1))
-    up = functools.partial(lax.ppermute, axis_name=GX, perm=chain(devices, -1))
+    with_next = functools.partial(lax.ppermute, axis_name=GX, perm=pairs_of(devices, 0))
+    with_last = functools.partial(lax.ppermute, axis_name=GX, perm=pairs_of(devices, 1))
     eight = (channels + 1, STEP, cols)
-    top, bottom, terms, mine = call(
+    one, two, terms, mine = call(
         prepare_kernel,
         (
             (VMEM, eight, bf16),
@@ -479,11 +487,13 @@
         conv_flops // 16,
         ((HBM, pair_feats), (HBM, residue_feats), (HBM, w_row.T), (HBM, w_col.T)),
     )
-    above, below = down(bottom), up(top)
+    one, two = with_next(one), with_last(two)
     terms = lax.all_to_all(terms, GX, 0, 0, tiled=True)
     gains = jnp.tile(jnp.concatenate([norm_scale, norm_shift], axis=0), (1, 2))
     near_side = swap(
-        jnp.concatenate([edge(above[:channels]), edge(pair_feats), edge(below[:channels])], axis=1)
+        jnp.concatenate(
+            [edge(one[:channels]), edge(pair_feats), edge(two[:channels])], axis=1
+        )
     )
 
     taps_shape = VMEM(first_taps.shape, bf16)
@@ -492,7 +502,7 @@
     wide = (STEP, cols + 2 * STEP, LANES)
     products = VMEM((2, cols + 2 * STEP, 3 * LANES), f32)
     sums = (devices, LANES)
-    own_rows, conv_own, own_give, conv_down, conv_up, edges, stats = call(
+    own_rows, conv_own, own_give, conv_one, conv_two, edges, stats = call(
         functools.partial(first_kernel, devices),
         (
             (HBM, whole, bf16),
@@ -508,11 +518,9 @@
             VMEM(wide, bf16),
             VMEM(whole, bf16),
             products,
-            VMEM(part, bf16),
-            VMEM(part, bf16),
+            VMEM((2, *part), bf16),
             VMEM(pair_feats.shape, bf16),
-            VMEM(eight, bf16),
-            VMEM(eight, bf16),
+            VMEM((2, *eight), bf16),
             taps_shape,
             flat_of(channels, rows, cols),
             flat_of(channels, STEP, cols),
@@ -523,17 +531,20 @@
         ],
         9,
         conv_flops,
-        ((HBM, pair_feats), (HBM, above), (HBM, below), (VMEM, near_side), (VMEM, terms),
+        ((HBM, pair_feats), (HBM, one), (HBM, two), (VMEM, near_side), (VMEM, terms),
          (VMEM, mine), (HBM, first_taps)),
     )
-    conv_above, conv_below = down(conv_down), up(conv_up)
+    conv_one, conv_two = with_next(conv_one), with_last(conv_two)
     stats = lax.all_to_all(stats, GX, 0, 0, tiled=True)
     stats_other = swap(stats)
     edges = swap(edges)
     last = cols - 2 * STEP
     corners = swap(
         jnp.stack(
-            [jnp.where(first_core, x[:, last:], x[:, : 2 * STEP]) for x in (conv_above, conv_below)]
+            [
+                jnp.where(first_core, x[:, last:], x[:, : 2 * STEP])
+                for x in (conv_one, conv_two)
+            ]
         )
     )
     own_other = swap(own_give)
@@ -546,13 +557,12 @@
             VMEM(whole, bf16),
             products,
             VMEM(whole, bf16),
-            VMEM(part, bf16),
-            VMEM(part, bf16),
+            VMEM((2, *part), bf16),
             taps_shape,
         ],
         4,
         conv_flops,
-        ((HBM, conv_own), (HBM, conv_above), (HBM, conv_below), (VMEM, edges),
+        ((HBM, conv_own), (HBM, conv_one), (HBM, conv_two), (VMEM, edges),
          (VMEM, corners), (VMEM, stats), (VMEM, stats_other), (VMEM, gains),
          (HBM, second_taps)),
     )

time: 203 us -> 200 us (0.985)
  starting transfers between devices: 53.3 us -> 48.9 us
    ppermute x8, starting transfers between devices: 30.9 us -> 27 us  [swap(): return lax.ppermute(x, 'gy', SWAP)]
  transfers between devices with their start and end apart: 13 -> 13, of which waited for: 6 -> 5; matrix products, arithmetic and copies ran while one was open for 0% -> 0% of each run, Pallas kernels for 3% -> 3%
where the time goes in v4:
time: 200 us; the launch traced here: 199 us
  blocking collectives  104 us (52%)
  starting transfers between devices  48.9 us (24%)
  Pallas kernels  25 us (12%)
  waiting for transfers between devices  19.1 us (10%)
    all_to_all x1, blocking collectives, body(): received = lax.all_to_all(send, GX, 0, 0, tiled=True)  55.4 us
    all_to_all x1, blocking collectives, body(): terms = lax.all_to_all(terms, GX, 0, 0, tiled=True)  31.1 us
    ppermute x8, starting transfers between devices, swap(): return lax.ppermute(x, 'gy', SWAP)  27 us
    pallas_call x5, Pallas kernels, call(): pl.pallas_call(kernel, out_shape=[space(shape, dtype) for space, shape, d...  25 us
    all_to_all x1, blocking collectives, body(): stats = lax.all_to_all(stats, GX, 0, 0, tiled=True)  17.8 us
    all_to_all x1, starting transfers between devices, body(): stats = lax.all_to_all(stats, GX, 0, 0, tiled=True)  10.8 us
    all_to_all x1, waiting for transfers between devices, body(): stats = lax.all_to_all(stats, GX, 0, 0, tiled=True)  9.94 us
    ppermute x2, starting transfers between devices, body(): one, two = (with_next(one), with_last(two))  7.87 us
  transfers between devices with their start and end apart: 13, of which 5 were waited for; matrix products, arithmetic and copies ran while one was open for 0% of the time, Pallas kernels for 3%

profile of v4, /device:TPU:33, one launch (start us, length us, event | category | flops | bytes accessed | tf_op | source)
XLA Modules:
  0.0 199.3 jit_solution(1263226042441607998)
XLA Ops:
  0.0 1.4 shard_map.82
  1.5 0.7 collective-permute-start.1
  2.2 7.2 %collective-permute-start = (bf16[65,8,512]{2,1,0:T(8,128)(2,1)S(1)}, bf16[65,8,512]{2,1,0:T(8,128)(2,1)S(1)}, u32[]{:S(2)}, u32[]{:S(2)}) collective-permute-start(bf16[65,8,512]{2,1,0:T(8,128)(2,1)S(1)} %get-tuple-element.21), channel_id=1, source_target_pairs={{0,2},{2,0},{4,6},{6,4},{8,10},{10,8},{12,14},{14,12},{16,18},{18,... | collective-permute-start | bytes 1597448 | tf_op jit(solution)/shard_map/ppermute | solution.py:490
  9.4 6.6 %collective-permute-done.one_in = bf16[65,8,512]{2,1,0:T(8,128)(2,1)S(1)} collective-permute-done((bf16[65,8,512]{2,1,0:T(8,128)(2,1)S(1)}, bf16[65,8,512]{2,1,0:T(8,128)(2,1)S(1)}, u32[]{:S(2)}, u32[]{:S(2)}) %collective-permute-start) | collective-permute-done | bytes 532512 | tf_op jit(solution)/shard_map/ppermute | solution.py:490
  16.1 0.7 copy-done.2
  16.8 16.0 %collective-permute-start.2 = (bf16[64,32,128]{2,1,0:T(8,128)(2,1)S(1)}, bf16[64,32,128]{2,1,0:T(8,128)(2,1)S(1)}, u32[]{:S(2)}, u32[]{:S(2)}) collective-permute-start(bf16[64,32,128]{2,1,0:T(8,128)(2,1)S(1)} %pad_maximum_fusion), channel_id=1, source_target_pairs={{0,1},{1,0},{2,3},{3,2},{4,5},{5,4},{6,7},{7,6},{8,9},{9,8},{10,11... | collective-permute-start | bytes 1572872 | tf_op jit(solution)/shard_map/ppermute | solution.py:468
  32.8 31.1 %all_to_all.32.terms = bf16[64,8,128]{2,1,0:T(8,128)(2,1)S(1)} all-to-all(bf16[64,8,128]{2,1,0:T(8,128)(2,1)S(1)} %get-tuple-element.23), channel_id=1, replica_groups=mesh['grp'=2,'gx_0'=4,'gx_1'=16,'gy'=2] {'gx_0','gx_1'}, dimensions={0} | all-to-all | bytes 262144 | tf_op jit(solution)/shard_map/all_to_all | solution.py:491
  63.9 9.8 %shard_map.83 = (bf16[8,512,128]{2,1,0:T(8,128)(2,1)}, bf16[8,512,128]{2,1,0:T(8,128)(2,1)}, bf16[4,512,128]{2,1,0:T(8,128)(2,1)}, bf16[4,512,128]{2,1,0:T(8,128...) custom-call(bf16[64,16,512]{2,1,0:T(8,128)(2,1)} %own_in.1, ...), custom_call_target="tpu_custom_call" | custom-call | flops 603979776 | bytes 1048576 | tf_op jit(solution)/shard_map/pallas_call | solution.py:28
  73.7 0.7 collective-permute-start.5
  74.4 2.6 %collective-permute-start.4 = (bf16[4,512,128]{2,1,0:T(8,128)(2,1)}, bf16[4,512,128]{2,1,0:T(8,128)(2,1)S(1)}, u32[]{:S(2)}, u32[]{:S(2)}) collective-permute-start(bf16[4,512,128]{2,1,0:T(8,128)(2,1)} %get-tuple-element.28), channel_id=1, source_target_pairs={{0,2},{2,0},{4,6},{6,4},{8,10},{10,8},{12,14},{14,12},{16,18},{18,... | collective-permute-start | bytes 1572872 | tf_op jit(solution)/shard_map/ppermute | solution.py:537
  77.0 10.8 %all-to-all-start.1 = ((f32[64,1,128]{2,1,0:T(1,128)}), f32[64,1,128]{2,1,0:T(1,128)S(1)}, u32[]{:S(2)}, u32[]{:S(2)}) async-start(f32[64,1,128]{2,1,0:T(1,128)} %bitcast.5), calls=%async_computation.1 | async-start | bytes 65536 | tf_op jit(solution)/shard_map/all_to_all | solution.py:538
  87.8 2.0 collective-permute-start.6
  89.8 9.9 %all-to-all-done.1 = f32[64,1,128]{2,1,0:T(1,128)S(1)} async-done(((f32[64,1,128]{2,1,0:T(1,128)}), f32[64,1,128]{2,1,0:T(1,128)S(1)}, u32[]{:S(2)}, u32[]{:S(2)}) %all-to-all-start.1) | async-done | bytes 32800 | tf_op jit(solution)/shard_map/all_to_all | solution.py:538
  99.7 3.0 %collective-permute-start.8 = (f32[64,128]{1,0:T(8,128)S(1)}, f32[64,128]{1,0:T(8,128)S(1)}, u32[]{:S(2)}, u32[]{:S(2)}) collective-permute-start(f32[64,128]{1,0:T(8,128)S(1)} %bitcast.14), channel_id=1, source_target_pairs={{0,1},{1,0},{2,3},{3,2},{4,5},{5,4},{6,7},{7,6},{8,9},{9,8},{10,11... | collective-permute-start | bytes 98312 | tf_op jit(solution)/shard_map/ppermute | solution.py:468
  103.0 0.5 copy-done.5
  104.2 5.6 %shard_map.84 = (bf16[8,512,128]{2,1,0:T(8,128)(2,1)}, bf16[4,512,128]{2,1,0:T(8,128)(2,1)}, f32[64,128]{1,0:T(8,128)S(1)}) custom-call(bf16[8,512,128]{2,1,0:T(8,128)(2,1)} %get-tuple-element.27.own_in, bf16[4,512,128]{2,1,0:T(8,128)(2,1)} %copy-done.4, bf16[4,512,128]{2,1,0:T(8,128)(2,1)} %copy-done.3, ...), custom_call_target="tpu_custom_call" | custom-call | flops 603979776 | bytes 1048576 | tf_op jit(solution)/shard_map/pallas_call | solution.py:28
  110.2 17.8 %all_to_all.33 = f32[64,1,128]{2,1,0:T(1,128)S(1)} all-to-all(f32[64,1,128]{2,1,0:T(1,128)S(1)} %bitcast.18), channel_id=1, replica_groups=mesh['grp'=2,'gx_0'=4,'gx_1'=16,'gy'=2] {'gx_0','gx_1'}, dimensions={0} | all-to-all | bytes 65536 | tf_op jit(solution)/shard_map/all_to_all | solution.py:569
  128.0 1.8 collective-permute-start.10
  129.8 0.9 collective-permute-done.10.stats_other
  130.7 3.4 %shard_map.85 = (bf16[8,512,128]{2,1,0:T(8,128)(2,1)}, bf16[64,4,16,128]{3,2,1,0:T(8,128)(2,1)S(1)}) custom-call(bf16[8,512,128]{2,1,0:T(8,128)(2,1)} %get-tuple-element.25.block_in, bf16[4,512,128]{2,1,0:T(8,128)(2,1)S(1)} %collective-permute-done.3.other, bf16[8,512,128]{2,1,0:T(8,128)(2,1)} %get-tuple-element.32.conv_in, ...), custom_call_target="tpu_custom_call" | custom-call | flops 603979776 | bytes 1048576 | tf_op jit(solution)/shard_map/pallas_call | solution.py:28
  134.1 55.4 %all_to_all.34.received = bf16[64,4,16,128]{3,2,1,0:T(8,128)(2,1)S(1)} all-to-all(bf16[64,4,16,128]{3,2,1,0:T(8,128)(2,1)S(1)} %get-tuple-element.36), channel_id=1, replica_groups=mesh['grp'=2,'gx_0'=4,'gx_1'=16,'gy'=2] {'gx_0','gx_1'}, dimensions={0} | all-to-all | bytes 2097152 | tf_op jit(solution)/shard_map/all_to_all | solution.py:585
  189.6 3.4 %collective-permute-start.11 = (bf16[32,4,16,128]{3,2,1,0:T(8,128)(2,1)S(1)}, bf16[32,4,16,128]{3,2,1,0:T(8,128)(2,1)S(1)}, u32[]{:S(2)}, u32[]{:S(2)}) collective-permute-start(bf16[32,4,16,128]{3,2,1,0:T(8,128)(2,1)S(1)} %slice_select_fusion), channel_id=1, source_target_pairs={{0,1},{1,0},{2,3},{3,2},{4,5},{5,4},{6,7},{7,6},{8,9},{9,8},{10,11... | collective-permute-start | bytes 1572872 | tf_op jit(solution)/shard_map/ppermute | solution.py:468
  193.0 1.5 collective-permute-done.11.other
  194.5 4.6 %shard_map.86 = bf16[64,16,512]{2,1,0:T(8,128)(2,1)} custom-call(bf16[8,512,128]{2,1,0:T(8,128)(2,1)} %get-tuple-element.35.own_in, bf16[64,4,16,128]{3,2,1,0:T(8,128)(2,1)S(1)} %all_to_all.34.received, bf16[32,4,16,128]{3,2,1,0:T(8,128)(2,1)S(1)} %collective-permute-done.11.other), custom_call_target="tpu_custom_call" | custom-call | flops 603979776 | bytes 1048576 | tf_op jit(solution)/shard_map/pallas_call | solution.py:28
  (35 shorter events, 1.4 us)
Async XLA Ops:
  0.0 9.3 %copy-start = (bf16[64,16,512]{2,1,0:T(8,128)(2,1)S(1)}, bf16[64,16,512]{2,1,0:T(8,128)(2,1)}, u32[]{:S(2)}) copy-start(bf16[64,16,512]{2,1,0:T(8,128)(2,1)} %own_in.1) | copy-start | bytes 3145732
  1.5 7.9 %collective-permute-start.1 = (bf16[65,8,512]{2,1,0:T(8,128)(2,1)S(1)}, bf16[65,8,512]{2,1,0:T(8,128)(2,1)S(1)}, u32[]{:S(2)}, u32[]{:S(2)}) collective-permute-start(bf16[65,8,512]{2,1,0:T(8,128)(2,1)S(1)} %get-tuple-element.22), channel_id=1, source_target_pairs={{2,4},{4,2},{6,8},{8,6},{10,12},{12,10},{14,16},{16,14},{18,20},{2... | collective-permute-start | bytes 1597448 | tf_op jit(solution)/shard_map/ppermute | solution.py:490
  2.2 13.8 %collective-permute-start = (bf16[65,8,512]{2,1,0:T(8,128)(2,1)S(1)}, bf16[65,8,512]{2,1,0:T(8,128)(2,1)S(1)}, u32[]{:S(2)}, u32[]{:S(2)}) collective-permute-start(bf16[65,8,512]{2,1,0:T(8,128)(2,1)S(1)} %get-tuple-element.21), channel_id=1, source_target_pairs={{0,2},{2,0},{4,6},{6,4},{8,10},{10,8},{12,14},{14,12},{16,18},{18,... | collective-permute-start | bytes 1597448 | tf_op jit(solution)/shard_map/ppermute | solution.py:490
  9.4 6.7 %copy-start.1 = (bf16[65,8,512]{2,1,0:T(8,128)(2,1)}, bf16[65,8,512]{2,1,0:T(8,128)(2,1)S(1)}, u32[]{:S(2)}) copy-start(bf16[65,8,512]{2,1,0:T(8,128)(2,1)S(1)} %collective-permute-done.1.two_in) | copy-start | bytes 1597444
  16.0 0.8 copy-start.2
  16.8 47.1 %collective-permute-start.2 = (bf16[64,32,128]{2,1,0:T(8,128)(2,1)S(1)}, bf16[64,32,128]{2,1,0:T(8,128)(2,1)S(1)}, u32[]{:S(2)}, u32[]{:S(2)}) collective-permute-start(bf16[64,32,128]{2,1,0:T(8,128)(2,1)S(1)} %pad_maximum_fusion), channel_id=1, source_target_pairs={{0,1},{1,0},{2,3},{3,2},{4,5},{5,4},{6,7},{7,6},{8,9},{9,8},{10,11... | collective-permute-start | bytes 1572872 | tf_op jit(solution)/shard_map/ppermute | solution.py:468
  73.7 29.0 %collective-permute-start.5 = (bf16[4,512,128]{2,1,0:T(8,128)(2,1)}, bf16[4,512,128]{2,1,0:T(8,128)(2,1)S(1)}, u32[]{:S(2)}, u32[]{:S(2)}) collective-permute-start(bf16[4,512,128]{2,1,0:T(8,128)(2,1)} %get-tuple-element.29), channel_id=1, source_target_pairs={{2,4},{4,2},{6,8},{8,6},{10,12},{12,10},{14,16},{16,14},{18,20},{2... | collective-permute-start | bytes 1572872 | tf_op jit(solution)/shard_map/ppermute | solution.py:537
  74.4 28.3 %collective-permute-start.4 = (bf16[4,512,128]{2,1,0:T(8,128)(2,1)}, bf16[4,512,128]{2,1,0:T(8,128)(2,1)S(1)}, u32[]{:S(2)}, u32[]{:S(2)}) collective-permute-start(bf16[4,512,128]{2,1,0:T(8,128)(2,1)} %get-tuple-element.28), channel_id=1, source_target_pairs={{0,2},{2,0},{4,6},{6,4},{8,10},{10,8},{12,14},{14,12},{16,18},{18,... | collective-permute-start | bytes 1572872 | tf_op jit(solution)/shard_map/ppermute | solution.py:537
  77.0 22.7 %all-to-all-start.1 = ((f32[64,1,128]{2,1,0:T(1,128)}), f32[64,1,128]{2,1,0:T(1,128)S(1)}, u32[]{:S(2)}, u32[]{:S(2)}) async-start(f32[64,1,128]{2,1,0:T(1,128)} %bitcast.5), calls=%async_computation.1 | async-start | bytes 65536 | tf_op jit(solution)/shard_map/all_to_all | solution.py:538
  87.8 16.1 %collective-permute-start.6 = (bf16[8,16,128]{2,1,0:T(8,128)(2,1)S(1)}, bf16[8,16,128]{2,1,0:T(8,128)(2,1)S(1)}, u32[]{:S(2)}, u32[]{:S(2)}) collective-permute-start(bf16[8,16,128]{2,1,0:T(8,128)(2,1)S(1)} %get-tuple-element.30), channel_id=1, source_target_pairs={{0,1},{1,0},{2,3},{3,2},{4,5},{5,4},{6,7},{7,6},{8,9},{9,8},{10,11... | collective-permute-start | bytes 98312 | tf_op jit(solution)/shard_map/ppermute | solution.py:468
  99.7 4.2 %collective-permute-start.8 = (f32[64,128]{1,0:T(8,128)S(1)}, f32[64,128]{1,0:T(8,128)S(1)}, u32[]{:S(2)}, u32[]{:S(2)}) collective-permute-start(f32[64,128]{1,0:T(8,128)S(1)} %bitcast.14), channel_id=1, source_target_pairs={{0,1},{1,0},{2,3},{3,2},{4,5},{5,4},{6,7},{7,6},{8,9},{9,8},{10,11... | collective-permute-start | bytes 98312 | tf_op jit(solution)/shard_map/ppermute | solution.py:468
  102.8 1.4 copy-start.3
  102.8 1.4 copy-start.4
  102.8 0.7 copy-start.5
  102.8 0.8 copy-start.6
  102.8 1.3 collective-permute-start.7
  103.7 26.1 %collective-permute-start.3 = (bf16[4,512,128]{2,1,0:T(8,128)(2,1)}, bf16[4,512,128]{2,1,0:T(8,128)(2,1)S(1)}, u32[]{:S(2)}, u32[]{:S(2)}) collective-permute-start(bf16[4,512,128]{2,1,0:T(8,128)(2,1)} %get-tuple-element.26), channel_id=1, source_target_pairs={{0,1},{1,0},{2,3},{3,2},{4,5},{5,4},{6,7},{7,6},{8,9},{9,8},{10,11... | collective-permute-start | bytes 1572872 | tf_op jit(solution)/shard_map/ppermute | solution.py:468
  109.8 20.9 %collective-permute-start.9 = (bf16[4,512,128]{2,1,0:T(8,128)(2,1)}, bf16[4,512,128]{2,1,0:T(8,128)(2,1)S(1)}, u32[]{:S(2)}, u32[]{:S(2)}) collective-permute-start(bf16[4,512,128]{2,1,0:T(8,128)(2,1)} %get-tuple-element.33), channel_id=1, source_target_pairs={{0,1},{1,0},{2,3},{3,2},{4,5},{5,4},{6,7},{7,6},{8,9},{9,8},{10,11... | collective-permute-start | bytes 1572872 | tf_op jit(solution)/shard_map/ppermute | solution.py:468
  128.0 2.7 %collective-permute-start.10 = (f32[64,128]{1,0:T(8,128)S(1)}, f32[64,128]{1,0:T(8,128)S(1)}, u32[]{:S(2)}, u32[]{:S(2)}) collective-permute-start(f32[64,128]{1,0:T(8,128)S(1)} %bitcast.16), channel_id=1, source_target_pairs={{0,1},{1,0},{2,3},{3,2},{4,5},{5,4},{6,7},{7,6},{8,9},{9,8},{10,11... | collective-permute-start | bytes 98312 | tf_op jit(solution)/shard_map/ppermute | solution.py:468
  189.6 5.0 %collective-permute-start.11 = (bf16[32,4,16,128]{3,2,1,0:T(8,128)(2,1)S(1)}, bf16[32,4,16,128]{3,2,1,0:T(8,128)(2,1)S(1)}, u32[]{:S(2)}, u32[]{:S(2)}) collective-permute-start(bf16[32,4,16,128]{3,2,1,0:T(8,128)(2,1)S(1)} %slice_select_fusion), channel_id=1, source_target_pairs={{0,1},{1,0},{2,3},{3,2},{4,5},{5,4},{6,7},{7,6},{8,9},{9,8},{10,11... | collective-permute-start | bytes 1572872 | tf_op jit(solution)/shard_map/ppermute | solution.py:468

commit v5 on v4

--- a/solution.py
+++ b/solution.py
@@ -97,30 +97,41 @@
     lax.fori_loop(0, channels // some, step, 0)
 
 
-def fill_rows(x_ref, sources, side_sources, row_terms, col_terms, scale, core, mask):
-    cols = col_terms.shape[0] - 2 * STEP
+def two_rows_turned(sources, block, i):
     channels = LANES // 2
-
-    def pair(sources, block, i):
-        return jnp.transpose(
-            jnp.concatenate(
-                [
-                    flat[block, pl.ds(first + i, channels, stride=rows), :]
-                    for flat, first, rows in sources
-                ],
-                axis=0,
-            )
+    return jnp.transpose(
+        jnp.concatenate(
+            [
+                flat[block, pl.ds(first + i, channels, stride=rows), :]
+                for flat, first, rows in sources
+            ],
+            axis=0,
         )
+    )
+
+
+def turn_rows(out_ref, sources):
+    def step(i, _):
+        for block in range(out_ref.shape[1] // LANES):
+            at = slice(block * LANES, (block + 1) * LANES)
+            out_ref[i, at, :] = two_rows_turned(sources, block, i).astype(jnp.bfloat16)
+        return 0
+
+    lax.fori_loop(0, STEP, step, 0)
+
+
+def add_terms(x_ref, raw_ref, side_sources, row_terms, col_terms, scale, core, mask):
+    cols = raw_ref.shape[1]
 
     def step(i, _):
         row = row_terms[pl.ds(i, 1), :]
         for block in range(cols // LANES):
             at = slice(block * LANES, (block + 1) * LANES)
-            value = pair(sources, block, i) + (row + col_terms[at, :])
+            value = raw_ref[i, at, :].astype(jnp.float32) + (row + col_terms[at, :])
             if scale is not None:
                 value = value * scale
             x_ref[i, at, :] = value.astype(jnp.bfloat16)
-        side = pair(side_sources, 0, i)
+        side = two_rows_turned(side_sources, 0, i)
         value = jnp.where(core == 0, side[: 2 * STEP], side[LANES - 2 * STEP :])
         value = value + (row + col_terms[cols:, :])
         if scale is not None:
@@ -221,21 +232,45 @@
     wait_all(parts)
 
 
+def turn_kernel(
+    pair, one, two, own_ref, near_ref, row_terms, own, own_flat, above_flat, below_flat, sem
+):
+    odd = lax.rem(lax.axis_index(GX), 2)
+    channels, rows, _ = own.shape
+    inputs = start_all(sem, 0, ((pair, own),))
+    one_rows, two_rows = one.at[pl.ds(0, channels)], two.at[pl.ds(0, channels)]
+
+    @pl.when(odd == 0)
+    def _():
+        widen(two_rows, above_flat)
+        widen(one_rows, below_flat)
+
+    @pl.when(odd == 1)
+    def _():
+        widen(one_rows, above_flat)
+        widen(two_rows, below_flat)
+
+    one_terms = one[channels, :, :LANES].astype(jnp.float32)
+    two_terms = two[channels, :, :LANES].astype(jnp.float32)
+    row_terms[...] = halves(
+        jnp.where(odd == 1, one_terms, two_terms), jnp.where(odd == 1, two_terms, one_terms)
+    )
+    turn_rows(near_ref, ((above_flat, 0, STEP), (below_flat, 0, STEP)))
+    wait_all(inputs)
+    widen(own, own_flat)
+    turn_rows(own_ref, ((own_flat, 0, rows), (own_flat, STEP, rows)))
+
+
 def first_kernel(
-    devices, own_in, one_in, two_in, side, terms, mine, taps_in,
-    own_out, conv_out, give_out, one_out, two_out, edge_ref, stats_ref,
-    x_own, x_near, conv_ref, p_ref, border_ref, own, halo, taps,
-    own_flat, above_flat, below_flat, side_flat, col_terms, row_terms, sem,
+    devices, own_raw, near_raw, near_terms, side, terms, mine, taps_in,
+    own_out, conv_out, give_out, one_ref, two_ref, edge_ref, stats_ref,
+    x_own, x_near, conv_ref, p_ref, taps, side_flat, col_terms, row_terms, sem,
 ):
     row_at, core = lax.axis_index(GX), lax.axis_index("gy")
-    channels, rows, cols = own.shape
-    half = STEP // 2
+    cols = own_raw.shape[1]
+    rows, half = 2 * STEP, STEP // 2
     odd = lax.rem(row_at, 2)
-    inputs = start_all(
-        sem, 0,
-        ((own_in, own), (one_in, halo.at[1 - odd]), (two_in, halo.at[odd]), (taps_in, taps)),
-    )
-    above, below = halo.at[0], halo.at[1]
+    inputs = start_all(sem, 0, ((taps_in, taps),))
 
     def put_terms(source, at):
         value = terms[source].astype(jnp.float32)
@@ -251,67 +286,50 @@
 
     lax.fori_loop(0, peers, put_own, 0)
     put_terms(peers - core, cols)
-    row_terms[0] = mine[...].astype(jnp.bfloat16).astype(jnp.float32)
+    row_terms[...] = mine[...].astype(jnp.bfloat16).astype(jnp.float32)
     mask = reach_mask(core)
     tall = rows + 2 * STEP
     above_at, below_at = (STEP + rows) * (1 - odd), (STEP + rows) * odd
     widen(side, side_flat)
-    inputs[0].wait()
-    widen(own, own_flat)
-    fill_rows(
-        x_own, ((own_flat, 0, rows), (own_flat, STEP, rows)),
-        ((side_flat, STEP, tall), (side_flat, 2 * STEP, tall)),
-        row_terms.at[0], col_terms, None, core, mask,
+    add_terms(
+        x_own, own_raw, ((side_flat, STEP, tall), (side_flat, 2 * STEP, tall)),
+        row_terms, col_terms, None, core, mask,
     )
     given = x_own.at[pl.ds(half * (1 - core), half), pl.ds(0, cols)]
-    outputs = start_all(sem, 4, ((x_own.at[:, pl.ds(0, cols)], own_out), (given, give_out)))
-    wait_all(inputs[1:3])
-    widen(above.at[pl.ds(0, channels)], above_flat)
-    widen(below.at[pl.ds(0, channels)], below_flat)
-    row_terms[1] = halves(
-        above[channels, :, :LANES].astype(jnp.float32),
-        below[channels, :, :LANES].astype(jnp.float32),
-    )
-    fill_rows(
-        x_near, ((above_flat, 0, STEP), (below_flat, 0, STEP)),
-        ((side_flat, above_at, tall), (side_flat, below_at, tall)),
-        row_terms.at[1], col_terms, inside_of(row_at, devices), core, mask,
-    )
-    inputs[3].wait()
+    outputs = start_all(sem, 1, ((x_own.at[:, pl.ds(0, cols)], own_out), (given, give_out)))
+    add_terms(
+        x_near, near_raw, ((side_flat, above_at, tall), (side_flat, below_at, tall)),
+        near_terms, col_terms, inside_of(row_at, devices), core, mask,
+    )
+    wait_all(inputs)
     stats = conv_own_rows(x_own, x_near, weights_of(taps, OWN_TAPS), p_ref, conv_ref)
-    outputs += start_all(sem, 6, ((conv_ref, conv_out),))
+    stats_ref[...] = jnp.broadcast_to(stats, stats_ref.shape)
+    outputs += start_all(sem, 3, ((conv_ref, conv_out),))
     lower = lane_half(LANES)
     for i in range(half):
         for first in range(0, cols, LANES):
             at = slice(first, first + LANES)
-            one = conv_ref[i, at, :].astype(jnp.float32)
-            two = conv_ref[i + half, at, :].astype(jnp.float32)
-            up = jnp.where(lower, one, pltpu.roll(two, LANES // 2, 1))
-            down = jnp.where(lower, pltpu.roll(one, LANES // 2, 1), two)
-            border_ref[0, i, at, :] = up.astype(jnp.bfloat16)
-            border_ref[1, i, at, :] = down.astype(jnp.bfloat16)
-    outputs += start_all(
-        sem, 7, ((border_ref.at[1 - odd], one_out), (border_ref.at[odd], two_out))
-    )
+            upper_one = conv_ref[i, at, :].astype(jnp.float32)
+            upper_two = conv_ref[i + half, at, :].astype(jnp.float32)
+            up = jnp.where(lower, upper_one, pltpu.roll(upper_two, LANES // 2, 1))
+            down = jnp.where(lower, pltpu.roll(upper_one, LANES // 2, 1), upper_two)
+            one_ref[i, at, :] = jnp.where(odd == 1, up, down).astype(jnp.bfloat16)
+            two_ref[i, at, :] = jnp.where(odd == 1, down, up).astype(jnp.bfloat16)
     edge_at = pl.multiple_of((cols - 2 * STEP) * (1 - core), 2 * STEP)
     edge_ref[...] = conv_ref[:, pl.ds(edge_at, 2 * STEP), :]
-    stats_ref[...] = jnp.broadcast_to(stats, stats_ref.shape)
     wait_all(outputs)
 
 
 def second_kernel(
-    devices, cells, own_in, one_in, two_in, edge, corner, stats, stats_other, gains, taps_in,
+    devices, cells, own_in, one, two, edge, corner, stats, stats_other, gains, taps_in,
     conv_out, give_out, stats_ref,
-    a_own, a_near, conv_ref, p_ref, own, halo, taps, sem,
+    a_own, a_near, conv_ref, p_ref, own, taps, sem,
 ):
     row_at, core = lax.axis_index(GX), lax.axis_index("gy")
     cols = own.shape[1]
     half = STEP // 2
     odd = lax.rem(row_at, 2)
-    inputs = start_all(
-        sem, 0,
-        ((own_in, own), (one_in, halo.at[1 - odd]), (two_in, halo.at[odd]), (taps_in, taps)),
-    )
+    inputs = start_all(sem, 0, ((own_in, own), (taps_in, taps)))
     factor, offset = affine_of(0, (stats, stats_other), gains, cells)
     inside = inside_of(row_at, devices)
     mask = reach_mask(core)
@@ -327,8 +345,9 @@
         a_own[i, cols:, :] = beyond.astype(jnp.bfloat16)
         return 0
 
-    def two_rows(up, down):
-        up, down = up.astype(jnp.float32), down.astype(jnp.float32)
+    def two_rows(one, two):
+        one, two = one.astype(jnp.float32), two.astype(jnp.float32)
+        up, down = jnp.where(odd == 1, one, two), jnp.where(odd == 1, two, one)
         lower = lane_half(up.shape[0])
         return (
             jnp.where(lower, up, pltpu.roll(down, LANES // 2, 1)),
@@ -338,17 +357,16 @@
     def fill_near(i, _):
         for first in range(0, cols, LANES):
             at = slice(first, first + LANES)
-            for k, value in enumerate(two_rows(halo[0, i, at, :], halo[1, i, at, :])):
+            for k, value in enumerate(two_rows(one[i, at, :], two[i, at, :])):
                 a_near[i + half * k, at, :] = (activated(value) * inside).astype(jnp.bfloat16)
-        for k, value in enumerate(two_rows(corner[1 - odd, i], corner[odd, i])):
+        for k, value in enumerate(two_rows(corner[0, i], corner[1, i])):
             beyond = jnp.where(mask, activated(value) * inside, 0.0)
             a_near[i + half * k, cols:, :] = beyond.astype(jnp.bfloat16)
         return 0
 
-    inputs[0].wait()
+    lax.fori_loop(0, half, fill_near, 0)
+    wait_all(inputs)
     lax.fori_loop(0, STEP, fill_own, 0)
-    wait_all(inputs[1:])
-    lax.fori_loop(0, half, fill_near, 0)
     stats = conv_own_rows(a_own, a_near, weights_of(taps, OWN_TAPS), p_ref, conv_ref)
     given = conv_ref.at[pl.ds(half * (1 - core), half)]
     outputs = start_all(sem, 0, ((given, give_out), (conv_ref, conv_out)))
@@ -502,14 +520,27 @@
     wide = (STEP, cols + 2 * STEP, LANES)
     products = VMEM((2, cols + 2 * STEP, 3 * LANES), f32)
     sums = (devices, LANES)
+    own_raw, near_raw, near_terms = call(
+        turn_kernel,
+        ((VMEM, whole, bf16), (VMEM, whole, bf16), (VMEM, (STEP, LANES), f32)),
+        [
+            VMEM(pair_feats.shape, bf16),
+            flat_of(channels, rows, cols),
+            flat_of(channels, STEP, cols),
+            flat_of(channels, STEP, cols),
+        ],
+        1,
+        conv_flops,
+        ((HBM, pair_feats), (VMEM, one), (VMEM, two)),
+    )
     own_rows, conv_own, own_give, conv_one, conv_two, edges, stats = call(
         functools.partial(first_kernel, devices),
         (
             (HBM, whole, bf16),
             (HBM, whole, bf16),
             (HBM, part, bf16),
-            (HBM, part, bf16),
-            (HBM, part, bf16),
+            (VMEM, part, bf16),
+            (VMEM, part, bf16),
             (VMEM, (STEP, 2 * STEP, LANES), bf16),
             (VMEM, sums, f32),
         ),
@@ -518,21 +549,15 @@
             VMEM(wide, bf16),
             VMEM(whole, bf16),
             products,
-            VMEM((2, *part), bf16),
-            VMEM(pair_feats.shape, bf16),
-            VMEM((2, *eight), bf16),
             taps_shape,
-            flat_of(channels, rows, cols),
-            flat_of(channels, STEP, cols),
-            flat_of(channels, STEP, cols),
             flat_of(channels, rows + 2 * STEP, LANES),
             VMEM(wide[1:], f32),
-            VMEM((2, STEP, LANES), f32),
+            VMEM((STEP, LANES), f32),
         ],
-        9,
+        4,
         conv_flops,
-        ((HBM, pair_feats), (HBM, one), (HBM, two), (VMEM, near_side), (VMEM, terms),
-         (VMEM, mine), (HBM, first_taps)),
+        ((VMEM, own_raw), (VMEM, near_raw), (VMEM, near_terms), (VMEM, near_side),
+         (VMEM, terms), (VMEM, mine), (HBM, first_taps)),
     )
     conv_one, conv_two = with_next(conv_one), with_last(conv_two)
     stats = lax.all_to_all(stats, GX, 0, 0, tiled=True)
@@ -557,12 +582,11 @@
             VMEM(whole, bf16),
             products,
             VMEM(whole, bf16),
-            VMEM((2, *part), bf16),
             taps_shape,
         ],
-        4,
+        2,
         conv_flops,
-        ((HBM, conv_own), (HBM, conv_one), (HBM, conv_two), (VMEM, edges),
+        ((HBM, conv_own), (VMEM, conv_one), (VMEM, conv_two), (VMEM, edges),
          (VMEM, corners), (VMEM, stats), (VMEM, stats_other), (VMEM, gains),
          (HBM, second_taps)),
     )

time: 200 us -> 198 us (0.990)
  blocking collectives: 104 us -> 73.2 us
  starting transfers between devices: 48.9 us -> 66.5 us
  waiting for transfers between devices: 19.1 us -> 28.7 us
    all_to_all x1 -> x0, blocking collectives: 31.1 us -> none  [body(): terms = lax.all_to_all(terms, GX, 0, 0, tiled=True)]
    all_to_all x0 -> x1, starting transfers between devices: none -> 17.7 us  [body(): terms = lax.all_to_all(terms, GX, 0, 0, tiled=True)]
    all_to_all x0 -> x1, waiting for transfers between devices: none -> 9.41 us  [body(): terms = lax.all_to_all(terms, GX, 0, 0, tiled=True)]
    pallas_call x5 -> x6, Pallas kernels: 25 us -> 25.6 us  [call(): pl.pallas_call(kernel, out_shape=[space(shape, dtype) for space, shape, d...]
  transfers between devices with their start and end apart: 13 -> 14, of which waited for: 5 -> 6; matrix products, arithmetic and copies ran while one was open for 0% -> 0% of each run, Pallas kernels for 3% -> 4%
where the time goes in v5:
time: 198 us; the launch traced here: 197 us
  blocking collectives  73.2 us (37%)
  starting transfers between devices  66.5 us (34%)
  waiting for transfers between devices  28.7 us (14%)
  Pallas kernels  25.6 us (13%)
    all_to_all x1, blocking collectives, body(): received = lax.all_to_all(send, GX, 0, 0, tiled=True)  55.5 us
    ppermute x8, starting transfers between devices, swap(): return lax.ppermute(x, 'gy', SWAP)  26.9 us
    pallas_call x6, Pallas kernels, call(): pl.pallas_call(kernel, out_shape=[space(shape, dtype) for space, shape, d...  25.6 us
    all_to_all x1, blocking collectives, body(): stats = lax.all_to_all(stats, GX, 0, 0, tiled=True)  17.7 us
    all_to_all x1, starting transfers between devices, body(): terms = lax.all_to_all(terms, GX, 0, 0, tiled=True)  17.7 us
    all_to_all x1, starting transfers between devices, body(): stats = lax.all_to_all(stats, GX, 0, 0, tiled=True)  10.8 us
    all_to_all x1, waiting for transfers between devices, body(): stats = lax.all_to_all(stats, GX, 0, 0, tiled=True)  10 us
    all_to_all x1, waiting for transfers between devices, body(): terms = lax.all_to_all(terms, GX, 0, 0, tiled=True)  9.41 us
  transfers between devices with their start and end apart: 14, of which 6 were waited for; matrix products, arithmetic and copies ran while one was open for 0% of the time, Pallas kernels for 4%

profile of v5, /device:TPU:33, one launch (start us, length us, event | category | flops | bytes accessed | tf_op | source)
XLA Modules:
  0.0 197.1 jit_solution(5959804034690194140)
XLA Ops:
  0.0 2.1 %shard_map.82 = (bf16[65,8,512]{2,1,0:T(8,128)(2,1)S(1)}, bf16[65,8,512]{2,1,0:T(8,128)(2,1)S(1)}, bf16[64,8,128]{2,1,0:T(8,128)(2,1)}, f32[8,128]{1,0:T(8,128)S(1)}) custom-call(bf16[64,16,512]{2,1,0:T(8,128)(2,1)} %pair.3, bf16[16,256]{1,0:T(8,128)(2,1)} %feats.1, bf16[64,256]{1,0:T(8,128)(2,1)} %bitcast.19, bf16[64,256]{1,0:T(8,128)(2,1)} %bitcast.20), custom_call_target="tpu_custom_call" | custom-call | flops 37748736 | bytes 1048576 | tf_op jit(solution)/shard_map/pallas_call | solution.py:28
  2.8 7.2 %collective-permute-start = (bf16[65,8,512]{2,1,0:T(8,128)(2,1)S(1)}, bf16[65,8,512]{2,1,0:T(8,128)(2,1)S(1)}, u32[]{:S(2)}, u32[]{:S(2)}) collective-permute-start(bf16[65,8,512]{2,1,0:T(8,128)(2,1)S(1)} %get-tuple-element.24), channel_id=1, source_target_pairs={{0,2},{2,0},{4,6},{6,4},{8,10},{10,8},{12,14},{14,12},{16,18},{18,... | collective-permute-start | bytes 1597448 | tf_op jit(solution)/shard_map/ppermute | solution.py:508
  10.1 6.6 %collective-permute-done.one = bf16[65,8,512]{2,1,0:T(8,128)(2,1)S(1)} collective-permute-done((bf16[65,8,512]{2,1,0:T(8,128)(2,1)S(1)}, bf16[65,8,512]{2,1,0:T(8,128)(2,1)S(1)}, u32[]{:S(2)}, u32[]{:S(2)}) %collective-permute-start) | collective-permute-done | bytes 532512 | tf_op jit(solution)/shard_map/ppermute | solution.py:508
  16.7 1.0 pad_maximum_fusion
  17.6 16.0 %collective-permute-start.2 = (bf16[64,32,128]{2,1,0:T(8,128)(2,1)}, bf16[64,32,128]{2,1,0:T(8,128)(2,1)S(1)}, u32[]{:S(2)}, u32[]{:S(2)}) collective-permute-start(bf16[64,32,128]{2,1,0:T(8,128)(2,1)} %pad_maximum_fusion), channel_id=1, source_target_pairs={{0,1},{1,0},{2,3},{3,2},{4,5},{5,4},{6,7},{7,6},{8,9},{9,8},{10,11... | collective-permute-start | bytes 1572872 | tf_op jit(solution)/shard_map/ppermute | solution.py:486
  33.6 17.7 %all-to-all-start = ((bf16[64,8,128]{2,1,0:T(8,128)(2,1)}), bf16[64,8,128]{2,1,0:T(8,128)(2,1)S(1)}, u32[]{:S(2)}, u32[]{:S(2)}) async-start(bf16[64,8,128]{2,1,0:T(8,128)(2,1)} %get-tuple-element.29), calls=%async_computation | async-start | bytes 262144 | tf_op jit(solution)/shard_map/all_to_all | solution.py:509
  51.3 1.0 copy-done.1
  52.3 3.1 %shard_map.83 = (bf16[8,512,128]{2,1,0:T(8,128)(2,1)S(1)}, bf16[8,512,128]{2,1,0:T(8,128)(2,1)S(1)}, f32[8,128]{1,0:T(8,128)S(1)}) custom-call(bf16[64,16,512]{2,1,0:T(8,128)(2,1)} %pair.3, bf16[65,8,512]{2,1,0:T(8,128)(2,1)S(1)} %copy-done.1, bf16[65,8,512]{2,1,0:T(8,128)(2,1)S(1)} %collective-permute-done.1.two), custom_call_target="tpu_custom_call" | custom-call | flops 603979776 | bytes 1048576 | tf_op jit(solution)/shard_map/pallas_call | solution.py:28
  55.4 9.4 %all-to-all-done.terms = bf16[64,8,128]{2,1,0:T(8,128)(2,1)S(1)} async-done(((bf16[64,8,128]{2,1,0:T(8,128)(2,1)}), bf16[64,8,128]{2,1,0:T(8,128)(2,1)S(1)}, u32[]{:S(2)}, u32[]{:S(2)}) %all-to-all-start) | async-done | bytes 131104 | tf_op jit(solution)/shard_map/all_to_all | solution.py:509
  64.8 7.9 %shard_map.84 = (bf16[8,512,128]{2,1,0:T(8,128)(2,1)}, bf16[8,512,128]{2,1,0:T(8,128)(2,1)}, bf16[4,512,128]{2,1,0:T(8,128)(2,1)}, bf16[4,512,128]{2,1,0:T(8,128...) custom-call(bf16[8,512,128]{2,1,0:T(8,128)(2,1)S(1)} %get-tuple-element.26.own_raw, ...), custom_call_target="tpu_custom_call" | custom-call | flops 603979776 | bytes 1048576 | tf_op jit(solution)/shard_map/pallas_call | solution.py:28
  73.4 2.6 %collective-permute-start.4 = (bf16[4,512,128]{2,1,0:T(8,128)(2,1)S(1)}, bf16[4,512,128]{2,1,0:T(8,128)(2,1)S(1)}, u32[]{:S(2)}, u32[]{:S(2)}) collective-permute-start(bf16[4,512,128]{2,1,0:T(8,128)(2,1)S(1)} %get-tuple-element.34), channel_id=1, source_target_pairs={{0,2},{2,0},{4,6},{6,4},{8,10},{10,8},{12,14},{14,12},{16,18},{18,... | collective-permute-start | bytes 1572872 | tf_op jit(solution)/shard_map/ppermute | solution.py:562
  76.0 10.8 %all-to-all-start.1 = ((f32[64,1,128]{2,1,0:T(1,128)}), f32[64,1,128]{2,1,0:T(1,128)S(1)}, u32[]{:S(2)}, u32[]{:S(2)}) async-start(f32[64,1,128]{2,1,0:T(1,128)} %bitcast.5), calls=%async_computation.1 | async-start | bytes 65536 | tf_op jit(solution)/shard_map/all_to_all | solution.py:563
  86.8 1.9 collective-permute-start.6
  88.8 10.0 %all-to-all-done.1 = f32[64,1,128]{2,1,0:T(1,128)S(1)} async-done(((f32[64,1,128]{2,1,0:T(1,128)}), f32[64,1,128]{2,1,0:T(1,128)S(1)}, u32[]{:S(2)}, u32[]{:S(2)}) %all-to-all-start.1) | async-done | bytes 32800 | tf_op jit(solution)/shard_map/all_to_all | solution.py:563
  98.8 3.0 %collective-permute-start.8 = (f32[64,128]{1,0:T(8,128)S(1)}, f32[64,128]{1,0:T(8,128)S(1)}, u32[]{:S(2)}, u32[]{:S(2)}) collective-permute-start(f32[64,128]{1,0:T(8,128)S(1)} %bitcast.14), channel_id=1, source_target_pairs={{0,1},{1,0},{2,3},{3,2},{4,5},{5,4},{6,7},{7,6},{8,9},{9,8},{10,11... | collective-permute-start | bytes 98312 | tf_op jit(solution)/shard_map/ppermute | solution.py:486
  103.2 4.5 %shard_map.85 = (bf16[8,512,128]{2,1,0:T(8,128)(2,1)}, bf16[4,512,128]{2,1,0:T(8,128)(2,1)}, f32[64,128]{1,0:T(8,128)S(1)}) custom-call(bf16[8,512,128]{2,1,0:T(8,128)(2,1)} %get-tuple-element.33.own_in, bf16[4,512,128]{2,1,0:T(8,128)(2,1)S(1)} %collective-permute-done.4.one, bf16[4,512,128]{2,1,0:T(8,128)(2,1)S(1)} %collective-permute-done.5.two, ...), custom_call_target="tpu_custom_call" | custom-call | flops 603979776 | bytes 1048576 | tf_op jit(solution)/shard_map/pallas_call | solution.py:28
  107.9 17.7 %all_to_all.32 = f32[64,1,128]{2,1,0:T(1,128)S(1)} all-to-all(f32[64,1,128]{2,1,0:T(1,128)S(1)} %bitcast.18), channel_id=1, replica_groups=mesh['grp'=2,'gx_0'=4,'gx_1'=16,'gy'=2] {'gx_0','gx_1'}, dimensions={0} | all-to-all | bytes 65536 | tf_op jit(solution)/shard_map/all_to_all | solution.py:593
  125.6 1.8 collective-permute-start.10
  127.5 0.9 collective-permute-done.10.stats_other
  128.3 3.4 %shard_map.86 = (bf16[8,512,128]{2,1,0:T(8,128)(2,1)}, bf16[64,4,16,128]{3,2,1,0:T(8,128)(2,1)S(1)}) custom-call(bf16[8,512,128]{2,1,0:T(8,128)(2,1)} %get-tuple-element.31.block_in, bf16[4,512,128]{2,1,0:T(8,128)(2,1)S(1)} %collective-permute-done.3.other, bf16[8,512,128]{2,1,0:T(8,128)(2,1)} %get-tuple-element.38.conv_in, ...), custom_call_target="tpu_custom_call" | custom-call | flops 603979776 | bytes 1048576 | tf_op jit(solution)/shard_map/pallas_call | solution.py:28
  131.7 55.5 %all_to_all.33.received = bf16[64,4,16,128]{3,2,1,0:T(8,128)(2,1)S(1)} all-to-all(bf16[64,4,16,128]{3,2,1,0:T(8,128)(2,1)S(1)} %get-tuple-element.42), channel_id=1, replica_groups=mesh['grp'=2,'gx_0'=4,'gx_1'=16,'gy'=2] {'gx_0','gx_1'}, dimensions={0} | all-to-all | bytes 2097152 | tf_op jit(solution)/shard_map/all_to_all | solution.py:609
  187.3 3.5 %collective-permute-start.11 = (bf16[32,4,16,128]{3,2,1,0:T(8,128)(2,1)S(1)}, bf16[32,4,16,128]{3,2,1,0:T(8,128)(2,1)S(1)}, u32[]{:S(2)}, u32[]{:S(2)}) collective-permute-start(bf16[32,4,16,128]{3,2,1,0:T(8,128)(2,1)S(1)} %slice_select_fusion), channel_id=1, source_target_pairs={{0,1},{1,0},{2,3},{3,2},{4,5},{5,4},{6,7},{7,6},{8,9},{9,8},{10,11... | collective-permute-start | bytes 1572872 | tf_op jit(solution)/shard_map/ppermute | solution.py:486
  190.8 1.5 collective-permute-done.11.other
  192.3 4.6 %shard_map.87 = bf16[64,16,512]{2,1,0:T(8,128)(2,1)} custom-call(bf16[8,512,128]{2,1,0:T(8,128)(2,1)} %get-tuple-element.41.own_in, bf16[64,4,16,128]{3,2,1,0:T(8,128)(2,1)S(1)} %all_to_all.33.received, bf16[32,4,16,128]{3,2,1,0:T(8,128)(2,1)S(1)} %collective-permute-done.11.other), custom_call_target="tpu_custom_call" | custom-call | flops 603979776 | bytes 1048576 | tf_op jit(solution)/shard_map/pallas_call | solution.py:28
  (33 shorter events, 3.2 us)
Async XLA Ops:
  0.0 10.0 %copy-start.2 = (bf16[64,16,512]{2,1,0:T(8,128)(2,1)S(1)}, bf16[64,16,512]{2,1,0:T(8,128)(2,1)}, u32[]{:S(2)}) copy-start(bf16[64,16,512]{2,1,0:T(8,128)(2,1)} %pair.3) | copy-start | bytes 3145732
  2.1 7.9 %collective-permute-start.1 = (bf16[65,8,512]{2,1,0:T(8,128)(2,1)S(1)}, bf16[65,8,512]{2,1,0:T(8,128)(2,1)S(1)}, u32[]{:S(2)}, u32[]{:S(2)}) collective-permute-start(bf16[65,8,512]{2,1,0:T(8,128)(2,1)S(1)} %get-tuple-element.25), channel_id=1, source_target_pairs={{2,4},{4,2},{6,8},{8,6},{10,12},{12,10},{14,16},{16,14},{18,20},{2... | collective-permute-start | bytes 1597448 | tf_op jit(solution)/shard_map/ppermute | solution.py:508
  2.8 13.8 %collective-permute-start = (bf16[65,8,512]{2,1,0:T(8,128)(2,1)S(1)}, bf16[65,8,512]{2,1,0:T(8,128)(2,1)S(1)}, u32[]{:S(2)}, u32[]{:S(2)}) collective-permute-start(bf16[65,8,512]{2,1,0:T(8,128)(2,1)S(1)} %get-tuple-element.24), channel_id=1, source_target_pairs={{0,2},{2,0},{4,6},{6,4},{8,10},{10,8},{12,14},{14,12},{16,18},{18,... | collective-permute-start | bytes 1597448 | tf_op jit(solution)/shard_map/ppermute | solution.py:508
  16.7 1.0 copy-start
  17.6 47.2 %collective-permute-start.2 = (bf16[64,32,128]{2,1,0:T(8,128)(2,1)}, bf16[64,32,128]{2,1,0:T(8,128)(2,1)S(1)}, u32[]{:S(2)}, u32[]{:S(2)}) collective-permute-start(bf16[64,32,128]{2,1,0:T(8,128)(2,1)} %pad_maximum_fusion), channel_id=1, source_target_pairs={{0,1},{1,0},{2,3},{3,2},{4,5},{5,4},{6,7},{7,6},{8,9},{9,8},{10,11... | collective-permute-start | bytes 1572872 | tf_op jit(solution)/shard_map/ppermute | solution.py:486
  33.6 31.2 %all-to-all-start = ((bf16[64,8,128]{2,1,0:T(8,128)(2,1)}), bf16[64,8,128]{2,1,0:T(8,128)(2,1)S(1)}, u32[]{:S(2)}, u32[]{:S(2)}) async-start(bf16[64,8,128]{2,1,0:T(8,128)(2,1)} %get-tuple-element.29), calls=%async_computation | async-start | bytes 262144 | tf_op jit(solution)/shard_map/all_to_all | solution.py:509
  51.3 1.0 copy-start.1
  72.7 29.0 %collective-permute-start.5 = (bf16[4,512,128]{2,1,0:T(8,128)(2,1)}, bf16[4,512,128]{2,1,0:T(8,128)(2,1)S(1)}, u32[]{:S(2)}, u32[]{:S(2)}) collective-permute-start(bf16[4,512,128]{2,1,0:T(8,128)(2,1)} %get-tuple-element.35), channel_id=1, source_target_pairs={{2,4},{4,2},{6,8},{8,6},{10,12},{12,10},{14,16},{16,14},{18,20},{2... | collective-permute-start | bytes 1572872 | tf_op jit(solution)/shard_map/ppermute | solution.py:562
  73.4 28.4 %collective-permute-start.4 = (bf16[4,512,128]{2,1,0:T(8,128)(2,1)S(1)}, bf16[4,512,128]{2,1,0:T(8,128)(2,1)S(1)}, u32[]{:S(2)}, u32[]{:S(2)}) collective-permute-start(bf16[4,512,128]{2,1,0:T(8,128)(2,1)S(1)} %get-tuple-element.34), channel_id=1, source_target_pairs={{0,2},{2,0},{4,6},{6,4},{8,10},{10,8},{12,14},{14,12},{16,18},{18,... | collective-permute-start | bytes 1572872 | tf_op jit(solution)/shard_map/ppermute | solution.py:562
  76.0 22.8 %all-to-all-start.1 = ((f32[64,1,128]{2,1,0:T(1,128)}), f32[64,1,128]{2,1,0:T(1,128)S(1)}, u32[]{:S(2)}, u32[]{:S(2)}) async-start(f32[64,1,128]{2,1,0:T(1,128)} %bitcast.5), calls=%async_computation.1 | async-start | bytes 65536 | tf_op jit(solution)/shard_map/all_to_all | solution.py:563
  86.8 16.0 %collective-permute-start.6 = (bf16[8,16,128]{2,1,0:T(8,128)(2,1)S(1)}, bf16[8,16,128]{2,1,0:T(8,128)(2,1)S(1)}, u32[]{:S(2)}, u32[]{:S(2)}) collective-permute-start(bf16[8,16,128]{2,1,0:T(8,128)(2,1)S(1)} %get-tuple-element.36), channel_id=1, source_target_pairs={{0,1},{1,0},{2,3},{3,2},{4,5},{5,4},{6,7},{7,6},{8,9},{9,8},{10,11... | collective-permute-start | bytes 98312 | tf_op jit(solution)/shard_map/ppermute | solution.py:486
  98.8 4.1 %collective-permute-start.8 = (f32[64,128]{1,0:T(8,128)S(1)}, f32[64,128]{1,0:T(8,128)S(1)}, u32[]{:S(2)}, u32[]{:S(2)}) collective-permute-start(f32[64,128]{1,0:T(8,128)S(1)} %bitcast.14), channel_id=1, source_target_pairs={{0,1},{1,0},{2,3},{3,2},{4,5},{5,4},{6,7},{7,6},{8,9},{9,8},{10,11... | collective-permute-start | bytes 98312 | tf_op jit(solution)/shard_map/ppermute | solution.py:486
  101.8 0.7 copy-start.3
  101.8 0.7 copy-start.4
  101.8 1.3 collective-permute-start.7
  102.6 24.9 %collective-permute-start.3 = (bf16[4,512,128]{2,1,0:T(8,128)(2,1)}, bf16[4,512,128]{2,1,0:T(8,128)(2,1)S(1)}, u32[]{:S(2)}, u32[]{:S(2)}) collective-permute-start(bf16[4,512,128]{2,1,0:T(8,128)(2,1)} %get-tuple-element.32), channel_id=1, source_target_pairs={{0,1},{1,0},{2,3},{3,2},{4,5},{5,4},{6,7},{7,6},{8,9},{9,8},{10,11... | collective-permute-start | bytes 1572872 | tf_op jit(solution)/shard_map/ppermute | solution.py:486
  107.6 20.7 %collective-permute-start.9 = (bf16[4,512,128]{2,1,0:T(8,128)(2,1)}, bf16[4,512,128]{2,1,0:T(8,128)(2,1)S(1)}, u32[]{:S(2)}, u32[]{:S(2)}) collective-permute-start(bf16[4,512,128]{2,1,0:T(8,128)(2,1)} %get-tuple-element.39), channel_id=1, source_target_pairs={{0,1},{1,0},{2,3},{3,2},{4,5},{5,4},{6,7},{7,6},{8,9},{9,8},{10,11... | collective-permute-start | bytes 1572872 | tf_op jit(solution)/shard_map/ppermute | solution.py:486
  125.6 2.7 %collective-permute-start.10 = (f32[64,128]{1,0:T(8,128)S(1)}, f32[64,128]{1,0:T(8,128)S(1)}, u32[]{:S(2)}, u32[]{:S(2)}) collective-permute-start(f32[64,128]{1,0:T(8,128)S(1)} %bitcast.16), channel_id=1, source_target_pairs={{0,1},{1,0},{2,3},{3,2},{4,5},{5,4},{6,7},{7,6},{8,9},{9,8},{10,11... | collective-permute-start | bytes 98312 | tf_op jit(solution)/shard_map/ppermute | solution.py:486
  187.3 5.0 %collective-permute-start.11 = (bf16[32,4,16,128]{3,2,1,0:T(8,128)(2,1)S(1)}, bf16[32,4,16,128]{3,2,1,0:T(8,128)(2,1)S(1)}, u32[]{:S(2)}, u32[]{:S(2)}) collective-permute-start(bf16[32,4,16,128]{3,2,1,0:T(8,128)(2,1)S(1)} %slice_select_fusion), channel_id=1, source_target_pairs={{0,1},{1,0},{2,3},{3,2},{4,5},{5,4},{6,7},{7,6},{8,9},{9,8},{10,11... | collective-permute-start | bytes 1572872 | tf_op jit(solution)/shard_map/ppermute | solution.py:486

commit v6 on v5

--- a/solution.py
+++ b/solution.py
@@ -123,6 +123,14 @@
 def add_terms(x_ref, raw_ref, side_sources, row_terms, col_terms, scale, core, mask):
     cols = raw_ref.shape[1]
 
+    for i in range(STEP):
+        side = two_rows_turned(side_sources, 0, i)
+        value = jnp.where(core == 0, side[: 2 * STEP], side[LANES - 2 * STEP :])
+        value = value + (row_terms[i : i + 1] + col_terms[cols:, :])
+        if scale is not None:
+            value = value * scale
+        x_ref[i, cols:, :] = jnp.where(mask, value, 0.0).astype(jnp.bfloat16)
+
     def step(i, _):
         row = row_terms[pl.ds(i, 1), :]
         for block in range(cols // LANES):
@@ -131,12 +139,6 @@
             if scale is not None:
                 value = value * scale
             x_ref[i, at, :] = value.astype(jnp.bfloat16)
-        side = two_rows_turned(side_sources, 0, i)
-        value = jnp.where(core == 0, side[: 2 * STEP], side[LANES - 2 * STEP :])
-        value = value + (row + col_terms[cols:, :])
-        if scale is not None:
-            value = value * scale
-        x_ref[i, cols:, :] = jnp.where(mask, value, 0.0).astype(jnp.bfloat16)
         return 0
 
     lax.fori_loop(0, STEP, step, 0)
@@ -272,20 +274,15 @@
     odd = lax.rem(row_at, 2)
     inputs = start_all(sem, 0, ((taps_in, taps),))
 
-    def put_terms(source, at):
-        value = terms[source].astype(jnp.float32)
-        other = pltpu.roll(value, LANES // 2, 1)
-        col_terms[pl.ds(at, STEP), :] = jnp.where(lane_half(STEP), value, other)
-        col_terms[pl.ds(at + STEP, STEP), :] = jnp.where(lane_half(STEP), other, value)
+    def put_terms(sources):
+        values = [(at, terms[source].astype(jnp.float32)) for source, at in sources]
+        values = [(at, value, pltpu.roll(value, LANES // 2, 1)) for at, value in values]
+        for at, value, other in values:
+            col_terms[at : at + STEP] = jnp.where(lane_half(STEP), value, other)
+            col_terms[at + STEP : at + 2 * STEP] = jnp.where(lane_half(STEP), other, value)
 
     peers = cols // rows
-
-    def put_own(i, _):
-        put_terms(peers * core + i, pl.multiple_of(i * rows, 2 * STEP))
-        return 0
-
-    lax.fori_loop(0, peers, put_own, 0)
-    put_terms(peers - core, cols)
+    put_terms([(peers * core + i, i * rows) for i in range(peers)] + [(peers - core, cols)])
     row_terms[...] = mine[...].astype(jnp.bfloat16).astype(jnp.float32)
     mask = reach_mask(core)
     tall = rows + 2 * STEP
@@ -382,7 +379,14 @@
     core = lax.axis_index("gy")
     cols = conv.shape[1]
     half = STEP // 2
-    inputs = start_all(sem, 0, ((block_in, own), (conv_in, conv)))
+    parts = [
+        start_all(
+            sem, 2 * n,
+            [(src.at[pl.ds(2 * n, 2)], dst.at[pl.ds(2 * n, 2)])
+             for src, dst in ((block_in, own), (conv_in, conv))],
+        )
+        for n in range(STEP // 2)
+    ]
     factor, offset = affine_of(1, (stats, stats_other), gains, cells)
     wide = 2 * STEP
     peers, some = cols // wide, LANES // wide
@@ -397,9 +401,10 @@
             out_ref[i, at, :] = block_out(own[i, at, :], conv[i, at, :])
         return 0
 
-    wait_all(inputs[:2])
-    lax.fori_loop(0, STEP, mine, 0)
-    outputs = start_all(sem, 2, ((out_ref, block_out_out),))
+    for n, part in enumerate(parts):
+        wait_all(part)
+        lax.fori_loop(2 * n, 2 * n + 2, mine, 0)
+    outputs = start_all(sem, STEP, ((out_ref, block_out_out),))
 
     def step(i, _):
         for first in range(0, cols, LANES):
@@ -601,7 +606,7 @@
             VMEM(whole, bf16),
             VMEM(whole, bf16),
         ],
-        3,
+        STEP + 1,
         conv_flops,
         ((HBM, own_rows), (VMEM, own_other), (HBM, conv_second), (VMEM, conv_other),
          (VMEM, stats), (VMEM, stats_other), (VMEM, gains)),

time: 198 us -> 194 us (0.980)
  Pallas kernels: 25.6 us -> 22.1 us
    pallas_call x6, Pallas kernels: 25.6 us -> 22.1 us  [call(): pl.pallas_call(kernel, out_shape=[space(shape, dtype) for space, shape, d...]
where the time goes in v6:
time: 194 us
  blocking collectives  73.2 us (38%)
  starting transfers between devices  66.5 us (34%)
  waiting for transfers between devices  28.7 us (15%)
  Pallas kernels  22.1 us (11%)
    all_to_all x1, blocking collectives, body(): received = lax.all_to_all(send, GX, 0, 0, tiled=True)  55.5 us
    ppermute x8, starting transfers between devices, swap(): return lax.ppermute(x, 'gy', SWAP)  26.9 us
    pallas_call x6, Pallas kernels, call(): pl.pallas_call(kernel, out_shape=[space(shape, dtype) for space, shape, d...  22.1 us
    all_to_all x1, blocking collectives, body(): stats = lax.all_to_all(stats, GX, 0, 0, tiled=True)  17.7 us
    all_to_all x1, starting transfers between devices, body(): terms = lax.all_to_all(terms, GX, 0, 0, tiled=True)  17.7 us
    all_to_all x1, starting transfers between devices, body(): stats = lax.all_to_all(stats, GX, 0, 0, tiled=True)  10.8 us
    all_to_all x1, waiting for transfers between devices, body(): stats = lax.all_to_all(stats, GX, 0, 0, tiled=True)  9.98 us
    all_to_all x1, waiting for transfers between devices, body(): terms = lax.all_to_all(terms, GX, 0, 0, tiled=True)  9.41 us
  transfers between devices with their start and end apart: 14, of which 6 were waited for; matrix products, arithmetic and copies ran while one was open for 0% of the time, Pallas kernels for 4%

profile of v6, /device:TPU:33, one launch (start us, length us, event | category | flops | bytes accessed | tf_op | source)
XLA Modules:
  0.0 193.6 jit_solution(8584785228992572529)
XLA Ops:
  0.0 2.1 %shard_map.82 = (bf16[65,8,512]{2,1,0:T(8,128)(2,1)S(1)}, bf16[65,8,512]{2,1,0:T(8,128)(2,1)S(1)}, bf16[64,8,128]{2,1,0:T(8,128)(2,1)}, f32[8,128]{1,0:T(8,128)S(1)}) custom-call(bf16[64,16,512]{2,1,0:T(8,128)(2,1)} %pair.3, bf16[16,256]{1,0:T(8,128)(2,1)} %feats.1, bf16[64,256]{1,0:T(8,128)(2,1)} %bitcast.19, bf16[64,256]{1,0:T(8,128)(2,1)} %bitcast.20), custom_call_target="tpu_custom_call" | custom-call | flops 37748736 | bytes 1048576 | tf_op jit(solution)/shard_map/pallas_call | solution.py:28
  2.8 7.2 %collective-permute-start = (bf16[65,8,512]{2,1,0:T(8,128)(2,1)S(1)}, bf16[65,8,512]{2,1,0:T(8,128)(2,1)S(1)}, u32[]{:S(2)}, u32[]{:S(2)}) collective-permute-start(bf16[65,8,512]{2,1,0:T(8,128)(2,1)S(1)} %get-tuple-element.24), channel_id=1, source_target_pairs={{0,2},{2,0},{4,6},{6,4},{8,10},{10,8},{12,14},{14,12},{16,18},{18,... | collective-permute-start | bytes 1597448 | tf_op jit(solution)/shard_map/ppermute | solution.py:513
  10.1 6.6 %collective-permute-done.one = bf16[65,8,512]{2,1,0:T(8,128)(2,1)S(1)} collective-permute-done((bf16[65,8,512]{2,1,0:T(8,128)(2,1)S(1)}, bf16[65,8,512]{2,1,0:T(8,128)(2,1)S(1)}, u32[]{:S(2)}, u32[]{:S(2)}) %collective-permute-start) | collective-permute-done | bytes 532512 | tf_op jit(solution)/shard_map/ppermute | solution.py:513
  16.7 1.0 pad_maximum_fusion
  17.6 16.0 %collective-permute-start.2 = (bf16[64,32,128]{2,1,0:T(8,128)(2,1)}, bf16[64,32,128]{2,1,0:T(8,128)(2,1)S(1)}, u32[]{:S(2)}, u32[]{:S(2)}) collective-permute-start(bf16[64,32,128]{2,1,0:T(8,128)(2,1)} %pad_maximum_fusion), channel_id=1, source_target_pairs={{0,1},{1,0},{2,3},{3,2},{4,5},{5,4},{6,7},{7,6},{8,9},{9,8},{10,11... | collective-permute-start | bytes 1572872 | tf_op jit(solution)/shard_map/ppermute | solution.py:491
  33.6 17.7 %all-to-all-start = ((bf16[64,8,128]{2,1,0:T(8,128)(2,1)}), bf16[64,8,128]{2,1,0:T(8,128)(2,1)S(1)}, u32[]{:S(2)}, u32[]{:S(2)}) async-start(bf16[64,8,128]{2,1,0:T(8,128)(2,1)} %get-tuple-element.29), calls=%async_computation | async-start | bytes 262144 | tf_op jit(solution)/shard_map/all_to_all | solution.py:514
  51.3 1.0 copy-done.1
  52.3 3.1 %shard_map.83 = (bf16[8,512,128]{2,1,0:T(8,128)(2,1)S(1)}, bf16[8,512,128]{2,1,0:T(8,128)(2,1)S(1)}, f32[8,128]{1,0:T(8,128)S(1)}) custom-call(bf16[64,16,512]{2,1,0:T(8,128)(2,1)} %pair.3, bf16[65,8,512]{2,1,0:T(8,128)(2,1)S(1)} %copy-done.1, bf16[65,8,512]{2,1,0:T(8,128)(2,1)S(1)} %collective-permute-done.1.two), custom_call_target="tpu_custom_call" | custom-call | flops 603979776 | bytes 1048576 | tf_op jit(solution)/shard_map/pallas_call | solution.py:28
  55.4 9.4 %all-to-all-done.terms = bf16[64,8,128]{2,1,0:T(8,128)(2,1)S(1)} async-done(((bf16[64,8,128]{2,1,0:T(8,128)(2,1)}), bf16[64,8,128]{2,1,0:T(8,128)(2,1)S(1)}, u32[]{:S(2)}, u32[]{:S(2)}) %all-to-all-start) | async-done | bytes 131104 | tf_op jit(solution)/shard_map/all_to_all | solution.py:514
  64.8 4.8 %shard_map.84 = (bf16[8,512,128]{2,1,0:T(8,128)(2,1)}, bf16[8,512,128]{2,1,0:T(8,128)(2,1)}, bf16[4,512,128]{2,1,0:T(8,128)(2,1)}, bf16[4,512,128]{2,1,0:T(8,128...) custom-call(bf16[8,512,128]{2,1,0:T(8,128)(2,1)S(1)} %get-tuple-element.26.own_raw, ...), custom_call_target="tpu_custom_call" | custom-call | flops 603979776 | bytes 1048576 | tf_op jit(solution)/shard_map/pallas_call | solution.py:28
  70.4 2.6 %collective-permute-start.4 = (bf16[4,512,128]{2,1,0:T(8,128)(2,1)S(1)}, bf16[4,512,128]{2,1,0:T(8,128)(2,1)S(1)}, u32[]{:S(2)}, u32[]{:S(2)}) collective-permute-start(bf16[4,512,128]{2,1,0:T(8,128)(2,1)S(1)} %get-tuple-element.34), channel_id=1, source_target_pairs={{0,2},{2,0},{4,6},{6,4},{8,10},{10,8},{12,14},{14,12},{16,18},{18,... | collective-permute-start | bytes 1572872 | tf_op jit(solution)/shard_map/ppermute | solution.py:567
  73.0 10.8 %all-to-all-start.1 = ((f32[64,1,128]{2,1,0:T(1,128)}), f32[64,1,128]{2,1,0:T(1,128)S(1)}, u32[]{:S(2)}, u32[]{:S(2)}) async-start(f32[64,1,128]{2,1,0:T(1,128)} %bitcast.5), calls=%async_computation.1 | async-start | bytes 65536 | tf_op jit(solution)/shard_map/all_to_all | solution.py:568
  83.8 2.0 %collective-permute-start.6 = (bf16[8,16,128]{2,1,0:T(8,128)(2,1)S(1)}, bf16[8,16,128]{2,1,0:T(8,128)(2,1)S(1)}, u32[]{:S(2)}, u32[]{:S(2)}) collective-permute-start(bf16[8,16,128]{2,1,0:T(8,128)(2,1)S(1)} %get-tuple-element.36), channel_id=1, source_target_pairs={{0,1},{1,0},{2,3},{3,2},{4,5},{5,4},{6,7},{7,6},{8,9},{9,8},{10,11... | collective-permute-start | bytes 98312 | tf_op jit(solution)/shard_map/ppermute | solution.py:491
  85.7 10.0 %all-to-all-done.1 = f32[64,1,128]{2,1,0:T(1,128)S(1)} async-done(((f32[64,1,128]{2,1,0:T(1,128)}), f32[64,1,128]{2,1,0:T(1,128)S(1)}, u32[]{:S(2)}, u32[]{:S(2)}) %all-to-all-start.1) | async-done | bytes 32800 | tf_op jit(solution)/shard_map/all_to_all | solution.py:568
  95.7 3.0 %collective-permute-start.8 = (f32[64,128]{1,0:T(8,128)S(1)}, f32[64,128]{1,0:T(8,128)S(1)}, u32[]{:S(2)}, u32[]{:S(2)}) collective-permute-start(f32[64,128]{1,0:T(8,128)S(1)} %bitcast.14), channel_id=1, source_target_pairs={{0,1},{1,0},{2,3},{3,2},{4,5},{5,4},{6,7},{7,6},{8,9},{9,8},{10,11... | collective-permute-start | bytes 98312 | tf_op jit(solution)/shard_map/ppermute | solution.py:491
  100.1 4.5 %shard_map.85 = (bf16[8,512,128]{2,1,0:T(8,128)(2,1)}, bf16[4,512,128]{2,1,0:T(8,128)(2,1)}, f32[64,128]{1,0:T(8,128)S(1)}) custom-call(bf16[8,512,128]{2,1,0:T(8,128)(2,1)} %get-tuple-element.33.own_in, bf16[4,512,128]{2,1,0:T(8,128)(2,1)S(1)} %collective-permute-done.4.one, bf16[4,512,128]{2,1,0:T(8,128)(2,1)S(1)} %collective-permute-done.5.two, ...), custom_call_target="tpu_custom_call" | custom-call | flops 603979776 | bytes 1048576 | tf_op jit(solution)/shard_map/pallas_call | solution.py:28
  104.9 17.7 %all_to_all.32 = f32[64,1,128]{2,1,0:T(1,128)S(1)} all-to-all(f32[64,1,128]{2,1,0:T(1,128)S(1)} %bitcast.18), channel_id=1, replica_groups=mesh['grp'=2,'gx_0'=4,'gx_1'=16,'gy'=2] {'gx_0','gx_1'}, dimensions={0} | all-to-all | bytes 65536 | tf_op jit(solution)/shard_map/all_to_all | solution.py:598
  122.6 1.8 collective-permute-start.10
  124.4 0.9 collective-permute-done.10.stats_other
  125.3 3.0 %shard_map.86 = (bf16[8,512,128]{2,1,0:T(8,128)(2,1)}, bf16[64,4,16,128]{3,2,1,0:T(8,128)(2,1)S(1)}) custom-call(bf16[8,512,128]{2,1,0:T(8,128)(2,1)} %get-tuple-element.31.block_in, bf16[4,512,128]{2,1,0:T(8,128)(2,1)S(1)} %collective-permute-done.3.other, bf16[8,512,128]{2,1,0:T(8,128)(2,1)} %get-tuple-element.38.conv_in, ...), custom_call_target="tpu_custom_call" | custom-call | flops 603979776 | bytes 1048576 | tf_op jit(solution)/shard_map/pallas_call | solution.py:28
  128.3 55.5 %all_to_all.33.received = bf16[64,4,16,128]{3,2,1,0:T(8,128)(2,1)S(1)} all-to-all(bf16[64,4,16,128]{3,2,1,0:T(8,128)(2,1)S(1)} %get-tuple-element.42), channel_id=1, replica_groups=mesh['grp'=2,'gx_0'=4,'gx_1'=16,'gy'=2] {'gx_0','gx_1'}, dimensions={0} | all-to-all | bytes 2097152 | tf_op jit(solution)/shard_map/all_to_all | solution.py:614
  183.8 3.5 %collective-permute-start.11 = (bf16[32,4,16,128]{3,2,1,0:T(8,128)(2,1)S(1)}, bf16[32,4,16,128]{3,2,1,0:T(8,128)(2,1)S(1)}, u32[]{:S(2)}, u32[]{:S(2)}) collective-permute-start(bf16[32,4,16,128]{3,2,1,0:T(8,128)(2,1)S(1)} %slice_select_fusion), channel_id=1, source_target_pairs={{0,1},{1,0},{2,3},{3,2},{4,5},{5,4},{6,7},{7,6},{8,9},{9,8},{10,11... | collective-permute-start | bytes 1572872 | tf_op jit(solution)/shard_map/ppermute | solution.py:491
  187.3 1.5 collective-permute-done.11.other
  188.8 4.6 %shard_map.87 = bf16[64,16,512]{2,1,0:T(8,128)(2,1)} custom-call(bf16[8,512,128]{2,1,0:T(8,128)(2,1)} %get-tuple-element.41.own_in, bf16[64,4,16,128]{3,2,1,0:T(8,128)(2,1)S(1)} %all_to_all.33.received, bf16[32,4,16,128]{3,2,1,0:T(8,128)(2,1)S(1)} %collective-permute-done.11.other), custom_call_target="tpu_custom_call" | custom-call | flops 603979776 | bytes 1048576 | tf_op jit(solution)/shard_map/pallas_call | solution.py:28
  (33 shorter events, 3.2 us)
Async XLA Ops:
  0.0 10.0 %copy-start.2 = (bf16[64,16,512]{2,1,0:T(8,128)(2,1)S(1)}, bf16[64,16,512]{2,1,0:T(8,128)(2,1)}, u32[]{:S(2)}) copy-start(bf16[64,16,512]{2,1,0:T(8,128)(2,1)} %pair.3) | copy-start | bytes 3145732
  2.1 7.9 %collective-permute-start.1 = (bf16[65,8,512]{2,1,0:T(8,128)(2,1)S(1)}, bf16[65,8,512]{2,1,0:T(8,128)(2,1)S(1)}, u32[]{:S(2)}, u32[]{:S(2)}) collective-permute-start(bf16[65,8,512]{2,1,0:T(8,128)(2,1)S(1)} %get-tuple-element.25), channel_id=1, source_target_pairs={{2,4},{4,2},{6,8},{8,6},{10,12},{12,10},{14,16},{16,14},{18,20},{2... | collective-permute-start | bytes 1597448 | tf_op jit(solution)/shard_map/ppermute | solution.py:513
  2.8 13.8 %collective-permute-start = (bf16[65,8,512]{2,1,0:T(8,128)(2,1)S(1)}, bf16[65,8,512]{2,1,0:T(8,128)(2,1)S(1)}, u32[]{:S(2)}, u32[]{:S(2)}) collective-permute-start(bf16[65,8,512]{2,1,0:T(8,128)(2,1)S(1)} %get-tuple-element.24), channel_id=1, source_target_pairs={{0,2},{2,0},{4,6},{6,4},{8,10},{10,8},{12,14},{14,12},{16,18},{18,... | collective-permute-start | bytes 1597448 | tf_op jit(solution)/shard_map/ppermute | solution.py:513
  16.7 1.0 copy-start
  17.6 47.2 %collective-permute-start.2 = (bf16[64,32,128]{2,1,0:T(8,128)(2,1)}, bf16[64,32,128]{2,1,0:T(8,128)(2,1)S(1)}, u32[]{:S(2)}, u32[]{:S(2)}) collective-permute-start(bf16[64,32,128]{2,1,0:T(8,128)(2,1)} %pad_maximum_fusion), channel_id=1, source_target_pairs={{0,1},{1,0},{2,3},{3,2},{4,5},{5,4},{6,7},{7,6},{8,9},{9,8},{10,11... | collective-permute-start | bytes 1572872 | tf_op jit(solution)/shard_map/ppermute | solution.py:491
  33.6 31.2 %all-to-all-start = ((bf16[64,8,128]{2,1,0:T(8,128)(2,1)}), bf16[64,8,128]{2,1,0:T(8,128)(2,1)S(1)}, u32[]{:S(2)}, u32[]{:S(2)}) async-start(bf16[64,8,128]{2,1,0:T(8,128)(2,1)} %get-tuple-element.29), calls=%async_computation | async-start | bytes 262144 | tf_op jit(solution)/shard_map/all_to_all | solution.py:514
  51.3 1.0 copy-start.1
  69.7 29.0 %collective-permute-start.5 = (bf16[4,512,128]{2,1,0:T(8,128)(2,1)}, bf16[4,512,128]{2,1,0:T(8,128)(2,1)S(1)}, u32[]{:S(2)}, u32[]{:S(2)}) collective-permute-start(bf16[4,512,128]{2,1,0:T(8,128)(2,1)} %get-tuple-element.35), channel_id=1, source_target_pairs={{2,4},{4,2},{6,8},{8,6},{10,12},{12,10},{14,16},{16,14},{18,20},{2... | collective-permute-start | bytes 1572872 | tf_op jit(solution)/shard_map/ppermute | solution.py:567
  70.4 28.4 %collective-permute-start.4 = (bf16[4,512,128]{2,1,0:T(8,128)(2,1)S(1)}, bf16[4,512,128]{2,1,0:T(8,128)(2,1)S(1)}, u32[]{:S(2)}, u32[]{:S(2)}) collective-permute-start(bf16[4,512,128]{2,1,0:T(8,128)(2,1)S(1)} %get-tuple-element.34), channel_id=1, source_target_pairs={{0,2},{2,0},{4,6},{6,4},{8,10},{10,8},{12,14},{14,12},{16,18},{18,... | collective-permute-start | bytes 1572872 | tf_op jit(solution)/shard_map/ppermute | solution.py:567
  73.0 22.7 %all-to-all-start.1 = ((f32[64,1,128]{2,1,0:T(1,128)}), f32[64,1,128]{2,1,0:T(1,128)S(1)}, u32[]{:S(2)}, u32[]{:S(2)}) async-start(f32[64,1,128]{2,1,0:T(1,128)} %bitcast.5), calls=%async_computation.1 | async-start | bytes 65536 | tf_op jit(solution)/shard_map/all_to_all | solution.py:568
  83.8 16.1 %collective-permute-start.6 = (bf16[8,16,128]{2,1,0:T(8,128)(2,1)S(1)}, bf16[8,16,128]{2,1,0:T(8,128)(2,1)S(1)}, u32[]{:S(2)}, u32[]{:S(2)}) collective-permute-start(bf16[8,16,128]{2,1,0:T(8,128)(2,1)S(1)} %get-tuple-element.36), channel_id=1, source_target_pairs={{0,1},{1,0},{2,3},{3,2},{4,5},{5,4},{6,7},{7,6},{8,9},{9,8},{10,11... | collective-permute-start | bytes 98312 | tf_op jit(solution)/shard_map/ppermute | solution.py:491
  95.7 4.1 %collective-permute-start.8 = (f32[64,128]{1,0:T(8,128)S(1)}, f32[64,128]{1,0:T(8,128)S(1)}, u32[]{:S(2)}, u32[]{:S(2)}) collective-permute-start(f32[64,128]{1,0:T(8,128)S(1)} %bitcast.14), channel_id=1, source_target_pairs={{0,1},{1,0},{2,3},{3,2},{4,5},{5,4},{6,7},{7,6},{8,9},{9,8},{10,11... | collective-permute-start | bytes 98312 | tf_op jit(solution)/shard_map/ppermute | solution.py:491
  98.8 0.7 copy-start.3
  98.8 0.7 copy-start.4
  98.8 1.3 collective-permute-start.7
  99.6 24.9 %collective-permute-start.3 = (bf16[4,512,128]{2,1,0:T(8,128)(2,1)}, bf16[4,512,128]{2,1,0:T(8,128)(2,1)S(1)}, u32[]{:S(2)}, u32[]{:S(2)}) collective-permute-start(bf16[4,512,128]{2,1,0:T(8,128)(2,1)} %get-tuple-element.32), channel_id=1, source_target_pairs={{0,1},{1,0},{2,3},{3,2},{4,5},{5,4},{6,7},{7,6},{8,9},{9,8},{10,11... | collective-permute-start | bytes 1572872 | tf_op jit(solution)/shard_map/ppermute | solution.py:491
  104.6 20.7 %collective-permute-start.9 = (bf16[4,512,128]{2,1,0:T(8,128)(2,1)}, bf16[4,512,128]{2,1,0:T(8,128)(2,1)S(1)}, u32[]{:S(2)}, u32[]{:S(2)}) collective-permute-start(bf16[4,512,128]{2,1,0:T(8,128)(2,1)} %get-tuple-element.39), channel_id=1, source_target_pairs={{0,1},{1,0},{2,3},{3,2},{4,5},{5,4},{6,7},{7,6},{8,9},{9,8},{10,11... | collective-permute-start | bytes 1572872 | tf_op jit(solution)/shard_map/ppermute | solution.py:491
  122.6 2.7 %collective-permute-start.10 = (f32[64,128]{1,0:T(8,128)S(1)}, f32[64,128]{1,0:T(8,128)S(1)}, u32[]{:S(2)}, u32[]{:S(2)}) collective-permute-start(f32[64,128]{1,0:T(8,128)S(1)} %bitcast.16), channel_id=1, source_target_pairs={{0,1},{1,0},{2,3},{3,2},{4,5},{5,4},{6,7},{7,6},{8,9},{9,8},{10,11... | collective-permute-start | bytes 98312 | tf_op jit(solution)/shard_map/ppermute | solution.py:491
  183.8 5.0 %collective-permute-start.11 = (bf16[32,4,16,128]{3,2,1,0:T(8,128)(2,1)S(1)}, bf16[32,4,16,128]{3,2,1,0:T(8,128)(2,1)S(1)}, u32[]{:S(2)}, u32[]{:S(2)}) collective-permute-start(bf16[32,4,16,128]{3,2,1,0:T(8,128)(2,1)S(1)} %slice_select_fusion), channel_id=1, source_target_pairs={{0,1},{1,0},{2,3},{3,2},{4,5},{5,4},{6,7},{7,6},{8,9},{9,8},{10,11... | collective-permute-start | bytes 1572872 | tf_op jit(solution)/shard_map/ppermute | solution.py:491

commit v7 on v6

--- a/solution.py
+++ b/solution.py
@@ -32,7 +32,7 @@
         out_specs=[pl.BlockSpec(memory_space=space) for space, _, _ in outs],
         scratch_shapes=[*scratch, pltpu.SemaphoreType.DMA((n_copies,))],
         cost_estimate=pl.CostEstimate(flops=flops, bytes_accessed=1 << 20, transcendentals=0),
-        compiler_params=pltpu.CompilerParams(vmem_limit_bytes=24 << 20),
+        compiler_params=pltpu.CompilerParams(vmem_limit_bytes=12 << 20),
     )(*held)
 
 
@@ -356,10 +356,12 @@
             at = slice(first, first + LANES)
             for k, value in enumerate(two_rows(one[i, at, :], two[i, at, :])):
                 a_near[i + half * k, at, :] = (activated(value) * inside).astype(jnp.bfloat16)
+        return 0
+
+    for i in range(half):
         for k, value in enumerate(two_rows(corner[0, i], corner[1, i])):
             beyond = jnp.where(mask, activated(value) * inside, 0.0)
             a_near[i + half * k, cols:, :] = beyond.astype(jnp.bfloat16)
-        return 0
 
     lax.fori_loop(0, half, fill_near, 0)
     wait_all(inputs)
@@ -436,7 +438,7 @@
     some = LANES // rows
     lower = lane_half(some * STEP)
 
-    def step(i, _):
+    def step(i):
         for block in range(cols // LANES):
             first = block * some * STEP * rows
             upper_row = flat[pl.ds(first + i, some * STEP, stride=rows), :]
@@ -457,21 +459,26 @@
                 flat_ref[block, pl.ds(high * STEP + i, channels, stride=rows), :] = value[
                     channels * high : channels * (high + 1)
                 ]
-        return 0
-
-    lax.fori_loop(0, STEP, step, 0)
-
-    def store(c, _):
+
+    for i in range(STEP):
+        step(i)
+
+    batch = 4
+
+    def store(n, _):
         for block in range(cols // LANES):
-            value = flat_ref[block, pl.ds(pl.multiple_of(c * rows, 8), rows), :]
-            out_ref[c, :, block * LANES : (block + 1) * LANES] = value.astype(jnp.bfloat16)
-        return 0
-
-    part = channels // 2
-    lax.fori_loop(0, part, store, 0)
-    outputs = start_all(sem, 1, ((out_ref.at[pl.ds(0, part)], result.at[pl.ds(0, part)]),))
-    lax.fori_loop(part, channels, store, 0)
-    outputs += start_all(sem, 2, ((out_ref.at[pl.ds(part, part)], result.at[pl.ds(part, part)]),))
+            value = flat_ref[block, pl.ds(pl.multiple_of(n * batch * rows, 8), batch * rows), :]
+            out_ref[pl.ds(n * batch, batch), :, block * LANES : (block + 1) * LANES] = value.reshape(
+                batch, rows, LANES
+            ).astype(jnp.bfloat16)
+        return 0
+
+    outputs = []
+    quarter = channels // 4
+    for n in range(4):
+        lax.fori_loop(n * quarter // batch, (n + 1) * quarter // batch, store, 0)
+        at = pl.ds(n * quarter, quarter)
+        outputs += start_all(sem, 1 + n, ((out_ref.at[at], result.at[at]),))
     wait_all(outputs)
 
 
@@ -623,7 +630,7 @@
             VMEM((peers, cores, STEP // 2, rows, LANES), f32),
             flat_of(channels, rows, cols),
         ],
-        3,
+        5,
         conv_flops,
         ((HBM, block_out), (VMEM, received), (VMEM, other)),
     )[0]

time: 194 us -> 193 us (level)
  no operation moved by 1% of the time
where the time goes in v7:
time: 193 us
  blocking collectives  73.2 us (38%)
  starting transfers between devices  66.5 us (34%)
  waiting for transfers between devices  28.7 us (15%)
  Pallas kernels  21.3 us (11%)
    all_to_all x1, blocking collectives, body(): received = lax.all_to_all(send, GX, 0, 0, tiled=True)  55.5 us
    ppermute x8, starting transfers between devices, swap(): return lax.ppermute(x, 'gy', SWAP)  26.9 us
    pallas_call x6, Pallas kernels, call(): pl.pallas_call(kernel, out_shape=[space(shape, dtype) for space, shape, d...  21.3 us
    all_to_all x1, blocking collectives, body(): stats = lax.all_to_all(stats, GX, 0, 0, tiled=True)  17.7 us
    all_to_all x1, starting transfers between devices, body(): terms = lax.all_to_all(terms, GX, 0, 0, tiled=True)  17.7 us
    all_to_all x1, starting transfers between devices, body(): stats = lax.all_to_all(stats, GX, 0, 0, tiled=True)  10.8 us
    all_to_all x1, waiting for transfers between devices, body(): stats = lax.all_to_all(stats, GX, 0, 0, tiled=True)  9.98 us
    all_to_all x1, waiting for transfers between devices, body(): terms = lax.all_to_all(terms, GX, 0, 0, tiled=True)  9.41 us
  transfers between devices with their start and end apart: 14, of which 6 were waited for; matrix products, arithmetic and copies ran while one was open for 0% of the time, Pallas kernels for 4%

profile of v7, /device:TPU:33, one launch (start us, length us, event | category | flops | bytes accessed | tf_op | source)
XLA Modules:
  0.0 192.8 jit_solution(17709611161964665906)
XLA Ops:
  0.0 2.1 %shard_map.82 = (bf16[65,8,512]{2,1,0:T(8,128)(2,1)S(1)}, bf16[65,8,512]{2,1,0:T(8,128)(2,1)S(1)}, bf16[64,8,128]{2,1,0:T(8,128)(2,1)}, f32[8,128]{1,0:T(8,128)S(1)}) custom-call(bf16[64,16,512]{2,1,0:T(8,128)(2,1)} %pair.3, bf16[16,256]{1,0:T(8,128)(2,1)} %feats.1, bf16[64,256]{1,0:T(8,128)(2,1)} %bitcast.19, bf16[64,256]{1,0:T(8,128)(2,1)} %bitcast.20), custom_call_target="tpu_custom_call" | custom-call | flops 37748736 | bytes 1048576 | tf_op jit(solution)/shard_map/pallas_call | solution.py:28
  2.8 7.2 %collective-permute-start = (bf16[65,8,512]{2,1,0:T(8,128)(2,1)S(1)}, bf16[65,8,512]{2,1,0:T(8,128)(2,1)S(1)}, u32[]{:S(2)}, u32[]{:S(2)}) collective-permute-start(bf16[65,8,512]{2,1,0:T(8,128)(2,1)S(1)} %get-tuple-element.24), channel_id=1, source_target_pairs={{0,2},{2,0},{4,6},{6,4},{8,10},{10,8},{12,14},{14,12},{16,18},{18,... | collective-permute-start | bytes 1597448 | tf_op jit(solution)/shard_map/ppermute | solution.py:520
  10.1 6.6 %collective-permute-done.one = bf16[65,8,512]{2,1,0:T(8,128)(2,1)S(1)} collective-permute-done((bf16[65,8,512]{2,1,0:T(8,128)(2,1)S(1)}, bf16[65,8,512]{2,1,0:T(8,128)(2,1)S(1)}, u32[]{:S(2)}, u32[]{:S(2)}) %collective-permute-start) | collective-permute-done | bytes 532512 | tf_op jit(solution)/shard_map/ppermute | solution.py:520
  16.7 1.0 pad_maximum_fusion
  17.6 16.0 %collective-permute-start.2 = (bf16[64,32,128]{2,1,0:T(8,128)(2,1)}, bf16[64,32,128]{2,1,0:T(8,128)(2,1)S(1)}, u32[]{:S(2)}, u32[]{:S(2)}) collective-permute-start(bf16[64,32,128]{2,1,0:T(8,128)(2,1)} %pad_maximum_fusion), channel_id=1, source_target_pairs={{0,1},{1,0},{2,3},{3,2},{4,5},{5,4},{6,7},{7,6},{8,9},{9,8},{10,11... | collective-permute-start | bytes 1572872 | tf_op jit(solution)/shard_map/ppermute | solution.py:498
  33.6 17.7 %all-to-all-start = ((bf16[64,8,128]{2,1,0:T(8,128)(2,1)}), bf16[64,8,128]{2,1,0:T(8,128)(2,1)S(1)}, u32[]{:S(2)}, u32[]{:S(2)}) async-start(bf16[64,8,128]{2,1,0:T(8,128)(2,1)} %get-tuple-element.29), calls=%async_computation | async-start | bytes 262144 | tf_op jit(solution)/shard_map/all_to_all | solution.py:521
  51.3 1.0 copy-done.1
  52.3 3.1 %shard_map.83 = (bf16[8,512,128]{2,1,0:T(8,128)(2,1)S(1)}, bf16[8,512,128]{2,1,0:T(8,128)(2,1)S(1)}, f32[8,128]{1,0:T(8,128)S(1)}) custom-call(bf16[64,16,512]{2,1,0:T(8,128)(2,1)} %pair.3, bf16[65,8,512]{2,1,0:T(8,128)(2,1)S(1)} %copy-done.1, bf16[65,8,512]{2,1,0:T(8,128)(2,1)S(1)} %collective-permute-done.1.two), custom_call_target="tpu_custom_call" | custom-call | flops 603979776 | bytes 1048576 | tf_op jit(solution)/shard_map/pallas_call | solution.py:28
  55.4 9.4 %all-to-all-done.terms = bf16[64,8,128]{2,1,0:T(8,128)(2,1)S(1)} async-done(((bf16[64,8,128]{2,1,0:T(8,128)(2,1)}), bf16[64,8,128]{2,1,0:T(8,128)(2,1)S(1)}, u32[]{:S(2)}, u32[]{:S(2)}) %all-to-all-start) | async-done | bytes 131104 | tf_op jit(solution)/shard_map/all_to_all | solution.py:521
  64.8 4.8 %shard_map.84 = (bf16[8,512,128]{2,1,0:T(8,128)(2,1)}, bf16[8,512,128]{2,1,0:T(8,128)(2,1)}, bf16[4,512,128]{2,1,0:T(8,128)(2,1)}, bf16[4,512,128]{2,1,0:T(8,128...) custom-call(bf16[8,512,128]{2,1,0:T(8,128)(2,1)S(1)} %get-tuple-element.26.own_raw, ...), custom_call_target="tpu_custom_call" | custom-call | flops 603979776 | bytes 1048576 | tf_op jit(solution)/shard_map/pallas_call | solution.py:28
  70.4 2.6 %collective-permute-start.4 = (bf16[4,512,128]{2,1,0:T(8,128)(2,1)S(1)}, bf16[4,512,128]{2,1,0:T(8,128)(2,1)S(1)}, u32[]{:S(2)}, u32[]{:S(2)}) collective-permute-start(bf16[4,512,128]{2,1,0:T(8,128)(2,1)S(1)} %get-tuple-element.34), channel_id=1, source_target_pairs={{0,2},{2,0},{4,6},{6,4},{8,10},{10,8},{12,14},{14,12},{16,18},{18,... | collective-permute-start | bytes 1572872 | tf_op jit(solution)/shard_map/ppermute | solution.py:574
  73.0 10.8 %all-to-all-start.1 = ((f32[64,1,128]{2,1,0:T(1,128)}), f32[64,1,128]{2,1,0:T(1,128)S(1)}, u32[]{:S(2)}, u32[]{:S(2)}) async-start(f32[64,1,128]{2,1,0:T(1,128)} %bitcast.5), calls=%async_computation.1 | async-start | bytes 65536 | tf_op jit(solution)/shard_map/all_to_all | solution.py:575
  83.8 2.0 %collective-permute-start.6 = (bf16[8,16,128]{2,1,0:T(8,128)(2,1)S(1)}, bf16[8,16,128]{2,1,0:T(8,128)(2,1)S(1)}, u32[]{:S(2)}, u32[]{:S(2)}) collective-permute-start(bf16[8,16,128]{2,1,0:T(8,128)(2,1)S(1)} %get-tuple-element.36), channel_id=1, source_target_pairs={{0,1},{1,0},{2,3},{3,2},{4,5},{5,4},{6,7},{7,6},{8,9},{9,8},{10,11... | collective-permute-start | bytes 98312 | tf_op jit(solution)/shard_map/ppermute | solution.py:498
  85.7 10.0 %all-to-all-done.1 = f32[64,1,128]{2,1,0:T(1,128)S(1)} async-done(((f32[64,1,128]{2,1,0:T(1,128)}), f32[64,1,128]{2,1,0:T(1,128)S(1)}, u32[]{:S(2)}, u32[]{:S(2)}) %all-to-all-start.1) | async-done | bytes 32800 | tf_op jit(solution)/shard_map/all_to_all | solution.py:575
  95.7 3.0 %collective-permute-start.8 = (f32[64,128]{1,0:T(8,128)S(1)}, f32[64,128]{1,0:T(8,128)S(1)}, u32[]{:S(2)}, u32[]{:S(2)}) collective-permute-start(f32[64,128]{1,0:T(8,128)S(1)} %bitcast.14), channel_id=1, source_target_pairs={{0,1},{1,0},{2,3},{3,2},{4,5},{5,4},{6,7},{7,6},{8,9},{9,8},{10,11... | collective-permute-start | bytes 98312 | tf_op jit(solution)/shard_map/ppermute | solution.py:498
  100.1 4.5 %shard_map.85 = (bf16[8,512,128]{2,1,0:T(8,128)(2,1)}, bf16[4,512,128]{2,1,0:T(8,128)(2,1)}, f32[64,128]{1,0:T(8,128)S(1)}) custom-call(bf16[8,512,128]{2,1,0:T(8,128)(2,1)} %get-tuple-element.33.own_in, bf16[4,512,128]{2,1,0:T(8,128)(2,1)S(1)} %collective-permute-done.4.one, bf16[4,512,128]{2,1,0:T(8,128)(2,1)S(1)} %collective-permute-done.5.two, ...), custom_call_target="tpu_custom_call" | custom-call | flops 603979776 | bytes 1048576 | tf_op jit(solution)/shard_map/pallas_call | solution.py:28
  104.9 17.7 %all_to_all.32 = f32[64,1,128]{2,1,0:T(1,128)S(1)} all-to-all(f32[64,1,128]{2,1,0:T(1,128)S(1)} %bitcast.18), channel_id=1, replica_groups=mesh['grp'=2,'gx_0'=4,'gx_1'=16,'gy'=2] {'gx_0','gx_1'}, dimensions={0} | all-to-all | bytes 65536 | tf_op jit(solution)/shard_map/all_to_all | solution.py:605
  122.6 1.8 collective-permute-start.10
  124.4 0.9 collective-permute-done.10.stats_other
  125.3 3.0 %shard_map.86 = (bf16[8,512,128]{2,1,0:T(8,128)(2,1)}, bf16[64,4,16,128]{3,2,1,0:T(8,128)(2,1)S(1)}) custom-call(bf16[8,512,128]{2,1,0:T(8,128)(2,1)} %get-tuple-element.31.block_in, bf16[4,512,128]{2,1,0:T(8,128)(2,1)S(1)} %collective-permute-done.3.other, bf16[8,512,128]{2,1,0:T(8,128)(2,1)} %get-tuple-element.38.conv_in, ...), custom_call_target="tpu_custom_call" | custom-call | flops 603979776 | bytes 1048576 | tf_op jit(solution)/shard_map/pallas_call | solution.py:28
  128.3 55.5 %all_to_all.33.received = bf16[64,4,16,128]{3,2,1,0:T(8,128)(2,1)S(1)} all-to-all(bf16[64,4,16,128]{3,2,1,0:T(8,128)(2,1)S(1)} %get-tuple-element.42), channel_id=1, replica_groups=mesh['grp'=2,'gx_0'=4,'gx_1'=16,'gy'=2] {'gx_0','gx_1'}, dimensions={0} | all-to-all | bytes 2097152 | tf_op jit(solution)/shard_map/all_to_all | solution.py:621
  183.8 3.5 %collective-permute-start.11 = (bf16[32,4,16,128]{3,2,1,0:T(8,128)(2,1)S(1)}, bf16[32,4,16,128]{3,2,1,0:T(8,128)(2,1)S(1)}, u32[]{:S(2)}, u32[]{:S(2)}) collective-permute-start(bf16[32,4,16,128]{3,2,1,0:T(8,128)(2,1)S(1)} %slice_select_fusion), channel_id=1, source_target_pairs={{0,1},{1,0},{2,3},{3,2},{4,5},{5,4},{6,7},{7,6},{8,9},{9,8},{10,11... | collective-permute-start | bytes 1572872 | tf_op jit(solution)/shard_map/ppermute | solution.py:498
  187.3 1.5 collective-permute-done.11.other
  188.8 3.8 %shard_map.87 = bf16[64,16,512]{2,1,0:T(8,128)(2,1)} custom-call(bf16[8,512,128]{2,1,0:T(8,128)(2,1)} %get-tuple-element.41.own_in, bf16[64,4,16,128]{3,2,1,0:T(8,128)(2,1)S(1)} %all_to_all.33.received, bf16[32,4,16,128]{3,2,1,0:T(8,128)(2,1)S(1)} %collective-permute-done.11.other), custom_call_target="tpu_custom_call" | custom-call | flops 603979776 | bytes 1048576 | tf_op jit(solution)/shard_map/pallas_call | solution.py:28
  (33 shorter events, 3.2 us)
Async XLA Ops:
  0.0 10.0 %copy-start.2 = (bf16[64,16,512]{2,1,0:T(8,128)(2,1)S(1)}, bf16[64,16,512]{2,1,0:T(8,128)(2,1)}, u32[]{:S(2)}) copy-start(bf16[64,16,512]{2,1,0:T(8,128)(2,1)} %pair.3) | copy-start | bytes 3145732
  2.1 7.9 %collective-permute-start.1 = (bf16[65,8,512]{2,1,0:T(8,128)(2,1)S(1)}, bf16[65,8,512]{2,1,0:T(8,128)(2,1)S(1)}, u32[]{:S(2)}, u32[]{:S(2)}) collective-permute-start(bf16[65,8,512]{2,1,0:T(8,128)(2,1)S(1)} %get-tuple-element.25), channel_id=1, source_target_pairs={{2,4},{4,2},{6,8},{8,6},{10,12},{12,10},{14,16},{16,14},{18,20},{2... | collective-permute-start | bytes 1597448 | tf_op jit(solution)/shard_map/ppermute | solution.py:520
  2.8 13.8 %collective-permute-start = (bf16[65,8,512]{2,1,0:T(8,128)(2,1)S(1)}, bf16[65,8,512]{2,1,0:T(8,128)(2,1)S(1)}, u32[]{:S(2)}, u32[]{:S(2)}) collective-permute-start(bf16[65,8,512]{2,1,0:T(8,128)(2,1)S(1)} %get-tuple-element.24), channel_id=1, source_target_pairs={{0,2},{2,0},{4,6},{6,4},{8,10},{10,8},{12,14},{14,12},{16,18},{18,... | collective-permute-start | bytes 1597448 | tf_op jit(solution)/shard_map/ppermute | solution.py:520
  16.7 1.0 copy-start
  17.6 47.2 %collective-permute-start.2 = (bf16[64,32,128]{2,1,0:T(8,128)(2,1)}, bf16[64,32,128]{2,1,0:T(8,128)(2,1)S(1)}, u32[]{:S(2)}, u32[]{:S(2)}) collective-permute-start(bf16[64,32,128]{2,1,0:T(8,128)(2,1)} %pad_maximum_fusion), channel_id=1, source_target_pairs={{0,1},{1,0},{2,3},{3,2},{4,5},{5,4},{6,7},{7,6},{8,9},{9,8},{10,11... | collective-permute-start | bytes 1572872 | tf_op jit(solution)/shard_map/ppermute | solution.py:498
  33.6 31.2 %all-to-all-start = ((bf16[64,8,128]{2,1,0:T(8,128)(2,1)}), bf16[64,8,128]{2,1,0:T(8,128)(2,1)S(1)}, u32[]{:S(2)}, u32[]{:S(2)}) async-start(bf16[64,8,128]{2,1,0:T(8,128)(2,1)} %get-tuple-element.29), calls=%async_computation | async-start | bytes 262144 | tf_op jit(solution)/shard_map/all_to_all | solution.py:521
  51.3 1.0 copy-start.1
  69.7 29.0 %collective-permute-start.5 = (bf16[4,512,128]{2,1,0:T(8,128)(2,1)}, bf16[4,512,128]{2,1,0:T(8,128)(2,1)S(1)}, u32[]{:S(2)}, u32[]{:S(2)}) collective-permute-start(bf16[4,512,128]{2,1,0:T(8,128)(2,1)} %get-tuple-element.35), channel_id=1, source_target_pairs={{2,4},{4,2},{6,8},{8,6},{10,12},{12,10},{14,16},{16,14},{18,20},{2... | collective-permute-start | bytes 1572872 | tf_op jit(solution)/shard_map/ppermute | solution.py:574
  70.4 28.4 %collective-permute-start.4 = (bf16[4,512,128]{2,1,0:T(8,128)(2,1)S(1)}, bf16[4,512,128]{2,1,0:T(8,128)(2,1)S(1)}, u32[]{:S(2)}, u32[]{:S(2)}) collective-permute-start(bf16[4,512,128]{2,1,0:T(8,128)(2,1)S(1)} %get-tuple-element.34), channel_id=1, source_target_pairs={{0,2},{2,0},{4,6},{6,4},{8,10},{10,8},{12,14},{14,12},{16,18},{18,... | collective-permute-start | bytes 1572872 | tf_op jit(solution)/shard_map/ppermute | solution.py:574
  73.0 22.7 %all-to-all-start.1 = ((f32[64,1,128]{2,1,0:T(1,128)}), f32[64,1,128]{2,1,0:T(1,128)S(1)}, u32[]{:S(2)}, u32[]{:S(2)}) async-start(f32[64,1,128]{2,1,0:T(1,128)} %bitcast.5), calls=%async_computation.1 | async-start | bytes 65536 | tf_op jit(solution)/shard_map/all_to_all | solution.py:575
  83.8 16.1 %collective-permute-start.6 = (bf16[8,16,128]{2,1,0:T(8,128)(2,1)S(1)}, bf16[8,16,128]{2,1,0:T(8,128)(2,1)S(1)}, u32[]{:S(2)}, u32[]{:S(2)}) collective-permute-start(bf16[8,16,128]{2,1,0:T(8,128)(2,1)S(1)} %get-tuple-element.36), channel_id=1, source_target_pairs={{0,1},{1,0},{2,3},{3,2},{4,5},{5,4},{6,7},{7,6},{8,9},{9,8},{10,11... | collective-permute-start | bytes 98312 | tf_op jit(solution)/shard_map/ppermute | solution.py:498
  95.7 4.1 %collective-permute-start.8 = (f32[64,128]{1,0:T(8,128)S(1)}, f32[64,128]{1,0:T(8,128)S(1)}, u32[]{:S(2)}, u32[]{:S(2)}) collective-permute-start(f32[64,128]{1,0:T(8,128)S(1)} %bitcast.14), channel_id=1, source_target_pairs={{0,1},{1,0},{2,3},{3,2},{4,5},{5,4},{6,7},{7,6},{8,9},{9,8},{10,11... | collective-permute-start | bytes 98312 | tf_op jit(solution)/shard_map/ppermute | solution.py:498
  98.8 0.7 copy-start.3
  98.8 0.7 copy-start.4
  98.8 1.3 collective-permute-start.7
  99.6 24.9 %collective-permute-start.3 = (bf16[4,512,128]{2,1,0:T(8,128)(2,1)}, bf16[4,512,128]{2,1,0:T(8,128)(2,1)S(1)}, u32[]{:S(2)}, u32[]{:S(2)}) collective-permute-start(bf16[4,512,128]{2,1,0:T(8,128)(2,1)} %get-tuple-element.32), channel_id=1, source_target_pairs={{0,1},{1,0},{2,3},{3,2},{4,5},{5,4},{6,7},{7,6},{8,9},{9,8},{10,11... | collective-permute-start | bytes 1572872 | tf_op jit(solution)/shard_map/ppermute | solution.py:498
  104.6 20.7 %collective-permute-start.9 = (bf16[4,512,128]{2,1,0:T(8,128)(2,1)}, bf16[4,512,128]{2,1,0:T(8,128)(2,1)S(1)}, u32[]{:S(2)}, u32[]{:S(2)}) collective-permute-start(bf16[4,512,128]{2,1,0:T(8,128)(2,1)} %get-tuple-element.39), channel_id=1, source_target_pairs={{0,1},{1,0},{2,3},{3,2},{4,5},{5,4},{6,7},{7,6},{8,9},{9,8},{10,11... | collective-permute-start | bytes 1572872 | tf_op jit(solution)/shard_map/ppermute | solution.py:498
  122.6 2.7 %collective-permute-start.10 = (f32[64,128]{1,0:T(8,128)S(1)}, f32[64,128]{1,0:T(8,128)S(1)}, u32[]{:S(2)}, u32[]{:S(2)}) collective-permute-start(f32[64,128]{1,0:T(8,128)S(1)} %bitcast.16), channel_id=1, source_target_pairs={{0,1},{1,0},{2,3},{3,2},{4,5},{5,4},{6,7},{7,6},{8,9},{9,8},{10,11... | collective-permute-start | bytes 98312 | tf_op jit(solution)/shard_map/ppermute | solution.py:498
  183.8 5.0 %collective-permute-start.11 = (bf16[32,4,16,128]{3,2,1,0:T(8,128)(2,1)S(1)}, bf16[32,4,16,128]{3,2,1,0:T(8,128)(2,1)S(1)}, u32[]{:S(2)}, u32[]{:S(2)}) collective-permute-start(bf16[32,4,16,128]{3,2,1,0:T(8,128)(2,1)S(1)} %slice_select_fusion), channel_id=1, source_target_pairs={{0,1},{1,0},{2,3},{3,2},{4,5},{5,4},{6,7},{7,6},{8,9},{9,8},{10,11... | collective-permute-start | bytes 1572872 | tf_op jit(solution)/shard_map/ppermute | solution.py:498

commit v8 on v7

--- a/solution.py
+++ b/solution.py
@@ -234,39 +234,45 @@
     wait_all(parts)
 
 
-def turn_kernel(
-    pair, one, two, own_ref, near_ref, row_terms, own, own_flat, above_flat, below_flat, sem
-):
+def turn_own_kernel(pair, own_ref, own, own_flat, sem):
+    rows = own.shape[1]
+    wait_all(start_all(sem, 0, ((pair, own),)))
+    widen(own, own_flat)
+    turn_rows(own_ref, ((own_flat, 0, rows), (own_flat, STEP, rows)))
+
+
+def widen_halo(halo, which, above_flat, below_flat):
+    is_above = lax.rem(lax.axis_index(GX) + which, 2)
+
+    @pl.when(is_above == 1)
+    def _():
+        widen(halo, above_flat)
+
+    @pl.when(is_above == 0)
+    def _():
+        widen(halo, below_flat)
+
+
+def turn_near_kernel(one, two_in, near_ref, row_terms, two, above_flat, below_flat, sem):
     odd = lax.rem(lax.axis_index(GX), 2)
-    channels, rows, _ = own.shape
-    inputs = start_all(sem, 0, ((pair, own),))
-    one_rows, two_rows = one.at[pl.ds(0, channels)], two.at[pl.ds(0, channels)]
-
-    @pl.when(odd == 0)
-    def _():
-        widen(two_rows, above_flat)
-        widen(one_rows, below_flat)
-
-    @pl.when(odd == 1)
-    def _():
-        widen(one_rows, above_flat)
-        widen(two_rows, below_flat)
-
+    channels = one.shape[0] - 1
+    inputs = start_all(sem, 0, ((two_in, two),))
+    widen_halo(one.at[pl.ds(0, channels)], 0, above_flat, below_flat)
     one_terms = one[channels, :, :LANES].astype(jnp.float32)
+    wait_all(inputs)
+    widen_halo(two.at[pl.ds(0, channels)], 1, above_flat, below_flat)
     two_terms = two[channels, :, :LANES].astype(jnp.float32)
     row_terms[...] = halves(
         jnp.where(odd == 1, one_terms, two_terms), jnp.where(odd == 1, two_terms, one_terms)
     )
     turn_rows(near_ref, ((above_flat, 0, STEP), (below_flat, 0, STEP)))
-    wait_all(inputs)
-    widen(own, own_flat)
-    turn_rows(own_ref, ((own_flat, 0, rows), (own_flat, STEP, rows)))
 
 
 def first_kernel(
-    devices, own_raw, near_raw, near_terms, side, terms, mine, taps_in,
+    devices, own_raw, near_raw, near_terms, side, side_one, side_two, terms, mine, taps_in,
     own_out, conv_out, give_out, one_ref, two_ref, edge_ref, stats_ref,
-    x_own, x_near, conv_ref, p_ref, taps, side_flat, col_terms, row_terms, sem,
+    x_own, x_near, conv_ref, p_ref, taps, side_flat, above_flat, below_flat, col_terms, row_terms,
+    sem,
 ):
     row_at, core = lax.axis_index(GX), lax.axis_index("gy")
     cols = own_raw.shape[1]
@@ -285,17 +291,17 @@
     put_terms([(peers * core + i, i * rows) for i in range(peers)] + [(peers - core, cols)])
     row_terms[...] = mine[...].astype(jnp.bfloat16).astype(jnp.float32)
     mask = reach_mask(core)
-    tall = rows + 2 * STEP
-    above_at, below_at = (STEP + rows) * (1 - odd), (STEP + rows) * odd
     widen(side, side_flat)
     add_terms(
-        x_own, own_raw, ((side_flat, STEP, tall), (side_flat, 2 * STEP, tall)),
+        x_own, own_raw, ((side_flat, 0, rows), (side_flat, STEP, rows)),
         row_terms, col_terms, None, core, mask,
     )
     given = x_own.at[pl.ds(half * (1 - core), half), pl.ds(0, cols)]
     outputs = start_all(sem, 1, ((x_own.at[:, pl.ds(0, cols)], own_out), (given, give_out)))
+    widen_halo(side_one, 0, above_flat, below_flat)
+    widen_halo(side_two, 1, above_flat, below_flat)
     add_terms(
-        x_near, near_raw, ((side_flat, above_at, tall), (side_flat, below_at, tall)),
+        x_near, near_raw, ((above_flat, 0, STEP), (below_flat, 0, STEP)),
         near_terms, col_terms, inside_of(row_at, devices), core, mask,
     )
     wait_all(inputs)
@@ -403,10 +409,12 @@
             out_ref[i, at, :] = block_out(own[i, at, :], conv[i, at, :])
         return 0
 
+    outputs = []
     for n, part in enumerate(parts):
         wait_all(part)
         lax.fori_loop(2 * n, 2 * n + 2, mine, 0)
-    outputs = start_all(sem, STEP, ((out_ref, block_out_out),))
+        at = pl.ds(2 * n, 2)
+        outputs += start_all(sem, STEP + n, ((out_ref.at[at], block_out_out.at[at]),))
 
     def step(i, _):
         for first in range(0, cols, LANES):
@@ -520,11 +528,8 @@
     one, two = with_next(one), with_last(two)
     terms = lax.all_to_all(terms, GX, 0, 0, tiled=True)
     gains = jnp.tile(jnp.concatenate([norm_scale, norm_shift], axis=0), (1, 2))
-    near_side = swap(
-        jnp.concatenate(
-            [edge(one[:channels]), edge(pair_feats), edge(two[:channels])], axis=1
-        )
-    )
+    own_side = swap(edge(pair_feats))
+    one_side, two_side = swap(edge(one[:channels])), swap(edge(two[:channels]))
 
     taps_shape = VMEM(first_taps.shape, bf16)
     whole = (STEP, cols, LANES)
@@ -532,18 +537,21 @@
     wide = (STEP, cols + 2 * STEP, LANES)
     products = VMEM((2, cols + 2 * STEP, 3 * LANES), f32)
     sums = (devices, LANES)
-    own_raw, near_raw, near_terms = call(
-        turn_kernel,
-        ((VMEM, whole, bf16), (VMEM, whole, bf16), (VMEM, (STEP, LANES), f32)),
-        [
-            VMEM(pair_feats.shape, bf16),
-            flat_of(channels, rows, cols),
-            flat_of(channels, STEP, cols),
-            flat_of(channels, STEP, cols),
-        ],
+    (own_raw,) = call(
+        turn_own_kernel,
+        ((VMEM, whole, bf16),),
+        [VMEM(pair_feats.shape, bf16), flat_of(channels, rows, cols)],
         1,
         conv_flops,
-        ((HBM, pair_feats), (VMEM, one), (VMEM, two)),
+        ((HBM, pair_feats),),
+    )
+    near_raw, near_terms = call(
+        turn_near_kernel,
+        ((VMEM, whole, bf16), (VMEM, (STEP, LANES), f32)),
+        [VMEM(two.shape, bf16), flat_of(channels, STEP, cols), flat_of(channels, STEP, cols)],
+        1,
+        conv_flops,
+        ((VMEM, one), (HBM, two)),
     )
     own_rows, conv_own, own_give, conv_one, conv_two, edges, stats = call(
         functools.partial(first_kernel, devices),
@@ -562,14 +570,16 @@
             VMEM(whole, bf16),
             products,
             taps_shape,
-            flat_of(channels, rows + 2 * STEP, LANES),
+            flat_of(channels, rows, LANES),
+            flat_of(channels, STEP, LANES),
+            flat_of(channels, STEP, LANES),
             VMEM(wide[1:], f32),
             VMEM((STEP, LANES), f32),
         ],
         4,
         conv_flops,
-        ((VMEM, own_raw), (VMEM, near_raw), (VMEM, near_terms), (VMEM, near_side),
-         (VMEM, terms), (VMEM, mine), (HBM, first_taps)),
+        ((VMEM, own_raw), (VMEM, near_raw), (VMEM, near_terms), (VMEM, own_side),
+         (VMEM, one_side), (VMEM, two_side), (VMEM, terms), (VMEM, mine), (HBM, first_taps)),
     )
     conv_one, conv_two = with_next(conv_one), with_last(conv_two)
     stats = lax.all_to_all(stats, GX, 0, 0, tiled=True)
@@ -613,7 +623,7 @@
             VMEM(whole, bf16),
             VMEM(whole, bf16),
         ],
-        STEP + 1,
+        STEP + STEP // 2,
         conv_flops,
         ((HBM, own_rows), (VMEM, own_other), (HBM, conv_second), (VMEM, conv_other),
          (VMEM, stats), (VMEM, stats_other), (VMEM, gains)),

time: 193 us -> 182 us (0.943)
  waiting for transfers between devices: 28.7 us -> 17.8 us
  starting transfers between devices: 66.5 us -> 61.5 us
  blocking collectives: 73.2 us -> 76 us
    ppermute x2, waiting for transfers between devices: 6.59 us -> 0.01 us  [body(): one, two = (with_next(one), with_last(two))]
    all_to_all x1, waiting for transfers between devices: 9.41 us -> 5.17 us  [body(): terms = lax.all_to_all(terms, GX, 0, 0, tiled=True)]
    all_to_all x1, starting transfers between devices: 17.7 us -> 13.5 us  [body(): terms = lax.all_to_all(terms, GX, 0, 0, tiled=True)]
    ppermute x2, starting transfers between devices: 7.87 us -> 4.9 us  [body(): one, two = (with_next(one), with_last(two))]
    all_to_all x1, blocking collectives: 17.7 us -> 20.5 us  [body(): stats = lax.all_to_all(stats, GX, 0, 0, tiled=True)]
    select_n x3, other arithmetic: 0.07 us -> 2.36 us  [edge(): return jnp.where(first_core, x[..., cols - LANES:], x[..., :LANES])]
    ppermute x8 -> x10, starting transfers between devices: 26.9 us -> 28.8 us  [swap(): return lax.ppermute(x, 'gy', SWAP)]
    pallas_call x6 -> x7, Pallas kernels: 21.3 us -> 22.9 us  [call(): pl.pallas_call(kernel, out_shape=[space(shape, dtype) for space, shape, d...]
  transfers between devices with their start and end apart: 14 -> 16, of which waited for: 6 -> 5; matrix products, arithmetic and copies ran while one was open for 0% -> 1% of each run, Pallas kernels for 4% -> 5%
where the time goes in v8:
time: 182 us
  blocking collectives  76 us (42%)
  starting transfers between devices  61.5 us (34%)
  Pallas kernels  22.9 us (13%)
  waiting for transfers between devices  17.8 us (10%)
  other arithmetic  2.44 us (1%)
    all_to_all x1, blocking collectives, body(): received = lax.all_to_all(send, GX, 0, 0, tiled=True)  55.5 us
    ppermute x10, starting transfers between devices, swap(): return lax.ppermute(x, 'gy', SWAP)  28.8 us
    pallas_call x7, Pallas kernels, call(): pl.pallas_call(kernel, out_shape=[space(shape, dtype) for space, shape, d...  22.9 us
    all_to_all x1, blocking collectives, body(): stats = lax.all_to_all(stats, GX, 0, 0, tiled=True)  20.5 us
    all_to_all x1, starting transfers between devices, body(): terms = lax.all_to_all(terms, GX, 0, 0, tiled=True)  13.5 us
    all_to_all x1, starting transfers between devices, body(): stats = lax.all_to_all(stats, GX, 0, 0, tiled=True)  10.9 us
    all_to_all x1, waiting for transfers between devices, body(): stats = lax.all_to_all(stats, GX, 0, 0, tiled=True)  9.93 us
    all_to_all x1, waiting for transfers between devices, body(): terms = lax.all_to_all(terms, GX, 0, 0, tiled=True)  5.17 us
  transfers between devices with their start and end apart: 16, of which 5 were waited for; matrix products, arithmetic and copies ran while one was open for 1% of the time, Pallas kernels for 5%

profile of v8, /device:TPU:33, one launch (start us, length us, event | category | flops | bytes accessed | tf_op | source)
XLA Modules:
  0.0 181.6 jit_solution(9818974177035235051)
XLA Ops:
  0.0 2.1 %shard_map.83 = (bf16[65,8,512]{2,1,0:T(8,128)(2,1)S(1)}, bf16[65,8,512]{2,1,0:T(8,128)(2,1)S(1)}, bf16[64,8,128]{2,1,0:T(8,128)(2,1)}, f32[8,128]{1,0:T(8,128)S(1)}) custom-call(bf16[64,16,512]{2,1,0:T(8,128)(2,1)} %pair.3, bf16[16,256]{1,0:T(8,128)(2,1)} %feats.1, bf16[64,256]{1,0:T(8,128)(2,1)} %bitcast.19, bf16[64,256]{1,0:T(8,128)(2,1)} %bitcast.20), custom_call_target="tpu_custom_call" | custom-call | flops 37748736 | bytes 1048576 | tf_op jit(solution)/shard_map/pallas_call | solution.py:28
  2.1 3.4 %collective-permute-start = (bf16[65,8,512]{2,1,0:T(8,128)(2,1)S(1)}, bf16[65,8,512]{2,1,0:T(8,128)(2,1)S(1)}, u32[]{:S(2)}, u32[]{:S(2)}) collective-permute-start(bf16[65,8,512]{2,1,0:T(8,128)(2,1)S(1)} %get-tuple-element.23), channel_id=1, source_target_pairs={{0,2},{2,0},{4,6},{6,4},{8,10},{10,8},{12,14},{14,12},{16,18},{18,... | collective-permute-start | bytes 1597448 | tf_op jit(solution)/shard_map/ppermute | solution.py:528
  5.6 1.5 collective-permute-start.1
  7.1 17.3 %collective-permute-start.2 = (bf16[64,16,128]{2,1,0:T(8,128)(2,1)S(1)}, bf16[64,16,128]{2,1,0:T(8,128)(2,1)S(1)}, u32[]{:S(2)}, u32[]{:S(2)}) collective-permute-start(bf16[64,16,128]{2,1,0:T(8,128)(2,1)S(1)} %slice_select_fusion.1), channel_id=1, source_target_pairs={{0,1},{1,0},{2,3},{3,2},{4,5},{5,4},{6,7},{7,6},{8,9},{9,8},{10,11... | collective-permute-start | bytes 786440 | tf_op jit(solution)/shard_map/ppermute | solution.py:506
  24.3 13.5 %all-to-all-start = ((bf16[64,8,128]{2,1,0:T(8,128)(2,1)}), bf16[64,8,128]{2,1,0:T(8,128)(2,1)S(1)}, u32[]{:S(2)}, u32[]{:S(2)}) async-start(bf16[64,8,128]{2,1,0:T(8,128)(2,1)} %get-tuple-element.27), calls=%async_computation | async-start | bytes 262144 | tf_op jit(solution)/shard_map/all_to_all | solution.py:529
  38.9 1.6 slice_select_fusion.2
  40.7 2.9 %shard_map.82.own_raw = bf16[8,512,128]{2,1,0:T(8,128)(2,1)S(1)} custom-call(bf16[64,16,512]{2,1,0:T(8,128)(2,1)} %pair.3), custom_call_target="tpu_custom_call" | custom-call | flops 603979776 | bytes 1048576 | tf_op jit(solution)/shard_map/pallas_call | solution.py:28
  43.7 2.3 %shard_map.84 = (bf16[8,512,128]{2,1,0:T(8,128)(2,1)S(1)}, f32[8,128]{1,0:T(8,128)S(1)}) custom-call(bf16[65,8,512]{2,1,0:T(8,128)(2,1)S(1)} %collective-permute-done.one, bf16[65,8,512]{2,1,0:T(8,128)(2,1)} %collective-permute-done.1.two_in), custom_call_target="tpu_custom_call" | custom-call | flops 603979776 | bytes 1048576 | tf_op jit(solution)/shard_map/pallas_call | solution.py:28
  46.0 5.2 %all-to-all-done.terms = bf16[64,8,128]{2,1,0:T(8,128)(2,1)S(1)} async-done(((bf16[64,8,128]{2,1,0:T(8,128)(2,1)}), bf16[64,8,128]{2,1,0:T(8,128)(2,1)S(1)}, u32[]{:S(2)}, u32[]{:S(2)}) %all-to-all-start) | async-done | bytes 131104 | tf_op jit(solution)/shard_map/all_to_all | solution.py:529
  51.2 4.6 %shard_map.85 = (bf16[8,512,128]{2,1,0:T(8,128)(2,1)}, bf16[8,512,128]{2,1,0:T(8,128)(2,1)}, bf16[4,512,128]{2,1,0:T(8,128)(2,1)}, bf16[4,512,128]{2,1,0:T(8,128...) custom-call(bf16[8,512,128]{2,1,0:T(8,128)(2,1)S(1)} %shard_map.82.own_raw, ...), custom_call_target="tpu_custom_call" | custom-call | flops 603979776 | bytes 1048576 | tf_op jit(solution)/shard_map/pallas_call | solution.py:28
  56.5 2.7 %collective-permute-start.6 = (bf16[4,512,128]{2,1,0:T(8,128)(2,1)S(1)}, bf16[4,512,128]{2,1,0:T(8,128)(2,1)S(1)}, u32[]{:S(2)}, u32[]{:S(2)}) collective-permute-start(bf16[4,512,128]{2,1,0:T(8,128)(2,1)S(1)} %get-tuple-element.32), channel_id=1, source_target_pairs={{0,2},{2,0},{4,6},{6,4},{8,10},{10,8},{12,14},{14,12},{16,18},{18,... | collective-permute-start | bytes 1572872 | tf_op jit(solution)/shard_map/ppermute | solution.py:584
  59.2 10.9 %all-to-all-start.1 = ((f32[64,1,128]{2,1,0:T(1,128)}), f32[64,1,128]{2,1,0:T(1,128)S(1)}, u32[]{:S(2)}, u32[]{:S(2)}) async-start(f32[64,1,128]{2,1,0:T(1,128)} %bitcast.5), calls=%async_computation.1 | async-start | bytes 65536 | tf_op jit(solution)/shard_map/all_to_all | solution.py:585
  70.1 2.0 %collective-permute-start.8 = (bf16[8,16,128]{2,1,0:T(8,128)(2,1)S(1)}, bf16[8,16,128]{2,1,0:T(8,128)(2,1)S(1)}, u32[]{:S(2)}, u32[]{:S(2)}) collective-permute-start(bf16[8,16,128]{2,1,0:T(8,128)(2,1)S(1)} %get-tuple-element.34), channel_id=1, source_target_pairs={{0,1},{1,0},{2,3},{3,2},{4,5},{5,4},{6,7},{7,6},{8,9},{9,8},{10,11... | collective-permute-start | bytes 98312 | tf_op jit(solution)/shard_map/ppermute | solution.py:506
  72.1 9.9 %all-to-all-done.1 = f32[64,1,128]{2,1,0:T(1,128)S(1)} async-done(((f32[64,1,128]{2,1,0:T(1,128)}), f32[64,1,128]{2,1,0:T(1,128)S(1)}, u32[]{:S(2)}, u32[]{:S(2)}) %all-to-all-start.1) | async-done | bytes 32800 | tf_op jit(solution)/shard_map/all_to_all | solution.py:585
  82.0 3.0 %collective-permute-start.10 = (f32[64,128]{1,0:T(8,128)S(1)}, f32[64,128]{1,0:T(8,128)S(1)}, u32[]{:S(2)}, u32[]{:S(2)}) collective-permute-start(f32[64,128]{1,0:T(8,128)S(1)} %bitcast.14), channel_id=1, source_target_pairs={{0,1},{1,0},{2,3},{3,2},{4,5},{5,4},{6,7},{7,6},{8,9},{9,8},{10,11... | collective-permute-start | bytes 98312 | tf_op jit(solution)/shard_map/ppermute | solution.py:506
  86.4 4.5 %shard_map.86 = (bf16[8,512,128]{2,1,0:T(8,128)(2,1)}, bf16[4,512,128]{2,1,0:T(8,128)(2,1)}, f32[64,128]{1,0:T(8,128)S(1)}) custom-call(bf16[8,512,128]{2,1,0:T(8,128)(2,1)} %get-tuple-element.31.own_in, bf16[4,512,128]{2,1,0:T(8,128)(2,1)S(1)} %collective-permute-done.6.one, bf16[4,512,128]{2,1,0:T(8,128)(2,1)S(1)} %collective-permute-done.7.two, ...), custom_call_target="tpu_custom_call" | custom-call | flops 603979776 | bytes 1048576 | tf_op jit(solution)/shard_map/pallas_call | solution.py:28
  91.2 20.5 %all_to_all.32 = f32[64,1,128]{2,1,0:T(1,128)S(1)} all-to-all(f32[64,1,128]{2,1,0:T(1,128)S(1)} %bitcast.18), channel_id=1, replica_groups=mesh['grp'=2,'gx_0'=4,'gx_1'=16,'gy'=2] {'gx_0','gx_1'}, dimensions={0} | all-to-all | bytes 65536 | tf_op jit(solution)/shard_map/all_to_all | solution.py:615
  111.7 1.8 %collective-permute-start.12 = (f32[64,128]{1,0:T(8,128)S(1)}, f32[64,128]{1,0:T(8,128)S(1)}, u32[]{:S(2)}, u32[]{:S(2)}) collective-permute-start(f32[64,128]{1,0:T(8,128)S(1)} %bitcast.16), channel_id=1, source_target_pairs={{0,1},{1,0},{2,3},{3,2},{4,5},{5,4},{6,7},{7,6},{8,9},{9,8},{10,11... | collective-permute-start | bytes 98312 | tf_op jit(solution)/shard_map/ppermute | solution.py:506
  113.5 0.9 collective-permute-done.12.stats_other
  114.4 2.7 %shard_map.87 = (bf16[8,512,128]{2,1,0:T(8,128)(2,1)}, bf16[64,4,16,128]{3,2,1,0:T(8,128)(2,1)S(1)}) custom-call(bf16[8,512,128]{2,1,0:T(8,128)(2,1)} %get-tuple-element.29.block_in, bf16[4,512,128]{2,1,0:T(8,128)(2,1)S(1)} %collective-permute-done.5.other, bf16[8,512,128]{2,1,0:T(8,128)(2,1)} %get-tuple-element.36.conv_in, ...), custom_call_target="tpu_custom_call" | custom-call | flops 603979776 | bytes 1048576 | tf_op jit(solution)/shard_map/pallas_call | solution.py:28
  117.1 55.5 %all_to_all.33.received = bf16[64,4,16,128]{3,2,1,0:T(8,128)(2,1)S(1)} all-to-all(bf16[64,4,16,128]{3,2,1,0:T(8,128)(2,1)S(1)} %get-tuple-element.40), channel_id=1, replica_groups=mesh['grp'=2,'gx_0'=4,'gx_1'=16,'gy'=2] {'gx_0','gx_1'}, dimensions={0} | all-to-all | bytes 2097152 | tf_op jit(solution)/shard_map/all_to_all | solution.py:631
  172.7 3.5 %collective-permute-start.13 = (bf16[32,4,16,128]{3,2,1,0:T(8,128)(2,1)S(1)}, bf16[32,4,16,128]{3,2,1,0:T(8,128)(2,1)S(1)}, u32[]{:S(2)}, u32[]{:S(2)}) collective-permute-start(bf16[32,4,16,128]{3,2,1,0:T(8,128)(2,1)S(1)} %slice_select_fusion), channel_id=1, source_target_pairs={{0,1},{1,0},{2,3},{3,2},{4,5},{5,4},{6,7},{7,6},{8,9},{9,8},{10,11... | collective-permute-start | bytes 1572872 | tf_op jit(solution)/shard_map/ppermute | solution.py:506
  176.1 1.5 collective-permute-done.13.other
  177.6 3.8 %shard_map.88 = bf16[64,16,512]{2,1,0:T(8,128)(2,1)} custom-call(bf16[8,512,128]{2,1,0:T(8,128)(2,1)} %get-tuple-element.39.own_in, bf16[64,4,16,128]{3,2,1,0:T(8,128)(2,1)S(1)} %all_to_all.33.received, bf16[32,4,16,128]{3,2,1,0:T(8,128)(2,1)S(1)} %collective-permute-done.13.other), custom_call_target="tpu_custom_call" | custom-call | flops 603979776 | bytes 1048576 | tf_op jit(solution)/shard_map/pallas_call | solution.py:28
  (33 shorter events, 3.6 us)
Async XLA Ops:
  0.0 7.0 %copy-start = (bf16[64,16,512]{2,1,0:T(8,128)(2,1)S(1)}, bf16[64,16,512]{2,1,0:T(8,128)(2,1)}, u32[]{:S(2)}) copy-start(bf16[64,16,512]{2,1,0:T(8,128)(2,1)} %pair.3) | copy-start | bytes 3145732
  2.1 35.7 %collective-permute-start = (bf16[65,8,512]{2,1,0:T(8,128)(2,1)S(1)}, bf16[65,8,512]{2,1,0:T(8,128)(2,1)S(1)}, u32[]{:S(2)}, u32[]{:S(2)}) collective-permute-start(bf16[65,8,512]{2,1,0:T(8,128)(2,1)S(1)} %get-tuple-element.23), channel_id=1, source_target_pairs={{0,2},{2,0},{4,6},{6,4},{8,10},{10,8},{12,14},{14,12},{16,18},{18,... | collective-permute-start | bytes 1597448 | tf_op jit(solution)/shard_map/ppermute | solution.py:528
  5.6 33.3 %collective-permute-start.1 = (bf16[65,8,512]{2,1,0:T(8,128)(2,1)S(1)}, bf16[65,8,512]{2,1,0:T(8,128)(2,1)}, u32[]{:S(2)}, u32[]{:S(2)}) collective-permute-start(bf16[65,8,512]{2,1,0:T(8,128)(2,1)S(1)} %get-tuple-element.24), channel_id=1, source_target_pairs={{2,4},{4,2},{6,8},{8,6},{10,12},{12,10},{14,16},{16,14},{18,20},{2... | collective-permute-start | bytes 1597448 | tf_op jit(solution)/shard_map/ppermute | solution.py:528
  7.1 38.9 %collective-permute-start.2 = (bf16[64,16,128]{2,1,0:T(8,128)(2,1)S(1)}, bf16[64,16,128]{2,1,0:T(8,128)(2,1)S(1)}, u32[]{:S(2)}, u32[]{:S(2)}) collective-permute-start(bf16[64,16,128]{2,1,0:T(8,128)(2,1)S(1)} %slice_select_fusion.1), channel_id=1, source_target_pairs={{0,1},{1,0},{2,3},{3,2},{4,5},{5,4},{6,7},{7,6},{8,9},{9,8},{10,11... | collective-permute-start | bytes 786440 | tf_op jit(solution)/shard_map/ppermute | solution.py:506
  24.3 26.9 %all-to-all-start = ((bf16[64,8,128]{2,1,0:T(8,128)(2,1)}), bf16[64,8,128]{2,1,0:T(8,128)(2,1)S(1)}, u32[]{:S(2)}, u32[]{:S(2)}) async-start(bf16[64,8,128]{2,1,0:T(8,128)(2,1)} %get-tuple-element.27), calls=%async_computation | async-start | bytes 262144 | tf_op jit(solution)/shard_map/all_to_all | solution.py:529
  38.5 12.6 %collective-permute-start.3 = (bf16[64,8,128]{2,1,0:T(8,128)(2,1)}, bf16[64,8,128]{2,1,0:T(8,128)(2,1)S(1)}, u32[]{:S(2)}, u32[]{:S(2)}) collective-permute-start(bf16[64,8,128]{2,1,0:T(8,128)(2,1)} %slice_select_fusion.3), channel_id=1, source_target_pairs={{0,1},{1,0},{2,3},{3,2},{4,5},{5,4},{6,7},{7,6},{8,9},{9,8},{10,11... | collective-permute-start | bytes 393224 | tf_op jit(solution)/shard_map/ppermute | solution.py:506
  40.5 10.7 %collective-permute-start.4 = (bf16[64,8,128]{2,1,0:T(8,128)(2,1)}, bf16[64,8,128]{2,1,0:T(8,128)(2,1)S(1)}, u32[]{:S(2)}, u32[]{:S(2)}) collective-permute-start(bf16[64,8,128]{2,1,0:T(8,128)(2,1)} %slice_select_fusion.2), channel_id=1, source_target_pairs={{0,1},{1,0},{2,3},{3,2},{4,5},{5,4},{6,7},{7,6},{8,9},{9,8},{10,11... | collective-permute-start | bytes 393224 | tf_op jit(solution)/shard_map/ppermute | solution.py:506
  55.8 29.3 %collective-permute-start.7 = (bf16[4,512,128]{2,1,0:T(8,128)(2,1)}, bf16[4,512,128]{2,1,0:T(8,128)(2,1)S(1)}, u32[]{:S(2)}, u32[]{:S(2)}) collective-permute-start(bf16[4,512,128]{2,1,0:T(8,128)(2,1)} %get-tuple-element.33), channel_id=1, source_target_pairs={{2,4},{4,2},{6,8},{8,6},{10,12},{12,10},{14,16},{16,14},{18,20},{2... | collective-permute-start | bytes 1572872 | tf_op jit(solution)/shard_map/ppermute | solution.py:584
  56.5 28.6 %collective-permute-start.6 = (bf16[4,512,128]{2,1,0:T(8,128)(2,1)S(1)}, bf16[4,512,128]{2,1,0:T(8,128)(2,1)S(1)}, u32[]{:S(2)}, u32[]{:S(2)}) collective-permute-start(bf16[4,512,128]{2,1,0:T(8,128)(2,1)S(1)} %get-tuple-element.32), channel_id=1, source_target_pairs={{0,2},{2,0},{4,6},{6,4},{8,10},{10,8},{12,14},{14,12},{16,18},{18,... | collective-permute-start | bytes 1572872 | tf_op jit(solution)/shard_map/ppermute | solution.py:584
  59.2 22.8 %all-to-all-start.1 = ((f32[64,1,128]{2,1,0:T(1,128)}), f32[64,1,128]{2,1,0:T(1,128)S(1)}, u32[]{:S(2)}, u32[]{:S(2)}) async-start(f32[64,1,128]{2,1,0:T(1,128)} %bitcast.5), calls=%async_computation.1 | async-start | bytes 65536 | tf_op jit(solution)/shard_map/all_to_all | solution.py:585
  70.1 16.0 %collective-permute-start.8 = (bf16[8,16,128]{2,1,0:T(8,128)(2,1)S(1)}, bf16[8,16,128]{2,1,0:T(8,128)(2,1)S(1)}, u32[]{:S(2)}, u32[]{:S(2)}) collective-permute-start(bf16[8,16,128]{2,1,0:T(8,128)(2,1)S(1)} %get-tuple-element.34), channel_id=1, source_target_pairs={{0,1},{1,0},{2,3},{3,2},{4,5},{5,4},{6,7},{7,6},{8,9},{9,8},{10,11... | collective-permute-start | bytes 98312 | tf_op jit(solution)/shard_map/ppermute | solution.py:506
  82.0 4.1 %collective-permute-start.10 = (f32[64,128]{1,0:T(8,128)S(1)}, f32[64,128]{1,0:T(8,128)S(1)}, u32[]{:S(2)}, u32[]{:S(2)}) collective-permute-start(f32[64,128]{1,0:T(8,128)S(1)} %bitcast.14), channel_id=1, source_target_pairs={{0,1},{1,0},{2,3},{3,2},{4,5},{5,4},{6,7},{7,6},{8,9},{9,8},{10,11... | collective-permute-start | bytes 98312 | tf_op jit(solution)/shard_map/ppermute | solution.py:506
  85.1 0.7 copy-start.1
  85.1 0.7 copy-start.2
  85.1 1.3 collective-permute-start.9
  85.9 27.7 %collective-permute-start.5 = (bf16[4,512,128]{2,1,0:T(8,128)(2,1)}, bf16[4,512,128]{2,1,0:T(8,128)(2,1)S(1)}, u32[]{:S(2)}, u32[]{:S(2)}) collective-permute-start(bf16[4,512,128]{2,1,0:T(8,128)(2,1)} %get-tuple-element.30), channel_id=1, source_target_pairs={{0,1},{1,0},{2,3},{3,2},{4,5},{5,4},{6,7},{7,6},{8,9},{9,8},{10,11... | collective-permute-start | bytes 1572872 | tf_op jit(solution)/shard_map/ppermute | solution.py:506
  90.9 23.5 %collective-permute-start.11 = (bf16[4,512,128]{2,1,0:T(8,128)(2,1)}, bf16[4,512,128]{2,1,0:T(8,128)(2,1)S(1)}, u32[]{:S(2)}, u32[]{:S(2)}) collective-permute-start(bf16[4,512,128]{2,1,0:T(8,128)(2,1)} %get-tuple-element.37), channel_id=1, source_target_pairs={{0,1},{1,0},{2,3},{3,2},{4,5},{5,4},{6,7},{7,6},{8,9},{9,8},{10,11... | collective-permute-start | bytes 1572872 | tf_op jit(solution)/shard_map/ppermute | solution.py:506
  111.7 2.7 %collective-permute-start.12 = (f32[64,128]{1,0:T(8,128)S(1)}, f32[64,128]{1,0:T(8,128)S(1)}, u32[]{:S(2)}, u32[]{:S(2)}) collective-permute-start(f32[64,128]{1,0:T(8,128)S(1)} %bitcast.16), channel_id=1, source_target_pairs={{0,1},{1,0},{2,3},{3,2},{4,5},{5,4},{6,7},{7,6},{8,9},{9,8},{10,11... | collective-permute-start | bytes 98312 | tf_op jit(solution)/shard_map/ppermute | solution.py:506
  172.7 5.0 %collective-permute-start.13 = (bf16[32,4,16,128]{3,2,1,0:T(8,128)(2,1)S(1)}, bf16[32,4,16,128]{3,2,1,0:T(8,128)(2,1)S(1)}, u32[]{:S(2)}, u32[]{:S(2)}) collective-permute-start(bf16[32,4,16,128]{3,2,1,0:T(8,128)(2,1)S(1)} %slice_select_fusion), channel_id=1, source_target_pairs={{0,1},{1,0},{2,3},{3,2},{4,5},{5,4},{6,7},{7,6},{8,9},{9,8},{10,11... | collective-permute-start | bytes 1572872 | tf_op jit(solution)/shard_map/ppermute | solution.py:506

commit v9 on v8

--- a/solution.py
+++ b/solution.py
@@ -111,13 +111,14 @@
 
 
 def turn_rows(out_ref, sources):
-    def step(i, _):
-        for block in range(out_ref.shape[1] // LANES):
-            at = slice(block * LANES, (block + 1) * LANES)
-            out_ref[i, at, :] = two_rows_turned(sources, block, i).astype(jnp.bfloat16)
-        return 0
-
-    lax.fori_loop(0, STEP, step, 0)
+    def step(n, _):
+        for i in (2 * n, 2 * n + 1):
+            for block in range(out_ref.shape[1] // LANES):
+                at = slice(block * LANES, (block + 1) * LANES)
+                out_ref[i, at, :] = two_rows_turned(sources, block, i).astype(jnp.bfloat16)
+        return 0
+
+    lax.fori_loop(0, STEP // 2, step, 0)
 
 
 def add_terms(x_ref, raw_ref, side_sources, row_terms, col_terms, scale, core, mask):
@@ -179,7 +180,7 @@
     return left + centre + right
 
 
-def conv_own_rows(own_ref, near_ref, weights, p_ref, out_ref):
+def conv_own_rows(own_ref, near_ref, weights, p_ref, out_ref, leave):
     cols = out_ref.shape[1]
     total = jnp.zeros((STEP, LANES), jnp.float32)
     squares = total
@@ -192,6 +193,7 @@
             value = value.reshape(LANES // STEP, STEP, LANES)
             total = total + jnp.sum(value, axis=0)
             squares = squares + jnp.sum(value * value, axis=0)
+        leave(i)
     total = total + pltpu.roll(total, LANES // 2, 1)
     squares = squares + pltpu.roll(squares, LANES // 2, 1)
     return jnp.sum(jnp.where(lane_half(STEP), total, squares), axis=0, keepdims=True)
@@ -253,15 +255,15 @@
         widen(halo, below_flat)
 
 
-def turn_near_kernel(one, two_in, near_ref, row_terms, two, above_flat, below_flat, sem):
+def turn_near_kernel(one_in, two, near_ref, row_terms, one, above_flat, below_flat, sem):
     odd = lax.rem(lax.axis_index(GX), 2)
-    channels = one.shape[0] - 1
-    inputs = start_all(sem, 0, ((two_in, two),))
+    channels = two.shape[0] - 1
+    inputs = start_all(sem, 0, ((one_in, one),))
+    widen_halo(two.at[pl.ds(0, channels)], 1, above_flat, below_flat)
+    two_terms = two[channels, :, :LANES].astype(jnp.float32)
+    wait_all(inputs)
     widen_halo(one.at[pl.ds(0, channels)], 0, above_flat, below_flat)
     one_terms = one[channels, :, :LANES].astype(jnp.float32)
-    wait_all(inputs)
-    widen_halo(two.at[pl.ds(0, channels)], 1, above_flat, below_flat)
-    two_terms = two[channels, :, :LANES].astype(jnp.float32)
     row_terms[...] = halves(
         jnp.where(odd == 1, one_terms, two_terms), jnp.where(odd == 1, two_terms, one_terms)
     )
@@ -305,9 +307,14 @@
         near_terms, col_terms, inside_of(row_at, devices), core, mask,
     )
     wait_all(inputs)
-    stats = conv_own_rows(x_own, x_near, weights_of(taps, OWN_TAPS), p_ref, conv_ref)
+
+    def leave(i):
+        if i % half == half - 1:
+            at = pl.ds(i - half + 1, half)
+            outputs.extend(start_all(sem, 3 + i // half, ((conv_ref.at[at], conv_out.at[at]),)))
+
+    stats = conv_own_rows(x_own, x_near, weights_of(taps, OWN_TAPS), p_ref, conv_ref, leave)
     stats_ref[...] = jnp.broadcast_to(stats, stats_ref.shape)
-    outputs += start_all(sem, 3, ((conv_ref, conv_out),))
     lower = lane_half(LANES)
     for i in range(half):
         for first in range(0, cols, LANES):
@@ -372,9 +379,16 @@
     lax.fori_loop(0, half, fill_near, 0)
     wait_all(inputs)
     lax.fori_loop(0, STEP, fill_own, 0)
-    stats = conv_own_rows(a_own, a_near, weights_of(taps, OWN_TAPS), p_ref, conv_ref)
+    outputs = []
+
+    def leave(i):
+        if i % half == half - 1:
+            at = pl.ds(i - half + 1, half)
+            outputs.extend(start_all(sem, i // half, ((conv_ref.at[at], conv_out.at[at]),)))
+
+    stats = conv_own_rows(a_own, a_near, weights_of(taps, OWN_TAPS), p_ref, conv_ref, leave)
     given = conv_ref.at[pl.ds(half * (1 - core), half)]
-    outputs = start_all(sem, 0, ((given, give_out), (conv_ref, conv_out)))
+    outputs += start_all(sem, 2, ((given, give_out),))
     stats_ref[...] = jnp.broadcast_to(stats, stats_ref.shape)
     wait_all(outputs)
 
@@ -551,7 +565,7 @@
         [VMEM(two.shape, bf16), flat_of(channels, STEP, cols), flat_of(channels, STEP, cols)],
         1,
         conv_flops,
-        ((VMEM, one), (HBM, two)),
+        ((HBM, one), (VMEM, two)),
     )
     own_rows, conv_own, own_give, conv_one, conv_two, edges, stats = call(
         functools.partial(first_kernel, devices),
@@ -576,7 +590,7 @@
             VMEM(wide[1:], f32),
             VMEM((STEP, LANES), f32),
         ],
-        4,
+        5,
         conv_flops,
         ((VMEM, own_raw), (VMEM, near_raw), (VMEM, near_terms), (VMEM, own_side),
          (VMEM, one_side), (VMEM, two_side), (VMEM, terms), (VMEM, mine), (HBM, first_taps)),
@@ -606,7 +620,7 @@
             VMEM(whole, bf16),
             taps_shape,
         ],
-        2,
+        3,
         conv_flops,
         ((HBM, conv_own), (VMEM, conv_one), (VMEM, conv_two), (VMEM, edges),
          (VMEM, corners), (VMEM, stats), (VMEM, stats_other), (VMEM, gains),

time: 182 us -> 180 us (0.989)
  blocking collectives: 76 us -> 74 us
    all_to_all x1, blocking collectives: 20.5 us -> 18.5 us  [body(): stats = lax.all_to_all(stats, GX, 0, 0, tiled=True)]
where the time goes in v9:
time: 180 us; the launch traced here: 179 us
  blocking collectives  74 us (41%)
  starting transfers between devices  61.4 us (34%)
  Pallas kernels  21.9 us (12%)
  waiting for transfers between devices  18.6 us (10%)
  other arithmetic  2.44 us (1%)
    all_to_all x1, blocking collectives, body(): received = lax.all_to_all(send, GX, 0, 0, tiled=True)  55.5 us
    ppermute x10, starting transfers between devices, swap(): return lax.ppermute(x, 'gy', SWAP)  28.7 us
    pallas_call x7, Pallas kernels, call(): pl.pallas_call(kernel, out_shape=[space(shape, dtype) for space, shape, d...  21.9 us
    all_to_all x1, blocking collectives, body(): stats = lax.all_to_all(stats, GX, 0, 0, tiled=True)  18.5 us
    all_to_all x1, starting transfers between devices, body(): terms = lax.all_to_all(terms, GX, 0, 0, tiled=True)  14.3 us
    all_to_all x1, starting transfers between devices, body(): stats = lax.all_to_all(stats, GX, 0, 0, tiled=True)  10.9 us
    all_to_all x1, waiting for transfers between devices, body(): stats = lax.all_to_all(stats, GX, 0, 0, tiled=True)  10 us
    all_to_all x1, waiting for transfers between devices, body(): terms = lax.all_to_all(terms, GX, 0, 0, tiled=True)  5.9 us
  transfers between devices with their start and end apart: 16, of which 5 were waited for; matrix products, arithmetic and copies ran while one was open for 1% of the time, Pallas kernels for 5%

profile of v9, /device:TPU:33, one launch (start us, length us, event | category | flops | bytes accessed | tf_op | source)
XLA Modules:
  0.0 179.2 jit_solution(4160130283918762463)
XLA Ops:
  0.0 2.1 %shard_map.83 = (bf16[65,8,512]{2,1,0:T(8,128)(2,1)S(1)}, bf16[65,8,512]{2,1,0:T(8,128)(2,1)S(1)}, bf16[64,8,128]{2,1,0:T(8,128)(2,1)}, f32[8,128]{1,0:T(8,128)S(1)}) custom-call(bf16[64,16,512]{2,1,0:T(8,128)(2,1)} %pair.3, bf16[16,256]{1,0:T(8,128)(2,1)} %feats.1, bf16[64,256]{1,0:T(8,128)(2,1)} %bitcast.19, bf16[64,256]{1,0:T(8,128)(2,1)} %bitcast.20), custom_call_target="tpu_custom_call" | custom-call | flops 37748736 | bytes 1048576 | tf_op jit(solution)/shard_map/pallas_call | solution.py:28
  2.1 3.4 %collective-permute-start = (bf16[65,8,512]{2,1,0:T(8,128)(2,1)S(1)}, bf16[65,8,512]{2,1,0:T(8,128)(2,1)}, u32[]{:S(2)}, u32[]{:S(2)}) collective-permute-start(bf16[65,8,512]{2,1,0:T(8,128)(2,1)S(1)} %get-tuple-element.23), channel_id=1, source_target_pairs={{0,2},{2,0},{4,6},{6,4},{8,10},{10,8},{12,14},{14,12},{16,18},{18,... | collective-permute-start | bytes 1597448 | tf_op jit(solution)/shard_map/ppermute | solution.py:542
  6.3 17.3 %collective-permute-start.2 = (bf16[64,16,128]{2,1,0:T(8,128)(2,1)S(1)}, bf16[64,16,128]{2,1,0:T(8,128)(2,1)S(1)}, u32[]{:S(2)}, u32[]{:S(2)}) collective-permute-start(bf16[64,16,128]{2,1,0:T(8,128)(2,1)S(1)} %slice_select_fusion.1), channel_id=1, source_target_pairs={{0,1},{1,0},{2,3},{3,2},{4,5},{5,4},{6,7},{7,6},{8,9},{9,8},{10,11... | collective-permute-start | bytes 786440 | tf_op jit(solution)/shard_map/ppermute | solution.py:520
  23.6 14.3 %all-to-all-start = ((bf16[64,8,128]{2,1,0:T(8,128)(2,1)}), bf16[64,8,128]{2,1,0:T(8,128)(2,1)S(1)}, u32[]{:S(2)}, u32[]{:S(2)}) async-start(bf16[64,8,128]{2,1,0:T(8,128)(2,1)} %get-tuple-element.27), calls=%async_computation | async-start | bytes 262144 | tf_op jit(solution)/shard_map/all_to_all | solution.py:543
  37.9 1.7 slice_select_fusion.3
  40.7 2.6 %shard_map.82.own_raw = bf16[8,512,128]{2,1,0:T(8,128)(2,1)S(1)} custom-call(bf16[64,16,512]{2,1,0:T(8,128)(2,1)} %pair.3), custom_call_target="tpu_custom_call" | custom-call | flops 603979776 | bytes 1048576 | tf_op jit(solution)/shard_map/pallas_call | solution.py:28
  43.3 2.0 %shard_map.84 = (bf16[8,512,128]{2,1,0:T(8,128)(2,1)S(1)}, f32[8,128]{1,0:T(8,128)S(1)}) custom-call(bf16[65,8,512]{2,1,0:T(8,128)(2,1)} %collective-permute-done.one_in, bf16[65,8,512]{2,1,0:T(8,128)(2,1)S(1)} %collective-permute-done.1.two), custom_call_target="tpu_custom_call" | custom-call | flops 603979776 | bytes 1048576 | tf_op jit(solution)/shard_map/pallas_call | solution.py:28
  45.3 5.9 %all-to-all-done.terms = bf16[64,8,128]{2,1,0:T(8,128)(2,1)S(1)} async-done(((bf16[64,8,128]{2,1,0:T(8,128)(2,1)}), bf16[64,8,128]{2,1,0:T(8,128)(2,1)S(1)}, u32[]{:S(2)}, u32[]{:S(2)}) %all-to-all-start) | async-done | bytes 131104 | tf_op jit(solution)/shard_map/all_to_all | solution.py:543
  51.2 4.4 %shard_map.85 = (bf16[8,512,128]{2,1,0:T(8,128)(2,1)}, bf16[8,512,128]{2,1,0:T(8,128)(2,1)}, bf16[4,512,128]{2,1,0:T(8,128)(2,1)}, bf16[4,512,128]{2,1,0:T(8,128...) custom-call(bf16[8,512,128]{2,1,0:T(8,128)(2,1)S(1)} %shard_map.82.own_raw, ...), custom_call_target="tpu_custom_call" | custom-call | flops 603979776 | bytes 1048576 | tf_op jit(solution)/shard_map/pallas_call | solution.py:28
  55.6 0.7 collective-permute-start.7
  56.3 2.7 %collective-permute-start.6 = (bf16[4,512,128]{2,1,0:T(8,128)(2,1)S(1)}, bf16[4,512,128]{2,1,0:T(8,128)(2,1)S(1)}, u32[]{:S(2)}, u32[]{:S(2)}) collective-permute-start(bf16[4,512,128]{2,1,0:T(8,128)(2,1)S(1)} %get-tuple-element.32), channel_id=1, source_target_pairs={{0,2},{2,0},{4,6},{6,4},{8,10},{10,8},{12,14},{14,12},{16,18},{18,... | collective-permute-start | bytes 1572872 | tf_op jit(solution)/shard_map/ppermute | solution.py:598
  59.0 10.9 %all-to-all-start.1 = ((f32[64,1,128]{2,1,0:T(1,128)}), f32[64,1,128]{2,1,0:T(1,128)S(1)}, u32[]{:S(2)}, u32[]{:S(2)}) async-start(f32[64,1,128]{2,1,0:T(1,128)} %bitcast.5), calls=%async_computation.1 | async-start | bytes 65536 | tf_op jit(solution)/shard_map/all_to_all | solution.py:599
  69.9 2.0 %collective-permute-start.8 = (bf16[8,16,128]{2,1,0:T(8,128)(2,1)S(1)}, bf16[8,16,128]{2,1,0:T(8,128)(2,1)S(1)}, u32[]{:S(2)}, u32[]{:S(2)}) collective-permute-start(bf16[8,16,128]{2,1,0:T(8,128)(2,1)S(1)} %get-tuple-element.34), channel_id=1, source_target_pairs={{0,1},{1,0},{2,3},{3,2},{4,5},{5,4},{6,7},{7,6},{8,9},{9,8},{10,11... | collective-permute-start | bytes 98312 | tf_op jit(solution)/shard_map/ppermute | solution.py:520
  71.9 10.0 %all-to-all-done.1 = f32[64,1,128]{2,1,0:T(1,128)S(1)} async-done(((f32[64,1,128]{2,1,0:T(1,128)}), f32[64,1,128]{2,1,0:T(1,128)S(1)}, u32[]{:S(2)}, u32[]{:S(2)}) %all-to-all-start.1) | async-done | bytes 32800 | tf_op jit(solution)/shard_map/all_to_all | solution.py:599
  81.9 3.0 %collective-permute-start.10 = (f32[64,128]{1,0:T(8,128)S(1)}, f32[64,128]{1,0:T(8,128)S(1)}, u32[]{:S(2)}, u32[]{:S(2)}) collective-permute-start(f32[64,128]{1,0:T(8,128)S(1)} %bitcast.14), channel_id=1, source_target_pairs={{0,1},{1,0},{2,3},{3,2},{4,5},{5,4},{6,7},{7,6},{8,9},{9,8},{10,11... | collective-permute-start | bytes 98312 | tf_op jit(solution)/shard_map/ppermute | solution.py:520
  86.2 4.3 %shard_map.86 = (bf16[8,512,128]{2,1,0:T(8,128)(2,1)}, bf16[4,512,128]{2,1,0:T(8,128)(2,1)}, f32[64,128]{1,0:T(8,128)S(1)}) custom-call(bf16[8,512,128]{2,1,0:T(8,128)(2,1)} %get-tuple-element.31.own_in, bf16[4,512,128]{2,1,0:T(8,128)(2,1)S(1)} %collective-permute-done.6.one, bf16[4,512,128]{2,1,0:T(8,128)(2,1)S(1)} %collective-permute-done.7.two, ...), custom_call_target="tpu_custom_call" | custom-call | flops 603979776 | bytes 1048576 | tf_op jit(solution)/shard_map/pallas_call | solution.py:28
  90.9 18.5 %all_to_all.32 = f32[64,1,128]{2,1,0:T(1,128)S(1)} all-to-all(f32[64,1,128]{2,1,0:T(1,128)S(1)} %bitcast.18), channel_id=1, replica_groups=mesh['grp'=2,'gx_0'=4,'gx_1'=16,'gy'=2] {'gx_0','gx_1'}, dimensions={0} | all-to-all | bytes 65536 | tf_op jit(solution)/shard_map/all_to_all | solution.py:629
  109.3 1.8 %collective-permute-start.12 = (f32[64,128]{1,0:T(8,128)S(1)}, f32[64,128]{1,0:T(8,128)S(1)}, u32[]{:S(2)}, u32[]{:S(2)}) collective-permute-start(f32[64,128]{1,0:T(8,128)S(1)} %bitcast.16), channel_id=1, source_target_pairs={{0,1},{1,0},{2,3},{3,2},{4,5},{5,4},{6,7},{7,6},{8,9},{9,8},{10,11... | collective-permute-start | bytes 98312 | tf_op jit(solution)/shard_map/ppermute | solution.py:520
  111.1 0.9 collective-permute-done.12.stats_other
  112.0 2.7 %shard_map.87 = (bf16[8,512,128]{2,1,0:T(8,128)(2,1)}, bf16[64,4,16,128]{3,2,1,0:T(8,128)(2,1)S(1)}) custom-call(bf16[8,512,128]{2,1,0:T(8,128)(2,1)} %get-tuple-element.29.block_in, bf16[4,512,128]{2,1,0:T(8,128)(2,1)S(1)} %collective-permute-done.5.other, bf16[8,512,128]{2,1,0:T(8,128)(2,1)} %get-tuple-element.36.conv_in, ...), custom_call_target="tpu_custom_call" | custom-call | flops 603979776 | bytes 1048576 | tf_op jit(solution)/shard_map/pallas_call | solution.py:28
  114.7 55.5 %all_to_all.33.received = bf16[64,4,16,128]{3,2,1,0:T(8,128)(2,1)S(1)} all-to-all(bf16[64,4,16,128]{3,2,1,0:T(8,128)(2,1)S(1)} %get-tuple-element.40), channel_id=1, replica_groups=mesh['grp'=2,'gx_0'=4,'gx_1'=16,'gy'=2] {'gx_0','gx_1'}, dimensions={0} | all-to-all | bytes 2097152 | tf_op jit(solution)/shard_map/all_to_all | solution.py:645
  170.3 3.5 %collective-permute-start.13 = (bf16[32,4,16,128]{3,2,1,0:T(8,128)(2,1)S(1)}, bf16[32,4,16,128]{3,2,1,0:T(8,128)(2,1)S(1)}, u32[]{:S(2)}, u32[]{:S(2)}) collective-permute-start(bf16[32,4,16,128]{3,2,1,0:T(8,128)(2,1)S(1)} %slice_select_fusion), channel_id=1, source_target_pairs={{0,1},{1,0},{2,3},{3,2},{4,5},{5,4},{6,7},{7,6},{8,9},{9,8},{10,11... | collective-permute-start | bytes 1572872 | tf_op jit(solution)/shard_map/ppermute | solution.py:520
  173.7 1.5 collective-permute-done.13.other
  175.3 3.8 %shard_map.88 = bf16[64,16,512]{2,1,0:T(8,128)(2,1)} custom-call(bf16[8,512,128]{2,1,0:T(8,128)(2,1)} %get-tuple-element.39.own_in, bf16[64,4,16,128]{3,2,1,0:T(8,128)(2,1)S(1)} %all_to_all.33.received, bf16[32,4,16,128]{3,2,1,0:T(8,128)(2,1)S(1)} %collective-permute-done.13.other), custom_call_target="tpu_custom_call" | custom-call | flops 603979776 | bytes 1048576 | tf_op jit(solution)/shard_map/pallas_call | solution.py:28
  (33 shorter events, 3.6 us)
Async XLA Ops:
  0.0 6.2 %copy-start = (bf16[64,16,512]{2,1,0:T(8,128)(2,1)S(1)}, bf16[64,16,512]{2,1,0:T(8,128)(2,1)}, u32[]{:S(2)}) copy-start(bf16[64,16,512]{2,1,0:T(8,128)(2,1)} %pair.3) | copy-start | bytes 3145732
  2.1 35.7 %collective-permute-start = (bf16[65,8,512]{2,1,0:T(8,128)(2,1)S(1)}, bf16[65,8,512]{2,1,0:T(8,128)(2,1)}, u32[]{:S(2)}, u32[]{:S(2)}) collective-permute-start(bf16[65,8,512]{2,1,0:T(8,128)(2,1)S(1)} %get-tuple-element.23), channel_id=1, source_target_pairs={{0,2},{2,0},{4,6},{6,4},{8,10},{10,8},{12,14},{14,12},{16,18},{18,... | collective-permute-start | bytes 1597448 | tf_op jit(solution)/shard_map/ppermute | solution.py:542
  5.6 34.3 %collective-permute-start.1 = (bf16[65,8,512]{2,1,0:T(8,128)(2,1)S(1)}, bf16[65,8,512]{2,1,0:T(8,128)(2,1)S(1)}, u32[]{:S(2)}, u32[]{:S(2)}) collective-permute-start(bf16[65,8,512]{2,1,0:T(8,128)(2,1)S(1)} %get-tuple-element.24), channel_id=1, source_target_pairs={{2,4},{4,2},{6,8},{8,6},{10,12},{12,10},{14,16},{16,14},{18,20},{2... | collective-permute-start | bytes 1597448 | tf_op jit(solution)/shard_map/ppermute | solution.py:542
  6.3 39.0 %collective-permute-start.2 = (bf16[64,16,128]{2,1,0:T(8,128)(2,1)S(1)}, bf16[64,16,128]{2,1,0:T(8,128)(2,1)S(1)}, u32[]{:S(2)}, u32[]{:S(2)}) collective-permute-start(bf16[64,16,128]{2,1,0:T(8,128)(2,1)S(1)} %slice_select_fusion.1), channel_id=1, source_target_pairs={{0,1},{1,0},{2,3},{3,2},{4,5},{5,4},{6,7},{7,6},{8,9},{9,8},{10,11... | collective-permute-start | bytes 786440 | tf_op jit(solution)/shard_map/ppermute | solution.py:520
  23.6 27.6 %all-to-all-start = ((bf16[64,8,128]{2,1,0:T(8,128)(2,1)}), bf16[64,8,128]{2,1,0:T(8,128)(2,1)S(1)}, u32[]{:S(2)}, u32[]{:S(2)}) async-start(bf16[64,8,128]{2,1,0:T(8,128)(2,1)} %get-tuple-element.27), calls=%async_computation | async-start | bytes 262144 | tf_op jit(solution)/shard_map/all_to_all | solution.py:543
  39.5 11.7 %collective-permute-start.3 = (bf16[64,8,128]{2,1,0:T(8,128)(2,1)}, bf16[64,8,128]{2,1,0:T(8,128)(2,1)S(1)}, u32[]{:S(2)}, u32[]{:S(2)}) collective-permute-start(bf16[64,8,128]{2,1,0:T(8,128)(2,1)} %slice_select_fusion.3), channel_id=1, source_target_pairs={{0,1},{1,0},{2,3},{3,2},{4,5},{5,4},{6,7},{7,6},{8,9},{9,8},{10,11... | collective-permute-start | bytes 393224 | tf_op jit(solution)/shard_map/ppermute | solution.py:520
  40.5 10.7 %collective-permute-start.4 = (bf16[64,8,128]{2,1,0:T(8,128)(2,1)}, bf16[64,8,128]{2,1,0:T(8,128)(2,1)S(1)}, u32[]{:S(2)}, u32[]{:S(2)}) collective-permute-start(bf16[64,8,128]{2,1,0:T(8,128)(2,1)} %slice_select_fusion.2), channel_id=1, source_target_pairs={{0,1},{1,0},{2,3},{3,2},{4,5},{5,4},{6,7},{7,6},{8,9},{9,8},{10,11... | collective-permute-start | bytes 393224 | tf_op jit(solution)/shard_map/ppermute | solution.py:520
  55.6 29.3 %collective-permute-start.7 = (bf16[4,512,128]{2,1,0:T(8,128)(2,1)}, bf16[4,512,128]{2,1,0:T(8,128)(2,1)S(1)}, u32[]{:S(2)}, u32[]{:S(2)}) collective-permute-start(bf16[4,512,128]{2,1,0:T(8,128)(2,1)} %get-tuple-element.33), channel_id=1, source_target_pairs={{2,4},{4,2},{6,8},{8,6},{10,12},{12,10},{14,16},{16,14},{18,20},{2... | collective-permute-start | bytes 1572872 | tf_op jit(solution)/shard_map/ppermute | solution.py:598
  56.3 28.6 %collective-permute-start.6 = (bf16[4,512,128]{2,1,0:T(8,128)(2,1)S(1)}, bf16[4,512,128]{2,1,0:T(8,128)(2,1)S(1)}, u32[]{:S(2)}, u32[]{:S(2)}) collective-permute-start(bf16[4,512,128]{2,1,0:T(8,128)(2,1)S(1)} %get-tuple-element.32), channel_id=1, source_target_pairs={{0,2},{2,0},{4,6},{6,4},{8,10},{10,8},{12,14},{14,12},{16,18},{18,... | collective-permute-start | bytes 1572872 | tf_op jit(solution)/shard_map/ppermute | solution.py:598
  59.0 22.9 %all-to-all-start.1 = ((f32[64,1,128]{2,1,0:T(1,128)}), f32[64,1,128]{2,1,0:T(1,128)S(1)}, u32[]{:S(2)}, u32[]{:S(2)}) async-start(f32[64,1,128]{2,1,0:T(1,128)} %bitcast.5), calls=%async_computation.1 | async-start | bytes 65536 | tf_op jit(solution)/shard_map/all_to_all | solution.py:599
  69.9 16.0 %collective-permute-start.8 = (bf16[8,16,128]{2,1,0:T(8,128)(2,1)S(1)}, bf16[8,16,128]{2,1,0:T(8,128)(2,1)S(1)}, u32[]{:S(2)}, u32[]{:S(2)}) collective-permute-start(bf16[8,16,128]{2,1,0:T(8,128)(2,1)S(1)} %get-tuple-element.34), channel_id=1, source_target_pairs={{0,1},{1,0},{2,3},{3,2},{4,5},{5,4},{6,7},{7,6},{8,9},{9,8},{10,11... | collective-permute-start | bytes 98312 | tf_op jit(solution)/shard_map/ppermute | solution.py:520
  81.9 4.1 %collective-permute-start.10 = (f32[64,128]{1,0:T(8,128)S(1)}, f32[64,128]{1,0:T(8,128)S(1)}, u32[]{:S(2)}, u32[]{:S(2)}) collective-permute-start(f32[64,128]{1,0:T(8,128)S(1)} %bitcast.14), channel_id=1, source_target_pairs={{0,1},{1,0},{2,3},{3,2},{4,5},{5,4},{6,7},{7,6},{8,9},{9,8},{10,11... | collective-permute-start | bytes 98312 | tf_op jit(solution)/shard_map/ppermute | solution.py:520
  84.9 0.7 copy-start.1
  84.9 0.7 copy-start.2
  84.9 1.3 collective-permute-start.9
  85.7 25.5 %collective-permute-start.5 = (bf16[4,512,128]{2,1,0:T(8,128)(2,1)}, bf16[4,512,128]{2,1,0:T(8,128)(2,1)S(1)}, u32[]{:S(2)}, u32[]{:S(2)}) collective-permute-start(bf16[4,512,128]{2,1,0:T(8,128)(2,1)} %get-tuple-element.30), channel_id=1, source_target_pairs={{0,1},{1,0},{2,3},{3,2},{4,5},{5,4},{6,7},{7,6},{8,9},{9,8},{10,11... | collective-permute-start | bytes 1572872 | tf_op jit(solution)/shard_map/ppermute | solution.py:520
  90.6 21.4 %collective-permute-start.11 = (bf16[4,512,128]{2,1,0:T(8,128)(2,1)}, bf16[4,512,128]{2,1,0:T(8,128)(2,1)S(1)}, u32[]{:S(2)}, u32[]{:S(2)}) collective-permute-start(bf16[4,512,128]{2,1,0:T(8,128)(2,1)} %get-tuple-element.37), channel_id=1, source_target_pairs={{0,1},{1,0},{2,3},{3,2},{4,5},{5,4},{6,7},{7,6},{8,9},{9,8},{10,11... | collective-permute-start | bytes 1572872 | tf_op jit(solution)/shard_map/ppermute | solution.py:520
  109.3 2.7 %collective-permute-start.12 = (f32[64,128]{1,0:T(8,128)S(1)}, f32[64,128]{1,0:T(8,128)S(1)}, u32[]{:S(2)}, u32[]{:S(2)}) collective-permute-start(f32[64,128]{1,0:T(8,128)S(1)} %bitcast.16), channel_id=1, source_target_pairs={{0,1},{1,0},{2,3},{3,2},{4,5},{5,4},{6,7},{7,6},{8,9},{9,8},{10,11... | collective-permute-start | bytes 98312 | tf_op jit(solution)/shard_map/ppermute | solution.py:520
  170.3 5.0 %collective-permute-start.13 = (bf16[32,4,16,128]{3,2,1,0:T(8,128)(2,1)S(1)}, bf16[32,4,16,128]{3,2,1,0:T(8,128)(2,1)S(1)}, u32[]{:S(2)}, u32[]{:S(2)}) collective-permute-start(bf16[32,4,16,128]{3,2,1,0:T(8,128)(2,1)S(1)} %slice_select_fusion), channel_id=1, source_target_pairs={{0,1},{1,0},{2,3},{3,2},{4,5},{5,4},{6,7},{7,6},{8,9},{9,8},{10,11... | collective-permute-start | bytes 1572872 | tf_op jit(solution)/shard_map/ppermute | solution.py:520

commit v10 on v9

--- a/solution.py
+++ b/solution.py
@@ -541,7 +541,8 @@
     )
     one, two = with_next(one), with_last(two)
     terms = lax.all_to_all(terms, GX, 0, 0, tiled=True)
-    gains = jnp.tile(jnp.concatenate([norm_scale, norm_shift], axis=0), (1, 2))
+    gains = jnp.concatenate([norm_scale, norm_shift], axis=0)
+    gains = jnp.concatenate([gains, gains], axis=1)
     own_side = swap(edge(pair_feats))
     one_side, two_side = swap(edge(one[:channels])), swap(edge(two[:channels]))
 
@@ -595,7 +596,8 @@
         ((VMEM, own_raw), (VMEM, near_raw), (VMEM, near_terms), (VMEM, own_side),
          (VMEM, one_side), (VMEM, two_side), (VMEM, terms), (VMEM, mine), (HBM, first_taps)),
     )
-    conv_one, conv_two = with_next(conv_one), with_last(conv_two)
+    conv_one = with_next(conv_one)
+    conv_two = with_last(conv_two)
     stats = lax.all_to_all(stats, GX, 0, 0, tiled=True)
     stats_other = swap(stats)
     edges = swap(edges)

time: 180 us -> 180 us (level)
  no operation moved by 1% of the time
where the time goes in v10:
time: 180 us; the launch traced here: 179 us
  blocking collectives  74 us (41%)
  starting transfers between devices  61.4 us (34%)
  Pallas kernels  21.9 us (12%)
  waiting for transfers between devices  18.6 us (10%)
  other arithmetic  2.51 us (1%)
    all_to_all x1, blocking collectives, body(): received = lax.all_to_all(send, GX, 0, 0, tiled=True)  55.5 us
    ppermute x10, starting transfers between devices, swap(): return lax.ppermute(x, 'gy', SWAP)  28.7 us
    pallas_call x7, Pallas kernels, call(): pl.pallas_call(kernel, out_shape=[space(shape, dtype) for space, shape, d...  21.9 us
    all_to_all x1, blocking collectives, body(): stats = lax.all_to_all(stats, GX, 0, 0, tiled=True)  18.4 us
    all_to_all x1, starting transfers between devices, body(): terms = lax.all_to_all(terms, GX, 0, 0, tiled=True)  14.3 us
    all_to_all x1, starting transfers between devices, body(): stats = lax.all_to_all(stats, GX, 0, 0, tiled=True)  10.9 us
    all_to_all x1, waiting for transfers between devices, body(): stats = lax.all_to_all(stats, GX, 0, 0, tiled=True)  10 us
    all_to_all x1, waiting for transfers between devices, body(): terms = lax.all_to_all(terms, GX, 0, 0, tiled=True)  5.9 us
  transfers between devices with their start and end apart: 16, of which 5 were waited for; matrix products, arithmetic and copies ran while one was open for 1% of the time, Pallas kernels for 5%

profile of v10, /device:TPU:33, one launch (start us, length us, event | category | flops | bytes accessed | tf_op | source)
XLA Modules:
  0.0 179.2 jit_solution(4409066435327930211)
XLA Ops:
  0.0 2.1 %shard_map.83 = (bf16[65,8,512]{2,1,0:T(8,128)(2,1)S(1)}, bf16[65,8,512]{2,1,0:T(8,128)(2,1)S(1)}, bf16[64,8,128]{2,1,0:T(8,128)(2,1)}, f32[8,128]{1,0:T(8,128)S(1)}) custom-call(bf16[64,16,512]{2,1,0:T(8,128)(2,1)} %pair.3, bf16[16,256]{1,0:T(8,128)(2,1)} %feats.1, bf16[64,256]{1,0:T(8,128)(2,1)} %bitcast.19, bf16[64,256]{1,0:T(8,128)(2,1)} %bitcast.20), custom_call_target="tpu_custom_call" | custom-call | flops 37748736 | bytes 1048576 | tf_op jit(solution)/shard_map/pallas_call | solution.py:28
  2.1 3.4 %collective-permute-start = (bf16[65,8,512]{2,1,0:T(8,128)(2,1)S(1)}, bf16[65,8,512]{2,1,0:T(8,128)(2,1)}, u32[]{:S(2)}, u32[]{:S(2)}) collective-permute-start(bf16[65,8,512]{2,1,0:T(8,128)(2,1)S(1)} %get-tuple-element.23), channel_id=1, source_target_pairs={{0,2},{2,0},{4,6},{6,4},{8,10},{10,8},{12,14},{14,12},{16,18},{18,... | collective-permute-start | bytes 1597448 | tf_op jit(solution)/shard_map/ppermute | solution.py:542
  6.3 17.3 %collective-permute-start.2 = (bf16[64,16,128]{2,1,0:T(8,128)(2,1)S(1)}, bf16[64,16,128]{2,1,0:T(8,128)(2,1)S(1)}, u32[]{:S(2)}, u32[]{:S(2)}) collective-permute-start(bf16[64,16,128]{2,1,0:T(8,128)(2,1)S(1)} %slice_select_fusion.1), channel_id=1, source_target_pairs={{0,1},{1,0},{2,3},{3,2},{4,5},{5,4},{6,7},{7,6},{8,9},{9,8},{10,11... | collective-permute-start | bytes 786440 | tf_op jit(solution)/shard_map/ppermute | solution.py:520
  23.6 14.3 %all-to-all-start = ((bf16[64,8,128]{2,1,0:T(8,128)(2,1)}), bf16[64,8,128]{2,1,0:T(8,128)(2,1)S(1)}, u32[]{:S(2)}, u32[]{:S(2)}) async-start(bf16[64,8,128]{2,1,0:T(8,128)(2,1)} %get-tuple-element.27), calls=%async_computation | async-start | bytes 262144 | tf_op jit(solution)/shard_map/all_to_all | solution.py:543
  37.9 1.7 slice_select_fusion.3
  40.7 2.6 %shard_map.82.own_raw = bf16[8,512,128]{2,1,0:T(8,128)(2,1)S(1)} custom-call(bf16[64,16,512]{2,1,0:T(8,128)(2,1)} %pair.3), custom_call_target="tpu_custom_call" | custom-call | flops 603979776 | bytes 1048576 | tf_op jit(solution)/shard_map/pallas_call | solution.py:28
  43.3 2.0 %shard_map.84 = (bf16[8,512,128]{2,1,0:T(8,128)(2,1)S(1)}, f32[8,128]{1,0:T(8,128)S(1)}) custom-call(bf16[65,8,512]{2,1,0:T(8,128)(2,1)} %collective-permute-done.one_in, bf16[65,8,512]{2,1,0:T(8,128)(2,1)S(1)} %collective-permute-done.1.two), custom_call_target="tpu_custom_call" | custom-call | flops 603979776 | bytes 1048576 | tf_op jit(solution)/shard_map/pallas_call | solution.py:28
  45.3 5.9 %all-to-all-done.terms = bf16[64,8,128]{2,1,0:T(8,128)(2,1)S(1)} async-done(((bf16[64,8,128]{2,1,0:T(8,128)(2,1)}), bf16[64,8,128]{2,1,0:T(8,128)(2,1)S(1)}, u32[]{:S(2)}, u32[]{:S(2)}) %all-to-all-start) | async-done | bytes 131104 | tf_op jit(solution)/shard_map/all_to_all | solution.py:543
  51.2 4.4 %shard_map.85 = (bf16[8,512,128]{2,1,0:T(8,128)(2,1)}, bf16[8,512,128]{2,1,0:T(8,128)(2,1)}, bf16[4,512,128]{2,1,0:T(8,128)(2,1)}, bf16[4,512,128]{2,1,0:T(8,128...) custom-call(bf16[8,512,128]{2,1,0:T(8,128)(2,1)S(1)} %shard_map.82.own_raw, ...), custom_call_target="tpu_custom_call" | custom-call | flops 603979776 | bytes 1048576 | tf_op jit(solution)/shard_map/pallas_call | solution.py:28
  55.6 0.7 collective-permute-start.7
  56.3 2.7 %collective-permute-start.6 = (bf16[4,512,128]{2,1,0:T(8,128)(2,1)S(1)}, bf16[4,512,128]{2,1,0:T(8,128)(2,1)S(1)}, u32[]{:S(2)}, u32[]{:S(2)}) collective-permute-start(bf16[4,512,128]{2,1,0:T(8,128)(2,1)S(1)} %get-tuple-element.32), channel_id=1, source_target_pairs={{0,2},{2,0},{4,6},{6,4},{8,10},{10,8},{12,14},{14,12},{16,18},{18,... | collective-permute-start | bytes 1572872 | tf_op jit(solution)/shard_map/ppermute | solution.py:599
  59.0 10.9 %all-to-all-start.1 = ((f32[64,1,128]{2,1,0:T(1,128)}), f32[64,1,128]{2,1,0:T(1,128)S(1)}, u32[]{:S(2)}, u32[]{:S(2)}) async-start(f32[64,1,128]{2,1,0:T(1,128)} %bitcast.5), calls=%async_computation.1 | async-start | bytes 65536 | tf_op jit(solution)/shard_map/all_to_all | solution.py:601
  69.9 2.0 %collective-permute-start.8 = (bf16[8,16,128]{2,1,0:T(8,128)(2,1)S(1)}, bf16[8,16,128]{2,1,0:T(8,128)(2,1)S(1)}, u32[]{:S(2)}, u32[]{:S(2)}) collective-permute-start(bf16[8,16,128]{2,1,0:T(8,128)(2,1)S(1)} %get-tuple-element.34), channel_id=1, source_target_pairs={{0,1},{1,0},{2,3},{3,2},{4,5},{5,4},{6,7},{7,6},{8,9},{9,8},{10,11... | collective-permute-start | bytes 98312 | tf_op jit(solution)/shard_map/ppermute | solution.py:520
  71.9 10.0 %all-to-all-done.1 = f32[64,1,128]{2,1,0:T(1,128)S(1)} async-done(((f32[64,1,128]{2,1,0:T(1,128)}), f32[64,1,128]{2,1,0:T(1,128)S(1)}, u32[]{:S(2)}, u32[]{:S(2)}) %all-to-all-start.1) | async-done | bytes 32800 | tf_op jit(solution)/shard_map/all_to_all | solution.py:601
  81.9 3.0 %collective-permute-start.10 = (f32[64,128]{1,0:T(8,128)S(1)}, f32[64,128]{1,0:T(8,128)S(1)}, u32[]{:S(2)}, u32[]{:S(2)}) collective-permute-start(f32[64,128]{1,0:T(8,128)S(1)} %bitcast.14), channel_id=1, source_target_pairs={{0,1},{1,0},{2,3},{3,2},{4,5},{5,4},{6,7},{7,6},{8,9},{9,8},{10,11... | collective-permute-start | bytes 98312 | tf_op jit(solution)/shard_map/ppermute | solution.py:520
  86.2 4.3 %shard_map.86 = (bf16[8,512,128]{2,1,0:T(8,128)(2,1)}, bf16[4,512,128]{2,1,0:T(8,128)(2,1)}, f32[64,128]{1,0:T(8,128)S(1)}) custom-call(bf16[8,512,128]{2,1,0:T(8,128)(2,1)} %get-tuple-element.31.own_in, bf16[4,512,128]{2,1,0:T(8,128)(2,1)S(1)} %collective-permute-done.6.one, bf16[4,512,128]{2,1,0:T(8,128)(2,1)S(1)} %collective-permute-done.7.two, ...), custom_call_target="tpu_custom_call" | custom-call | flops 603979776 | bytes 1048576 | tf_op jit(solution)/shard_map/pallas_call | solution.py:28
  90.8 18.4 %all_to_all.32 = f32[64,1,128]{2,1,0:T(1,128)S(1)} all-to-all(f32[64,1,128]{2,1,0:T(1,128)S(1)} %bitcast.18), channel_id=1, replica_groups=mesh['grp'=2,'gx_0'=4,'gx_1'=16,'gy'=2] {'gx_0','gx_1'}, dimensions={0} | all-to-all | bytes 65536 | tf_op jit(solution)/shard_map/all_to_all | solution.py:631
  109.3 1.8 %collective-permute-start.12 = (f32[64,128]{1,0:T(8,128)S(1)}, f32[64,128]{1,0:T(8,128)S(1)}, u32[]{:S(2)}, u32[]{:S(2)}) collective-permute-start(f32[64,128]{1,0:T(8,128)S(1)} %bitcast.16), channel_id=1, source_target_pairs={{0,1},{1,0},{2,3},{3,2},{4,5},{5,4},{6,7},{7,6},{8,9},{9,8},{10,11... | collective-permute-start | bytes 98312 | tf_op jit(solution)/shard_map/ppermute | solution.py:520
  111.1 0.9 collective-permute-done.12.stats_other
  112.0 2.7 %shard_map.87 = (bf16[8,512,128]{2,1,0:T(8,128)(2,1)}, bf16[64,4,16,128]{3,2,1,0:T(8,128)(2,1)S(1)}) custom-call(bf16[8,512,128]{2,1,0:T(8,128)(2,1)} %get-tuple-element.29.block_in, bf16[4,512,128]{2,1,0:T(8,128)(2,1)S(1)} %collective-permute-done.5.other, bf16[8,512,128]{2,1,0:T(8,128)(2,1)} %get-tuple-element.36.conv_in, ...), custom_call_target="tpu_custom_call" | custom-call | flops 603979776 | bytes 1048576 | tf_op jit(solution)/shard_map/pallas_call | solution.py:28
  114.7 55.5 %all_to_all.33.received = bf16[64,4,16,128]{3,2,1,0:T(8,128)(2,1)S(1)} all-to-all(bf16[64,4,16,128]{3,2,1,0:T(8,128)(2,1)S(1)} %get-tuple-element.40), channel_id=1, replica_groups=mesh['grp'=2,'gx_0'=4,'gx_1'=16,'gy'=2] {'gx_0','gx_1'}, dimensions={0} | all-to-all | bytes 2097152 | tf_op jit(solution)/shard_map/all_to_all | solution.py:647
  170.3 3.5 %collective-permute-start.13 = (bf16[32,4,16,128]{3,2,1,0:T(8,128)(2,1)S(1)}, bf16[32,4,16,128]{3,2,1,0:T(8,128)(2,1)S(1)}, u32[]{:S(2)}, u32[]{:S(2)}) collective-permute-start(bf16[32,4,16,128]{3,2,1,0:T(8,128)(2,1)S(1)} %slice_select_fusion), channel_id=1, source_target_pairs={{0,1},{1,0},{2,3},{3,2},{4,5},{5,4},{6,7},{7,6},{8,9},{9,8},{10,11... | collective-permute-start | bytes 1572872 | tf_op jit(solution)/shard_map/ppermute | solution.py:520
  173.7 1.5 collective-permute-done.13.other
  175.3 3.8 %shard_map.88 = bf16[64,16,512]{2,1,0:T(8,128)(2,1)} custom-call(bf16[8,512,128]{2,1,0:T(8,128)(2,1)} %get-tuple-element.39.own_in, bf16[64,4,16,128]{3,2,1,0:T(8,128)(2,1)S(1)} %all_to_all.33.received, bf16[32,4,16,128]{3,2,1,0:T(8,128)(2,1)S(1)} %collective-permute-done.13.other), custom_call_target="tpu_custom_call" | custom-call | flops 603979776 | bytes 1048576 | tf_op jit(solution)/shard_map/pallas_call | solution.py:28
  (31 shorter events, 3.6 us)
Async XLA Ops:
  0.0 6.2 %copy-start = (bf16[64,16,512]{2,1,0:T(8,128)(2,1)S(1)}, bf16[64,16,512]{2,1,0:T(8,128)(2,1)}, u32[]{:S(2)}) copy-start(bf16[64,16,512]{2,1,0:T(8,128)(2,1)} %pair.3) | copy-start | bytes 3145732
  2.1 35.7 %collective-permute-start = (bf16[65,8,512]{2,1,0:T(8,128)(2,1)S(1)}, bf16[65,8,512]{2,1,0:T(8,128)(2,1)}, u32[]{:S(2)}, u32[]{:S(2)}) collective-permute-start(bf16[65,8,512]{2,1,0:T(8,128)(2,1)S(1)} %get-tuple-element.23), channel_id=1, source_target_pairs={{0,2},{2,0},{4,6},{6,4},{8,10},{10,8},{12,14},{14,12},{16,18},{18,... | collective-permute-start | bytes 1597448 | tf_op jit(solution)/shard_map/ppermute | solution.py:542
  5.6 34.3 %collective-permute-start.1 = (bf16[65,8,512]{2,1,0:T(8,128)(2,1)S(1)}, bf16[65,8,512]{2,1,0:T(8,128)(2,1)S(1)}, u32[]{:S(2)}, u32[]{:S(2)}) collective-permute-start(bf16[65,8,512]{2,1,0:T(8,128)(2,1)S(1)} %get-tuple-element.24), channel_id=1, source_target_pairs={{2,4},{4,2},{6,8},{8,6},{10,12},{12,10},{14,16},{16,14},{18,20},{2... | collective-permute-start | bytes 1597448 | tf_op jit(solution)/shard_map/ppermute | solution.py:542
  6.3 39.0 %collective-permute-start.2 = (bf16[64,16,128]{2,1,0:T(8,128)(2,1)S(1)}, bf16[64,16,128]{2,1,0:T(8,128)(2,1)S(1)}, u32[]{:S(2)}, u32[]{:S(2)}) collective-permute-start(bf16[64,16,128]{2,1,0:T(8,128)(2,1)S(1)} %slice_select_fusion.1), channel_id=1, source_target_pairs={{0,1},{1,0},{2,3},{3,2},{4,5},{5,4},{6,7},{7,6},{8,9},{9,8},{10,11... | collective-permute-start | bytes 786440 | tf_op jit(solution)/shard_map/ppermute | solution.py:520
  23.6 27.6 %all-to-all-start = ((bf16[64,8,128]{2,1,0:T(8,128)(2,1)}), bf16[64,8,128]{2,1,0:T(8,128)(2,1)S(1)}, u32[]{:S(2)}, u32[]{:S(2)}) async-start(bf16[64,8,128]{2,1,0:T(8,128)(2,1)} %get-tuple-element.27), calls=%async_computation | async-start | bytes 262144 | tf_op jit(solution)/shard_map/all_to_all | solution.py:543
  39.5 11.7 %collective-permute-start.3 = (bf16[64,8,128]{2,1,0:T(8,128)(2,1)}, bf16[64,8,128]{2,1,0:T(8,128)(2,1)S(1)}, u32[]{:S(2)}, u32[]{:S(2)}) collective-permute-start(bf16[64,8,128]{2,1,0:T(8,128)(2,1)} %slice_select_fusion.3), channel_id=1, source_target_pairs={{0,1},{1,0},{2,3},{3,2},{4,5},{5,4},{6,7},{7,6},{8,9},{9,8},{10,11... | collective-permute-start | bytes 393224 | tf_op jit(solution)/shard_map/ppermute | solution.py:520
  40.5 10.7 %collective-permute-start.4 = (bf16[64,8,128]{2,1,0:T(8,128)(2,1)}, bf16[64,8,128]{2,1,0:T(8,128)(2,1)S(1)}, u32[]{:S(2)}, u32[]{:S(2)}) collective-permute-start(bf16[64,8,128]{2,1,0:T(8,128)(2,1)} %slice_select_fusion.2), channel_id=1, source_target_pairs={{0,1},{1,0},{2,3},{3,2},{4,5},{5,4},{6,7},{7,6},{8,9},{9,8},{10,11... | collective-permute-start | bytes 393224 | tf_op jit(solution)/shard_map/ppermute | solution.py:520
  55.6 29.3 %collective-permute-start.7 = (bf16[4,512,128]{2,1,0:T(8,128)(2,1)}, bf16[4,512,128]{2,1,0:T(8,128)(2,1)S(1)}, u32[]{:S(2)}, u32[]{:S(2)}) collective-permute-start(bf16[4,512,128]{2,1,0:T(8,128)(2,1)} %get-tuple-element.33), channel_id=1, source_target_pairs={{2,4},{4,2},{6,8},{8,6},{10,12},{12,10},{14,16},{16,14},{18,20},{2... | collective-permute-start | bytes 1572872 | tf_op jit(solution)/shard_map/ppermute | solution.py:600
  56.3 28.6 %collective-permute-start.6 = (bf16[4,512,128]{2,1,0:T(8,128)(2,1)S(1)}, bf16[4,512,128]{2,1,0:T(8,128)(2,1)S(1)}, u32[]{:S(2)}, u32[]{:S(2)}) collective-permute-start(bf16[4,512,128]{2,1,0:T(8,128)(2,1)S(1)} %get-tuple-element.32), channel_id=1, source_target_pairs={{0,2},{2,0},{4,6},{6,4},{8,10},{10,8},{12,14},{14,12},{16,18},{18,... | collective-permute-start | bytes 1572872 | tf_op jit(solution)/shard_map/ppermute | solution.py:599
  59.0 22.9 %all-to-all-start.1 = ((f32[64,1,128]{2,1,0:T(1,128)}), f32[64,1,128]{2,1,0:T(1,128)S(1)}, u32[]{:S(2)}, u32[]{:S(2)}) async-start(f32[64,1,128]{2,1,0:T(1,128)} %bitcast.5), calls=%async_computation.1 | async-start | bytes 65536 | tf_op jit(solution)/shard_map/all_to_all | solution.py:601
  69.9 16.0 %collective-permute-start.8 = (bf16[8,16,128]{2,1,0:T(8,128)(2,1)S(1)}, bf16[8,16,128]{2,1,0:T(8,128)(2,1)S(1)}, u32[]{:S(2)}, u32[]{:S(2)}) collective-permute-start(bf16[8,16,128]{2,1,0:T(8,128)(2,1)S(1)} %get-tuple-element.34), channel_id=1, source_target_pairs={{0,1},{1,0},{2,3},{3,2},{4,5},{5,4},{6,7},{7,6},{8,9},{9,8},{10,11... | collective-permute-start | bytes 98312 | tf_op jit(solution)/shard_map/ppermute | solution.py:520
  81.9 4.0 %collective-permute-start.10 = (f32[64,128]{1,0:T(8,128)S(1)}, f32[64,128]{1,0:T(8,128)S(1)}, u32[]{:S(2)}, u32[]{:S(2)}) collective-permute-start(f32[64,128]{1,0:T(8,128)S(1)} %bitcast.14), channel_id=1, source_target_pairs={{0,1},{1,0},{2,3},{3,2},{4,5},{5,4},{6,7},{7,6},{8,9},{9,8},{10,11... | collective-permute-start | bytes 98312 | tf_op jit(solution)/shard_map/ppermute | solution.py:520
  84.9 0.7 copy-start.1
  84.9 0.7 copy-start.2
  84.9 1.3 collective-permute-start.9
  85.6 25.5 %collective-permute-start.5 = (bf16[4,512,128]{2,1,0:T(8,128)(2,1)}, bf16[4,512,128]{2,1,0:T(8,128)(2,1)S(1)}, u32[]{:S(2)}, u32[]{:S(2)}) collective-permute-start(bf16[4,512,128]{2,1,0:T(8,128)(2,1)} %get-tuple-element.30), channel_id=1, source_target_pairs={{0,1},{1,0},{2,3},{3,2},{4,5},{5,4},{6,7},{7,6},{8,9},{9,8},{10,11... | collective-permute-start | bytes 1572872 | tf_op jit(solution)/shard_map/ppermute | solution.py:520
  90.6 21.4 %collective-permute-start.11 = (bf16[4,512,128]{2,1,0:T(8,128)(2,1)}, bf16[4,512,128]{2,1,0:T(8,128)(2,1)S(1)}, u32[]{:S(2)}, u32[]{:S(2)}) collective-permute-start(bf16[4,512,128]{2,1,0:T(8,128)(2,1)} %get-tuple-element.37), channel_id=1, source_target_pairs={{0,1},{1,0},{2,3},{3,2},{4,5},{5,4},{6,7},{7,6},{8,9},{9,8},{10,11... | collective-permute-start | bytes 1572872 | tf_op jit(solution)/shard_map/ppermute | solution.py:520
  109.3 2.7 %collective-permute-start.12 = (f32[64,128]{1,0:T(8,128)S(1)}, f32[64,128]{1,0:T(8,128)S(1)}, u32[]{:S(2)}, u32[]{:S(2)}) collective-permute-start(f32[64,128]{1,0:T(8,128)S(1)} %bitcast.16), channel_id=1, source_target_pairs={{0,1},{1,0},{2,3},{3,2},{4,5},{5,4},{6,7},{7,6},{8,9},{9,8},{10,11... | collective-permute-start | bytes 98312 | tf_op jit(solution)/shard_map/ppermute | solution.py:520
  170.3 5.0 %collective-permute-start.13 = (bf16[32,4,16,128]{3,2,1,0:T(8,128)(2,1)S(1)}, bf16[32,4,16,128]{3,2,1,0:T(8,128)(2,1)S(1)}, u32[]{:S(2)}, u32[]{:S(2)}) collective-permute-start(bf16[32,4,16,128]{3,2,1,0:T(8,128)(2,1)S(1)} %slice_select_fusion), channel_id=1, source_target_pairs={{0,1},{1,0},{2,3},{3,2},{4,5},{5,4},{6,7},{7,6},{8,9},{9,8},{10,11... | collective-permute-start | bytes 1572872 | tf_op jit(solution)/shard_map/ppermute | solution.py:520
